TPU v7x, 32 devices: a whole 2x2x4 slice. The times are simulated.
32 devices in a mesh: fsdp: 8 (over z, y), tensor: 4 (over x, core).
Axes of the slice: x: 2, y: 2, z: 4, core: 2. Of those that a mesh axis runs over, the one named last changes fastest.
Arguments:
- hidden_in: bfloat16 [8192, 2048], P(('fsdp', 'tensor')), may hold values from -6 to 6
- lengths: int32 [8], P('fsdp'), may hold values from 256 to 1024, as said below
- attn_gain: float32 [2048], replicated, may hold values from 0.5 to 2
- query_weight: bfloat16 [2048, 2048], P('fsdp', 'tensor'), may hold values from -0.125 to 0.125
- key_weight: bfloat16 [2048, 1024], P('fsdp', 'tensor'), may hold values from -0.125 to 0.125
- value_weight: bfloat16 [2048, 1024], P('fsdp', 'tensor'), may hold values from -0.125 to 0.125
- output_gate: bfloat16 [2048, 2048], P('fsdp', 'tensor'), may hold values from -0.125 to 0.125
- query_gain: float32 [128], replicated, may hold values from 0.5 to 2
- key_gain: float32 [128], replicated, may hold values from 0.5 to 2
- out_weight: bfloat16 [2048, 2048], P('tensor', 'fsdp'), may hold values from -3 to 3
- mlp_gain: float32 [2048], replicated, may hold values from 0.5 to 2
- gate_weight: bfloat16 [2048, 6144], P('fsdp', 'tensor'), may hold values from -0.125 to 0.125
- up_weight: bfloat16 [2048, 6144], P('fsdp', 'tensor'), may hold values from -0.125 to 0.125
- down_weight: bfloat16 [6144, 2048], P('tensor', 'fsdp'), may hold values from -0.15625 to 0.15625
- cotangent: bfloat16 [8192, 2048], P(('fsdp', 'tensor')), may hold values from -6 to 6
Outputs:
- output: bfloat16 [8192, 2048], P(('fsdp', 'tensor'))
- grad_hidden: float32 [8192, 2048], P(('fsdp', 'tensor'))
- grad_attn_gain: float32 [2048], replicated
- grad_query_weight: float32 [2048, 2048], P('fsdp', 'tensor')
- grad_key_weight: float32 [2048, 1024], P('fsdp', 'tensor')
- grad_value_weight: float32 [2048, 1024], P('fsdp', 'tensor')
- grad_output_gate: float32 [2048, 2048], P('fsdp', 'tensor')
- grad_query_gain: float32 [128], replicated
- grad_key_gain: float32 [128], replicated
- grad_out_weight: float32 [2048, 2048], P('tensor', 'fsdp')
- grad_mlp_gain: float32 [2048], replicated
- grad_gate_weight: float32 [2048, 6144], P('fsdp', 'tensor')
- grad_up_weight: float32 [2048, 6144], P('fsdp', 'tensor')
- grad_down_weight: float32 [6144, 2048], P('tensor', 'fsdp')
Inputs may be any that keep to these rules, and one draw needn't show every extreme that they name: The first lengths[s] slots of sequence s hold real tokens, the rest padding; some sequence has all 1024 and some 1024 // 4.
All inputs are finite; a program needn't handle non-finite values.
Results may differ from a plain program's by a relative error of at most 0.019.
Values may be sent and summed in bfloat16 or wider, within the bound.
A program may use at most 192 MiB of HBM per device.

v0:
```python
import jax
import jax.numpy as jnp
from jax import lax
from jax.sharding import PartitionSpec as P

NORM_EPSILON = 1e-06
ROPE_THETA = 1000000.0
SCORE_BLOCK = 512
MASKED_LOGIT = -1e30


def rows_in(values):
    return lax.all_gather(values, "tensor", axis=0, tiled=True)


def rows_out(values):
    return lax.psum_scatter(values, "tensor", scatter_dimension=0, tiled=True)


def matmul(first_op, second_op):
    return jnp.dot(first_op, second_op, preferred_element_type=jnp.float32)


def matmul_tn(first_op, second_op):
    return lax.dot_general(
        first_op, second_op, (((0,), (0,)), ((), ())), preferred_element_type=jnp.float32
    )


def matmul_nt(first_op, second_op):
    return lax.dot_general(
        first_op, second_op, (((1,), (1,)), ((), ())), preferred_element_type=jnp.float32
    )


def normalize(values):
    inv_root = lax.rsqrt(jnp.mean(values * values, axis=-1, keepdims=True) + NORM_EPSILON)
    return (values * inv_root, inv_root)


def norm_back(gradient, unit_rows, inv_root, gain_vec):
    scaled = gradient * gain_vec
    return inv_root * (scaled - unit_rows * jnp.mean(scaled * unit_rows, axis=-1, keepdims=True))


def rotate_half(values):
    half_width = values.shape[-1] // 2
    return jnp.concatenate([-values[..., half_width:], values[..., :half_width]], axis=-1)


def rotate_back(values):
    half_width = values.shape[-1] // 2
    return jnp.concatenate([values[..., half_width:], -values[..., :half_width]], axis=-1)


def rope_tables(slot_count, head_size):
    half_width = head_size // 2
    inverse = ROPE_THETA ** (-(jnp.arange(half_width, dtype=jnp.float32) * 2.0 / head_size))
    angles = jnp.arange(slot_count, dtype=jnp.float32)[:, None] * inverse[None, :]
    cosine = jnp.concatenate([jnp.cos(angles), jnp.cos(angles)], axis=-1)
    sine_table = jnp.concatenate([jnp.sin(angles), jnp.sin(angles)], axis=-1)
    return (cosine[:, None, :], sine_table[:, None, :])


def head_forward(raw_heads, gain_vec, cosine, sine_table):
    unit_rows, inv_root = normalize(raw_heads)
    normed = unit_rows * gain_vec
    turned = normed * cosine + rotate_half(normed) * sine_table
    return (turned.astype(jnp.bfloat16), unit_rows, inv_root)


def head_backward(gradient, unit_rows, inv_root, gain_vec, cosine, sine_table):
    normed_grad = gradient * cosine + rotate_back(gradient * sine_table)
    gain_part = jnp.sum(normed_grad * unit_rows, axis=(0, 1))
    return (norm_back(normed_grad, unit_rows, inv_root, gain_vec), gain_part)


def block_mask(first_row, block_rows, seq_len, length):
    row_index = first_row + jnp.arange(block_rows)[:, None]
    col_index = jnp.arange(seq_len)[None, :]
    return (col_index <= row_index) & (col_index < length)


def attend_forward(queries, keys_b, values_b, length, score_scale):
    seq_len, kv_heads, head_size = keys_b.shape
    head_count = queries.shape[1]
    group_size = head_count // kv_heads
    block_rows = min(SCORE_BLOCK, seq_len)
    block_count = seq_len // block_rows
    grouped = queries.reshape(block_count, block_rows, kv_heads, group_size, head_size)
    starts = jnp.arange(block_count, dtype=jnp.int32) * block_rows

    def one_block(inputs):
        qblock, first_row = inputs
        scores = jnp.einsum("qkgd,skd->kgqs", qblock, keys_b, preferred_element_type=jnp.float32)
        allowed = block_mask(first_row, block_rows, seq_len, length)
        logits = jnp.where(allowed, scores * score_scale, MASKED_LOGIT)
        highest = jnp.max(logits, axis=-1, keepdims=True)
        weights_raw = jnp.exp(logits - highest)
        row_total = jnp.sum(weights_raw, axis=-1, keepdims=True)
        probabilities = (weights_raw / row_total).astype(jnp.bfloat16)
        result = jnp.einsum(
            "kgqs,skd->qkgd", probabilities, values_b, preferred_element_type=jnp.float32
        )
        return (result, highest + jnp.log(row_total))

    outputs, log_total = lax.map(one_block, (grouped, starts))
    return (outputs.reshape(seq_len, head_count * head_size), log_total)


def attend_backward(queries, keys_b, values_b, grad_out, log_total, length, score_scale):
    seq_len, kv_heads, head_size = keys_b.shape
    head_count = queries.shape[1]
    group_size = head_count // kv_heads
    block_rows = min(SCORE_BLOCK, seq_len)
    block_count = seq_len // block_rows
    grouped = queries.reshape(block_count, block_rows, kv_heads, group_size, head_size)
    grad_grouped = grad_out.reshape(block_count, block_rows, kv_heads, group_size, head_size)
    starts = jnp.arange(block_count, dtype=jnp.int32) * block_rows

    def one_block(carried, inputs):
        key_grad, value_grad = carried
        qblock, gblock, block_lse, first_row = inputs
        scores = jnp.einsum("qkgd,skd->kgqs", qblock, keys_b, preferred_element_type=jnp.float32)
        allowed = block_mask(first_row, block_rows, seq_len, length)
        logits = jnp.where(allowed, scores * score_scale, MASKED_LOGIT)
        soft = jnp.where(allowed, jnp.exp(logits - block_lse), 0.0)
        probs_low = soft.astype(jnp.bfloat16)
        prob_grad = jnp.einsum(
            "qkgd,skd->kgqs", gblock, values_b, preferred_element_type=jnp.float32
        )
        centre = jnp.sum(soft * prob_grad, axis=-1, keepdims=True)
        score_grad = (score_scale * soft * (prob_grad - centre)).astype(jnp.bfloat16)
        query_grad = jnp.einsum(
            "kgqs,skd->qkgd", score_grad, keys_b, preferred_element_type=jnp.float32
        )
        key_grad = key_grad + jnp.einsum(
            "kgqs,qkgd->skd", score_grad, qblock, preferred_element_type=jnp.float32
        )
        value_grad = value_grad + jnp.einsum(
            "kgqs,qkgd->skd", probs_low, gblock, preferred_element_type=jnp.float32
        )
        return ((key_grad, value_grad), query_grad)

    zero_grad = jnp.zeros((seq_len, kv_heads, head_size), jnp.float32)
    (key_grad, value_grad), query_grads = lax.scan(
        one_block, (zero_grad, zero_grad), (grouped, grad_grouped, log_total, starts)
    )
    return (query_grads.reshape(seq_len, head_count, head_size), key_grad, value_grad)


def body(
    hidden_in,
    lengths,
    attn_gain,
    query_weight,
    key_weight,
    value_weight,
    output_gate,
    query_gain,
    key_gain,
    out_weight,
    mlp_gain,
    gate_weight,
    up_weight,
    down_weight,
    cotangent,
):
    local_rows = hidden_in.shape[0]
    length = lengths[0]
    head_size = query_gain.shape[0]
    kv_heads = key_weight.shape[1] // head_size
    head_count = query_weight.shape[1] // head_size
    score_scale = head_size ** (-0.5)
    position = lax.axis_index("tensor") * local_rows + jnp.arange(local_rows)
    valid_rows = (position < length).astype(jnp.float32)[:, None]
    attn_kept = (
        lax.all_gather(query_weight, "fsdp", axis=0, tiled=True),
        lax.all_gather(key_weight, "fsdp", axis=0, tiled=True),
        lax.all_gather(value_weight, "fsdp", axis=0, tiled=True),
        lax.all_gather(output_gate, "fsdp", axis=0, tiled=True),
        lax.all_gather(out_weight, "fsdp", axis=1, tiled=True),
    )
    query_full, key_full, value_full, gate_full, out_full = attn_kept
    residual = hidden_in.astype(jnp.float32)
    unit_one, root_one = normalize(residual)
    normed_one = rows_in((unit_one * attn_gain).astype(jnp.bfloat16))
    seq_len = normed_one.shape[0]
    cosine, sine_table = rope_tables(seq_len, head_size)
    query_raw = matmul(normed_one, query_full).reshape(seq_len, head_count, head_size)
    key_raw = matmul(normed_one, key_full).reshape(seq_len, kv_heads, head_size)
    value_b = (
        matmul(normed_one, value_full).astype(jnp.bfloat16).reshape(seq_len, kv_heads, head_size)
    )
    gate_pre = matmul(normed_one, gate_full)
    query_b, query_unit, query_root = head_forward(query_raw, query_gain, cosine, sine_table)
    key_b, key_unit, key_root = head_forward(key_raw, key_gain, cosine, sine_table)
    attended, log_total = attend_forward(query_b, key_b, value_b, length, score_scale)
    gate_sig = jax.nn.sigmoid(gate_pre)
    gated_out = (attended * gate_sig).astype(jnp.bfloat16)
    middle = residual + rows_out(matmul(gated_out, out_full))
    unit_two, root_two = normalize(middle)
    normed_two = rows_in((unit_two * mlp_gain).astype(jnp.bfloat16))
    ffn_kept = (
        lax.all_gather(gate_weight, "fsdp", axis=0, tiled=True),
        lax.all_gather(up_weight, "fsdp", axis=0, tiled=True),
        lax.all_gather(down_weight, "fsdp", axis=1, tiled=True),
    )
    gate_weights, up_weights, down_weights = ffn_kept
    ffn_gate = matmul(normed_two, gate_weights)
    ffn_up = matmul(normed_two, up_weights)
    ffn_sig = jax.nn.sigmoid(ffn_gate)
    ffn_act = ffn_gate * ffn_sig
    ffn_mid = (ffn_act * ffn_up).astype(jnp.bfloat16)
    ffn_branch = rows_out(matmul(ffn_mid, down_weights))
    output = ((middle + ffn_branch) * valid_rows).astype(jnp.bfloat16)
    gate_again, up_again, down_again = (
        lax.all_gather(gate_weight, "fsdp", axis=0, tiled=True),
        lax.all_gather(up_weight, "fsdp", axis=0, tiled=True),
        lax.all_gather(down_weight, "fsdp", axis=1, tiled=True),
    )
    query_again, key_again, value_again, gate_attn_again, out_again = (
        lax.all_gather(query_weight, "fsdp", axis=0, tiled=True),
        lax.all_gather(key_weight, "fsdp", axis=0, tiled=True),
        lax.all_gather(value_weight, "fsdp", axis=0, tiled=True),
        lax.all_gather(output_gate, "fsdp", axis=0, tiled=True),
        lax.all_gather(out_weight, "fsdp", axis=1, tiled=True),
    )
    grad_rows = cotangent.astype(jnp.float32) * valid_rows
    branch_full = rows_in(grad_rows.astype(jnp.bfloat16))
    mid_grad = matmul_nt(branch_full, down_again)
    down_grad = matmul_tn(ffn_mid, branch_full)
    gate_grad = (mid_grad * ffn_up * ffn_sig * (1.0 + ffn_gate * (1.0 - ffn_sig))).astype(
        jnp.bfloat16
    )
    up_grad = (mid_grad * ffn_act).astype(jnp.bfloat16)
    gate_w_grad = matmul_tn(normed_two, gate_grad)
    up_w_grad = matmul_tn(normed_two, up_grad)
    norm_two_grad = rows_out(matmul_nt(gate_grad, gate_again) + matmul_nt(up_grad, up_again))
    mlp_gain_part = jnp.sum(norm_two_grad * unit_two, axis=0)
    middle_grad = grad_rows + norm_back(norm_two_grad, unit_two, root_two, mlp_gain)
    ffn_shards = (
        lax.psum_scatter(
            gate_w_grad.astype(jnp.bfloat16), "fsdp", scatter_dimension=0, tiled=True
        ).astype(jnp.float32),
        lax.psum_scatter(
            up_w_grad.astype(jnp.bfloat16), "fsdp", scatter_dimension=0, tiled=True
        ).astype(jnp.float32),
        lax.psum_scatter(
            down_grad.astype(jnp.bfloat16), "fsdp", scatter_dimension=1, tiled=True
        ).astype(jnp.float32),
    )
    attn_full_grad = rows_in(middle_grad.astype(jnp.bfloat16))
    gated_grad = matmul_nt(attn_full_grad, out_again)
    out_grad = matmul_tn(gated_out, attn_full_grad)
    attended_grad = (gated_grad * gate_sig).astype(jnp.bfloat16)
    gate_pre_grad = (gated_grad * attended * gate_sig * (1.0 - gate_sig)).astype(jnp.bfloat16)
    query_grad, key_grad, value_grad = attend_backward(
        query_b,
        key_b,
        value_b,
        attended_grad.reshape(seq_len, head_count, head_size),
        log_total,
        length,
        score_scale,
    )
    query_back, query_gain_part = head_backward(
        query_grad, query_unit, query_root, query_gain, cosine, sine_table
    )
    key_back, key_gain_part = head_backward(
        key_grad, key_unit, key_root, key_gain, cosine, sine_table
    )
    query_send = query_back.reshape(seq_len, head_count * head_size).astype(jnp.bfloat16)
    key_send = key_back.reshape(seq_len, kv_heads * head_size).astype(jnp.bfloat16)
    value_send = value_grad.reshape(seq_len, kv_heads * head_size).astype(jnp.bfloat16)
    norm_one_grad = rows_out(
        matmul_nt(query_send, query_again)
        + matmul_nt(key_send, key_again)
        + matmul_nt(value_send, value_again)
        + matmul_nt(gate_pre_grad, gate_attn_again)
    )
    attn_gain_part = jnp.sum(norm_one_grad * unit_one, axis=0)
    grad_hidden = middle_grad + norm_back(norm_one_grad, unit_one, root_one, attn_gain)
    attn_shards = (
        lax.psum_scatter(
            matmul_tn(normed_one, query_send).astype(jnp.bfloat16),
            "fsdp",
            scatter_dimension=0,
            tiled=True,
        ).astype(jnp.float32),
        lax.psum_scatter(
            matmul_tn(normed_one, key_send).astype(jnp.bfloat16),
            "fsdp",
            scatter_dimension=0,
            tiled=True,
        ).astype(jnp.float32),
        lax.psum_scatter(
            matmul_tn(normed_one, value_send).astype(jnp.bfloat16),
            "fsdp",
            scatter_dimension=0,
            tiled=True,
        ).astype(jnp.float32),
        lax.psum_scatter(
            matmul_tn(normed_one, gate_pre_grad).astype(jnp.bfloat16),
            "fsdp",
            scatter_dimension=0,
            tiled=True,
        ).astype(jnp.float32),
        lax.psum_scatter(
            out_grad.astype(jnp.bfloat16), "fsdp", scatter_dimension=1, tiled=True
        ).astype(jnp.float32),
    )
    gain_totals = lax.psum(
        (attn_gain_part, query_gain_part, key_gain_part, mlp_gain_part), ("fsdp", "tensor")
    )
    return (
        output,
        grad_hidden,
        gain_totals[0],
        attn_shards[0],
        attn_shards[1],
        attn_shards[2],
        attn_shards[3],
        gain_totals[1],
        gain_totals[2],
        attn_shards[4],
        gain_totals[3],
        ffn_shards[0],
        ffn_shards[1],
        ffn_shards[2],
    )


def solution(mesh):
    return jax.shard_map(
        body,
        mesh=mesh,
        in_specs=(
            P(("fsdp", "tensor"), None),
            P("fsdp"),
            P(),
            P("fsdp", "tensor"),
            P("fsdp", "tensor"),
            P("fsdp", "tensor"),
            P("fsdp", "tensor"),
            P(),
            P(),
            P("tensor", "fsdp"),
            P(),
            P("fsdp", "tensor"),
            P("fsdp", "tensor"),
            P("tensor", "fsdp"),
            P(("fsdp", "tensor"), None),
        ),
        out_specs=(
            P(("fsdp", "tensor"), None),
            P(("fsdp", "tensor"), None),
            P(),
            P("fsdp", "tensor"),
            P("fsdp", "tensor"),
            P("fsdp", "tensor"),
            P("fsdp", "tensor"),
            P(),
            P(),
            P("tensor", "fsdp"),
            P(),
            P("fsdp", "tensor"),
            P("fsdp", "tensor"),
            P("tensor", "fsdp"),
        ),
        check_vma=False,
    )
```

profile of v0, /device:TPU:0, one launch (start us, length us, event | category | flops | bytes accessed | tf_op | source)
XLA Modules:
  0.0 1791.3 jit_solution(14274165698364133224)
XLA Ops:
  23.3 29.7 %all-gather.17.cloned.1.call-done = bf16[2048,256]{1,0:T(8,128)(2,1)} async-done(((bf16[256,256]{1,0:T(8,128)(2,1)}), bf16[2048,256]{1,0:T(8,128)(2,1)}) %all-gather.17.cloned.1.call-update) | async-done | bytes 1048592 | tf_op jit(solution)/shard_map/all_gather | solution.py:179
  53.0 35.4 %all-gather.13.cloned.1.call-done = bf16[1024,2048]{1,0:T(8,128)(2,1)} async-done(((bf16[256,2048]{1,0:T(8,128)(2,1)}), bf16[1024,2048]{1,0:T(8,128)(2,1)}) %all-gather.13.cloned.1.call-update) | async-done | bytes 4194320 | tf_op jit(solution)/shard_map/all_gather | solution.py:13
  93.9 46.0 %all-gather.15.cloned.1.call-done = bf16[2048,512]{1,0:T(8,128)(2,1)} async-done(((bf16[256,512]{1,0:T(8,128)(2,1)}), bf16[2048,512]{1,0:T(8,128)(2,1)}) %all-gather.15.cloned.1.call-update) | async-done | bytes 2097168 | tf_op jit(solution)/shard_map/all_gather | solution.py:178
  184.6 23.4 %while.27 = (s32[]{:T(128)}, f32[2,512,2,2,128]{4,3,2,1,0:T(2,128)}, f32[2,2,2,512,1]{3,2,1,4,0:T(2,128)S(1)}, s32[2]{0:T(128)S(1)}, s32[]{:T(128)}, /*index=5*/...) while((s32[]{:T(128)}, ...), condition=%wide.region_6.7_spmd, body=%wide.region_3.6_spmd.sunk | while | flops 1099955712 | bytes 32053880 | solution.py:107
  212.7 17.9 all-gather.21.cloned.1.call-done
  238.0 44.1 %all-gather.23.cloned.1.call-done = bf16[512,2048]{1,0:T(8,128)(2,1)} async-done(((bf16[512,256]{1,0:T(8,128)(2,1)}), bf16[512,2048]{1,0:T(8,128)(2,1)}) %all-gather.23.cloned.1.call-update) | async-done | bytes 2097168 | tf_op jit(solution)/shard_map/all_gather | solution.py:182
  290.2 69.2 %reduce-scatter.13.cloned.1.call-done = f32[256,2048]{1,0:T(8,128)} async-done(((f32[1024,2048]{1,0:T(8,128)}), f32[256,2048]{1,0:T(8,128)}) %reduce-scatter.13.cloned.1.call-update) | async-done | bytes 2097168 | tf_op jit(solution)/shard_map/reduce_scatter | solution.py:17
  366.0 94.9 %all-gather.27.cloned.1.call-done = bf16[2048,1536]{1,0:T(8,128)(2,1)} async-done(((bf16[256,1536]{1,0:T(8,128)(2,1)}), bf16[2048,1536]{1,0:T(8,128)(2,1)}) %all-gather.27.cloned.1.call-update) | async-done | bytes 6291472 | tf_op jit(solution)/shard_map/all_gather | solution.py:205
  460.9 34.9 %all-gather.25.cloned.1.call-done = bf16[1024,2048]{1,0:T(8,128)(2,1)} async-done(((bf16[256,2048]{1,0:T(8,128)(2,1)}), bf16[1024,2048]{1,0:T(8,128)(2,1)}) %all-gather.25.cloned.1.call-update) | async-done | bytes 4194320 | tf_op jit(solution)/shard_map/all_gather | solution.py:13
  507.6 89.5 %all-gather.29.cloned.1.call-done = bf16[2048,1536]{1,0:T(8,128)(2,1)} async-done(((bf16[256,1536]{1,0:T(8,128)(2,1)}), bf16[2048,1536]{1,0:T(8,128)(2,1)}) %all-gather.29.cloned.1.call-update) | async-done | bytes 6291472 | tf_op jit(solution)/shard_map/all_gather | solution.py:206
  608.9 23.2 %all-gather.33.cloned.1.call-done = bf16[1024,2048]{1,0:T(8,128)(2,1)} async-done(((bf16[256,2048]{1,0:T(8,128)(2,1)}), bf16[1024,2048]{1,0:T(8,128)(2,1)}) %all-gather.33.cloned.1.call-update) | async-done | bytes 4194320 | tf_op jit(solution)/shard_map/all_gather | solution.py:13
  632.1 102.1 %all-gather.31.cloned.1.call-done = bf16[1536,2048]{1,0:T(8,128)(2,1)} async-done(((bf16[1536,256]{1,0:T(8,128)(2,1)}), bf16[1536,2048]{1,0:T(8,128)(2,1)}) %all-gather.31.cloned.1.call-update) | async-done | bytes 6291472 | tf_op jit(solution)/shard_map/all_gather | solution.py:207
  783.7 57.8 %reduce-scatter.17.cloned.1.call-done = f32[256,2048]{1,0:T(8,128)} async-done(((f32[1024,2048]{1,0:T(8,128)}), f32[256,2048]{1,0:T(8,128)}) %reduce-scatter.17.cloned.1.call-update) | async-done | bytes 2097168 | tf_op jit(solution)/shard_map/reduce_scatter | solution.py:17
  844.2 71.4 %reduce-scatter.15.cloned.1.call-done = f32[256,2048]{1,0:T(8,128)} async-done(((f32[1024,2048]{1,0:T(8,128)}), f32[256,2048]{1,0:T(8,128)}) %reduce-scatter.15.cloned.1.call-update) | async-done | bytes 2097168 | tf_op jit(solution)/shard_map/reduce_scatter | solution.py:17
  969.1 48.3 %while.28 = (s32[]{:T(128)}, f32[1024,2,128]{0,2,1:T(8,128)S(1)}, f32[1024,2,128]{0,2,1:T(8,128)S(1)}, f32[2,512,2,2,128]{4,1,3,2,0:T(8,128)}, bf16[2,512,2,2,12...) while((s32[]{:T(128)}, f32[1024,2,128]{0,2,1:T(8,128)S(1)}, ...), condition=%wide.region_14.15_spmd.clone, body=%wide.region_12.14_spmd.clone.sunk | while | flops 2709519872 | bytes 162577680 | solution.py:146
  1103.6 94.8 %reduce-scatter.33.cloned.1.call-done = bf16[256,1536]{1,0:T(8,128)(2,1)} async-done(((bf16[2048,1536]{1,0:T(8,128)(2,1)}), bf16[256,1536]{1,0:T(8,128)(2,1)}) %reduce-scatter.33.cloned.1.call-update) | async-done | bytes 786448 | tf_op jit(solution)/shard_map/reduce_scatter | solution.py:246
  1200.8 119.0 %reduce-scatter.35.cloned.1.call-done = bf16[1536,256]{1,0:T(8,128)(2,1)} async-done(((bf16[1536,2048]{1,0:T(8,128)(2,1)}), bf16[1536,256]{1,0:T(8,128)(2,1)}) %reduce-scatter.35.cloned.1.call-update) | async-done | bytes 786448 | tf_op jit(solution)/shard_map/reduce_scatter | solution.py:249
  1322.2 64.0 %reduce-scatter.23.cloned.1.call-done = bf16[256,256]{1,0:T(8,128)(2,1)} async-done(((bf16[2048,256]{1,0:T(8,128)(2,1)}), bf16[256,256]{1,0:T(8,128)(2,1)}) %reduce-scatter.23.cloned.1.call-update) | async-done | bytes 131088 | tf_op jit(solution)/shard_map/reduce_scatter | solution.py:291
  1387.8 64.2 %reduce-scatter.25.cloned.1.call-done = bf16[256,256]{1,0:T(8,128)(2,1)} async-done(((bf16[2048,256]{1,0:T(8,128)(2,1)}), bf16[256,256]{1,0:T(8,128)(2,1)}) %reduce-scatter.25.cloned.1.call-update) | async-done | bytes 131088 | tf_op jit(solution)/shard_map/reduce_scatter | solution.py:297
  1453.6 69.5 %reduce-scatter.21.cloned.1.call-done = bf16[256,512]{1,0:T(8,128)(2,1)} async-done(((bf16[2048,512]{1,0:T(8,128)(2,1)}), bf16[256,512]{1,0:T(8,128)(2,1)}) %reduce-scatter.21.cloned.1.call-update) | async-done | bytes 262160 | tf_op jit(solution)/shard_map/reduce_scatter | solution.py:285
  1524.9 69.3 %reduce-scatter.29.cloned.1.call-done = bf16[512,256]{1,0:T(8,128)(2,1)} async-done(((bf16[512,2048]{1,0:T(8,128)(2,1)}), bf16[512,256]{1,0:T(8,128)(2,1)}) %reduce-scatter.29.cloned.1.call-update) | async-done | bytes 262160 | tf_op jit(solution)/shard_map/reduce_scatter | solution.py:309
  1595.9 69.0 %reduce-scatter.27.cloned.1.call-done = bf16[256,512]{1,0:T(8,128)(2,1)} async-done(((bf16[2048,512]{1,0:T(8,128)(2,1)}), bf16[256,512]{1,0:T(8,128)(2,1)}) %reduce-scatter.27.cloned.1.call-update) | async-done | bytes 262160 | tf_op jit(solution)/shard_map/reduce_scatter | solution.py:303
  1666.7 71.6 %reduce-scatter.19.cloned.1.call-done = f32[256,2048]{1,0:T(8,128)} async-done(((f32[1024,2048]{1,0:T(8,128)}), f32[256,2048]{1,0:T(8,128)}) %reduce-scatter.19.cloned.1.call-update) | async-done | bytes 2097168 | tf_op jit(solution)/shard_map/reduce_scatter | solution.py:17
  1740.7 39.8 %all-reduce = (f32[2048]{0:T(1024)}, f32[128]{0:T(128)}, f32[128]{0:T(128)}, f32[2048]{0:T(1024)}) all-reduce(f32[2048]{0:T(1024)S(1)} %get-tuple-element.199, f32[128]{0:T(128)S(1)} %get-tuple-element.195, f32[128]{0:T(128)S(1)} %get-tuple-element.201, f32[2048]{0:T(1024)S(1)} %copy-done.48), channel_id=1, replica_groups=mesh['fsdp'=8,'tensor'=4] {'fsdp','tensor'}, use_global_device_ids=true, to_apply=%region_20.21 | all-reduce | flops 4352 | bytes 34816 | tf_op jit(solution)/shard_map/psum | solution.py:313
  (339 shorter events, 397.5 us)
Async XLA Ops:
  7.2 45.8 %all-gather.17.cloned.1.call-start = ((), (), s32[]{:S(2)}) async-start(), calls=%async_computation.14 | async-start | bytes 1179648 | tf_op jit(solution)/shard_map/all_gather | solution.py:179
  7.9 80.5 %all-gather.13.cloned.1.call-start = ((), (), s32[]{:S(2)}) async-start(), calls=%async_computation.12 | async-start | bytes 5242880 | tf_op jit(solution)/shard_map/all_gather | solution.py:13
  12.6 127.3 %all-gather.15.cloned.1.call-start = ((), (), s32[]{:S(2)}) async-start(), calls=%async_computation.13 | async-start | bytes 2359296 | tf_op jit(solution)/shard_map/all_gather | solution.py:178
  13.3 167.2 %all-gather.19.cloned.1.call-start = ((), (), s32[]{:S(2)}) async-start(), calls=%async_computation.15 | async-start | bytes 1179648 | tf_op jit(solution)/shard_map/all_gather | solution.py:180
  13.9 216.7 %all-gather.21.cloned.1.call-start = ((), (), s32[]{:S(2)}) async-start(), calls=%async_computation.16 | async-start | bytes 2359296 | tf_op jit(solution)/shard_map/all_gather | solution.py:181
  14.5 267.6 %all-gather.23.cloned.1.call-start = ((), (), s32[]{:S(2)}) async-start(), calls=%async_computation.17 | async-start | bytes 2359296 | tf_op jit(solution)/shard_map/all_gather | solution.py:182
  15.1 344.3 %reduce-scatter.13.cloned.1.call-start = ((), (), s32[]{:S(2)}) async-start(), calls=%async_computation.18 | async-start | bytes 10485760 | tf_op jit(solution)/shard_map/reduce_scatter | solution.py:17
  289.4 171.5 %all-gather.27.cloned.1.call-start = ((), (), s32[]{:S(2)}) async-start(), calls=%async_computation.20 | async-start | bytes 7077888 | tf_op jit(solution)/shard_map/all_gather | solution.py:205
  290.1 205.7 %all-gather.25.cloned.1.call-start = ((), (), s32[]{:S(2)}) async-start(), calls=%async_computation.19 | async-start | bytes 5242880 | tf_op jit(solution)/shard_map/all_gather | solution.py:13
  362.6 234.5 %all-gather.29.cloned.1.call-start = ((), (), s32[]{:S(2)}) async-start(), calls=%async_computation.21 | async-start | bytes 7077888 | tf_op jit(solution)/shard_map/all_gather | solution.py:206
  363.2 268.8 %all-gather.33.cloned.1.call-start = ((), (), s32[]{:S(2)}) async-start(), calls=%async_computation.24 | async-start | bytes 5242880 | tf_op jit(solution)/shard_map/all_gather | solution.py:13
  365.3 368.8 %all-gather.31.cloned.1.call-start = ((), (), s32[]{:S(2)}) async-start(), calls=%async_computation.22 | async-start | bytes 7077888 | tf_op jit(solution)/shard_map/all_gather | solution.py:207
  365.9 475.6 %reduce-scatter.17.cloned.1.call-start = ((), (), s32[]{:S(2)}) async-start(), calls=%async_computation.25 | async-start | bytes 10485760 | tf_op jit(solution)/shard_map/reduce_scatter | solution.py:17
  771.4 144.3 %reduce-scatter.15.cloned.1.call-start = ((), (), s32[]{:S(2)}) async-start(), calls=%async_computation.23 | async-start | bytes 10485760 | tf_op jit(solution)/shard_map/reduce_scatter | solution.py:17
  783.6 175.2 %all-gather.35.cloned.1.call-start = ((), (), s32[]{:S(2)}) async-start(), calls=%async_computation.26 | async-start | bytes 5242880 | tf_op jit(solution)/shard_map/all_gather | solution.py:13
  920.8 180.3 %reduce-scatter.31.cloned.1.call-start = ((), (), s32[]{:S(2)}) async-start(), calls=%async_computation.33 | async-start | bytes 7077888 | tf_op jit(solution)/shard_map/reduce_scatter | solution.py:243
  932.4 265.9 %reduce-scatter.33.cloned.1.call-start = ((), (), s32[]{:S(2)}) async-start(), calls=%async_computation.34 | async-start | bytes 7077888 | tf_op jit(solution)/shard_map/reduce_scatter | solution.py:246
  945.8 373.9 %reduce-scatter.35.cloned.1.call-start = ((), (), s32[]{:S(2)}) async-start(), calls=%async_computation.35 | async-start | bytes 7077888 | tf_op jit(solution)/shard_map/reduce_scatter | solution.py:249
  958.7 427.5 %reduce-scatter.23.cloned.1.call-start = ((), (), s32[]{:S(2)}) async-start(), calls=%async_computation.29 | async-start | bytes 1179648 | tf_op jit(solution)/shard_map/reduce_scatter | solution.py:291
  1023.7 428.2 %reduce-scatter.25.cloned.1.call-start = ((), (), s32[]{:S(2)}) async-start(), calls=%async_computation.30 | async-start | bytes 1179648 | tf_op jit(solution)/shard_map/reduce_scatter | solution.py:297
  1036.9 486.1 %reduce-scatter.21.cloned.1.call-start = ((), (), s32[]{:S(2)}) async-start(), calls=%async_computation.28 | async-start | bytes 2359296 | tf_op jit(solution)/shard_map/reduce_scatter | solution.py:285
  1067.1 527.1 %reduce-scatter.29.cloned.1.call-start = ((), (), s32[]{:S(2)}) async-start(), calls=%async_computation.32 | async-start | bytes 2359296 | tf_op jit(solution)/shard_map/reduce_scatter | solution.py:309
  1074.2 590.7 %reduce-scatter.27.cloned.1.call-start = ((), (), s32[]{:S(2)}) async-start(), calls=%async_computation.31 | async-start | bytes 2359296 | tf_op jit(solution)/shard_map/reduce_scatter | solution.py:303
  1081.3 657.0 %reduce-scatter.19.cloned.1.call-start = ((), (), s32[]{:S(2)}) async-start(), calls=%async_computation.27 | async-start | bytes 10485760 | tf_op jit(solution)/shard_map/reduce_scatter | solution.py:17
  (74 other events, 2256.7 us)
Sparse Core Ops, SparseCore 0:
  10.1 42.8 all-gather.16
  55.2 33.2 all-gather.12
  90.6 49.2 all-gather.14
  141.9 38.6 all-gather.18
  182.5 48.0 all-gather.20
  232.5 49.5 all-gather.22
  289.5 69.8 reduce-scatter.12
  361.8 99.0 all-gather.26
  463.1 32.6 all-gather.24
  498.1 99.0 all-gather.28
  599.4 32.6 all-gather.32
  634.1 99.9 all-gather.30
  771.5 69.9 reduce-scatter.16
  843.9 71.7 reduce-scatter.14
  920.9 34.4 all-gather.34
  959.3 117.9 reduce-scatter.30
  1081.2 117.0 reduce-scatter.32
  1202.2 117.4 reduce-scatter.34
  1323.5 62.5 reduce-scatter.22
  1389.4 62.5 reduce-scatter.24
  1456.5 66.5 reduce-scatter.20
  1527.0 67.0 reduce-scatter.28
  1598.1 66.7 reduce-scatter.26
  1667.5 70.7 reduce-scatter.18
where the time goes:
time: 1800 us; the launch traced here: 1790 us
  waiting for transfers between devices  1360 us (76%)
  matrix products  218 us (12%)
  other arithmetic  85.1 us (5%)
  local copies, waits for them, and re-layouts  71.1 us (4%)
  blocking collectives  39.8 us (2%)
    reduce_scatter x4, waiting for transfers between devices, rows_out(): return lax.psum_scatter(values, 'tensor', scatter_dimension=0, tiled=True)  270 us
    reduce_scatter x1, waiting for transfers between devices, body(): lax.psum_scatter(down_grad.astype(jnp.bfloat16), 'fsdp', scatter_dimensio...  119 us
    all_gather x1, waiting for transfers between devices, body(): lax.all_gather(down_weight, 'fsdp', axis=1, tiled=True)  102 us
    all_gather x1, waiting for transfers between devices, body(): lax.all_gather(gate_weight, 'fsdp', axis=0, tiled=True)  94.9 us
    reduce_scatter x1, waiting for transfers between devices, body(): lax.psum_scatter(up_w_grad.astype(jnp.bfloat16), 'fsdp', scatter_dimensio...  94.8 us
    all_gather x4, waiting for transfers between devices, rows_in(): return lax.all_gather(values, 'tensor', axis=0, tiled=True)  93.5 us
    all_gather x1, waiting for transfers between devices, body(): lax.all_gather(up_weight, 'fsdp', axis=0, tiled=True)  89.5 us
    reduce_scatter x1, waiting for transfers between devices, body(): lax.psum_scatter(matmul_tn(normed_one, query_send).astype(jnp.bfloat16),...  69.5 us
  transfers between devices with their start and end apart: 24, of which 22 were waited for; matrix products, arithmetic and copies ran while one was open for 16% of the time, Pallas kernels for 0%

commit v1 on v0

v1 whole, which is shorter than its diff:
```python
import jax
import jax.numpy as jnp
from jax import lax
from jax.sharding import PartitionSpec as P

NORM_EPSILON = 1e-06
ROPE_THETA = 1000000.0
SCORE_BLOCK = 512
MASKED_LOGIT = -1e30
F32 = jnp.float32
BF16 = jnp.bfloat16


def exchange(values, axis, size, mask):
    return lax.ppermute(values, axis, [(i, i ^ mask) for i in range(size)])


def position_mask(position, count):
    half = count // 2
    return (position // half) | ((position % half) << 1)


def gather_blocks(shard, count, axis):
    half = count // 2
    near = [shard]
    far = [exchange(shard, "fsdp", count, 1)]
    for step in range(1, half):
        near.append(exchange(shard, "fsdp", count, step << 1))
    for step in range(1, half):
        far.append(exchange(near[step], "fsdp", count, 1))
    return jnp.concatenate(near + far, axis=axis)


def scatter_blocks(near, far, count, axis):
    half = count // 2
    arrived = exchange(far.astype(BF16), "fsdp", count, 1)
    width = near.shape[axis] // half
    total = near.astype(F32) + arrived.astype(F32)
    pieces = [lax.slice_in_dim(total, i * width, (i + 1) * width, axis=axis) for i in range(half)]
    result = pieces[0]
    moved = [
        exchange(pieces[step].astype(BF16), "fsdp", count, step << 1) for step in range(1, half)
    ]
    for piece in moved:
        result = result + piece.astype(F32)
    return result


def to_relative(values, me, count):
    width = values.shape[-1] // count
    parts = [
        lax.dynamic_slice_in_dim(
            values, (me ^ position_mask(p, count)) * width, width, axis=values.ndim - 1
        )
        for p in range(count)
    ]
    return jnp.concatenate(parts, axis=-1)


def to_absolute(values, me, count):
    width = values.shape[-1] // count
    half = count // 2
    parts = []
    for block in range(count):
        mask = me ^ block
        place = (mask & 1) * half + (mask >> 1)
        parts.append(lax.dynamic_slice_in_dim(values, place * width, width, axis=values.ndim - 1))
    return jnp.concatenate(parts, axis=-1)


def row_masks(count):
    half = count // 2
    return [((p % half) << 1) | (p // half) for p in range(count)]


def rows_in(values, count):
    half = count // 2
    near = [values] + [exchange(values, "tensor", count, step << 1) for step in range(1, half)]
    far = [exchange(piece, "tensor", count, 1) for piece in near]
    return jnp.concatenate(near + far, axis=0)


def rows_out(partial, count):
    half = count // 2
    rows = partial.shape[0] // count
    blocks = [partial[p * rows : (p + 1) * rows] for p in range(count)]
    sums = [None] * half
    for step in list(range(1, half)) + [0]:
        arrived = exchange(blocks[half + step].astype(BF16), "tensor", count, 1)
        sums[step] = blocks[step].astype(F32) + arrived.astype(F32)
    result = sums[0]
    for step in range(1, half):
        result = result + exchange(sums[step].astype(BF16), "tensor", count, step << 1).astype(F32)
    return result


def sum_everywhere(values, axes):
    for axis, count in axes:
        mask = 1
        while mask < count:
            values = values + exchange(values, axis, count, mask)
            mask <<= 1
    return values


def matmul(first_op, second_op):
    return jnp.dot(first_op, second_op, preferred_element_type=F32)


def matmul_tn(first_op, second_op):
    return lax.dot_general(
        first_op, second_op, (((0,), (0,)), ((), ())), preferred_element_type=F32
    )


def matmul_nt(first_op, second_op):
    return lax.dot_general(
        first_op, second_op, (((1,), (1,)), ((), ())), preferred_element_type=F32
    )


def normalize(values):
    inv_root = lax.rsqrt(jnp.mean(values * values, axis=-1, keepdims=True) + NORM_EPSILON)
    return (values * inv_root, inv_root)


def norm_back(gradient, unit_rows, inv_root, gain_vec):
    scaled = gradient * gain_vec
    return inv_root * (scaled - unit_rows * jnp.mean(scaled * unit_rows, axis=-1, keepdims=True))


def rotate_half(values):
    half_width = values.shape[-1] // 2
    return jnp.concatenate([-values[..., half_width:], values[..., :half_width]], axis=-1)


def rotate_back(values):
    half_width = values.shape[-1] // 2
    return jnp.concatenate([values[..., half_width:], -values[..., :half_width]], axis=-1)


def rope_tables(slots, head_size):
    half_width = head_size // 2
    inverse = ROPE_THETA ** (-(jnp.arange(half_width, dtype=F32) * 2.0 / head_size))
    angles = slots.astype(F32)[:, None] * inverse[None, :]
    cosine = jnp.concatenate([jnp.cos(angles), jnp.cos(angles)], axis=-1)
    sine_table = jnp.concatenate([jnp.sin(angles), jnp.sin(angles)], axis=-1)
    return (cosine[:, None, :], sine_table[:, None, :])


def head_forward(raw_heads, gain_vec, cosine, sine_table):
    unit_rows, inv_root = normalize(raw_heads)
    normed = unit_rows * gain_vec
    turned = normed * cosine + rotate_half(normed) * sine_table
    return (turned.astype(BF16), unit_rows, inv_root)


def head_backward(gradient, unit_rows, inv_root, gain_vec, cosine, sine_table):
    normed_grad = gradient * cosine + rotate_back(gradient * sine_table)
    gain_part = jnp.sum(normed_grad * unit_rows, axis=(0, 1))
    return (norm_back(normed_grad, unit_rows, inv_root, gain_vec), gain_part)


def block_mask(row_slots, col_slots, length):
    rows, cols = row_slots[:, None], col_slots[None, :]
    return (cols <= rows) & (cols < length)


def attend_forward(queries, keys_b, values_b, slots, length, score_scale):
    seq_len, kv_heads, head_size = keys_b.shape
    head_count = queries.shape[1]
    group_size = head_count // kv_heads
    block_rows = min(SCORE_BLOCK, seq_len)
    block_count = seq_len // block_rows
    grouped = queries.reshape(block_count, block_rows, kv_heads, group_size, head_size)

    def one_block(inputs):
        qblock, row_slots = inputs
        scores = jnp.einsum("qkgd,skd->kgqs", qblock, keys_b, preferred_element_type=F32)
        allowed = block_mask(row_slots, slots, length)
        logits = jnp.where(allowed, scores * score_scale, MASKED_LOGIT)
        highest = jnp.max(logits, axis=-1, keepdims=True)
        weights_raw = jnp.exp(logits - highest)
        row_total = jnp.sum(weights_raw, axis=-1, keepdims=True)
        probabilities = (weights_raw / row_total).astype(BF16)
        result = jnp.einsum("kgqs,skd->qkgd", probabilities, values_b, preferred_element_type=F32)
        return (result, highest + jnp.log(row_total))

    outputs, log_total = lax.map(one_block, (grouped, slots.reshape(block_count, block_rows)))
    return (outputs.reshape(seq_len, head_count * head_size), log_total)


def attend_backward(queries, keys_b, values_b, grad_out, log_total, slots, length, score_scale):
    seq_len, kv_heads, head_size = keys_b.shape
    head_count = queries.shape[1]
    group_size = head_count // kv_heads
    block_rows = min(SCORE_BLOCK, seq_len)
    block_count = seq_len // block_rows
    grouped = queries.reshape(block_count, block_rows, kv_heads, group_size, head_size)
    grad_grouped = grad_out.reshape(block_count, block_rows, kv_heads, group_size, head_size)

    def one_block(carried, inputs):
        key_grad, value_grad = carried
        qblock, gblock, block_lse, row_slots = inputs
        scores = jnp.einsum("qkgd,skd->kgqs", qblock, keys_b, preferred_element_type=F32)
        allowed = block_mask(row_slots, slots, length)
        logits = jnp.where(allowed, scores * score_scale, MASKED_LOGIT)
        soft = jnp.where(allowed, jnp.exp(logits - block_lse), 0.0)
        probs_low = soft.astype(BF16)
        prob_grad = jnp.einsum("qkgd,skd->kgqs", gblock, values_b, preferred_element_type=F32)
        centre = jnp.sum(soft * prob_grad, axis=-1, keepdims=True)
        score_grad = (score_scale * soft * (prob_grad - centre)).astype(BF16)
        query_grad = jnp.einsum("kgqs,skd->qkgd", score_grad, keys_b, preferred_element_type=F32)
        key_grad = key_grad + jnp.einsum(
            "kgqs,qkgd->skd", score_grad, qblock, preferred_element_type=F32
        )
        value_grad = value_grad + jnp.einsum(
            "kgqs,qkgd->skd", probs_low, gblock, preferred_element_type=F32
        )
        return ((key_grad, value_grad), query_grad)

    zero_grad = jnp.zeros((seq_len, kv_heads, head_size), F32)
    (key_grad, value_grad), query_grads = lax.scan(
        one_block,
        (zero_grad, zero_grad),
        (grouped, grad_grouped, log_total, slots.reshape(block_count, block_rows)),
    )
    return (query_grads.reshape(seq_len, head_count, head_size), key_grad, value_grad)


def body(
    members,
    shares,
    hidden_in,
    lengths,
    attn_gain,
    query_weight,
    key_weight,
    value_weight,
    output_gate,
    query_gain,
    key_gain,
    out_weight,
    mlp_gain,
    gate_weight,
    up_weight,
    down_weight,
    cotangent,
):
    me = lax.axis_index("fsdp")
    share = lax.axis_index("tensor")
    local_rows = hidden_in.shape[0]
    length = lengths[0]
    head_size = query_gain.shape[0]
    key_width = key_weight.shape[1]
    query_width = query_weight.shape[1]
    kv_heads = key_width // head_size
    head_count = query_width // head_size
    score_scale = head_size ** (-0.5)
    steps = jnp.arange(local_rows)
    slots = jnp.concatenate([(share ^ mask) * local_rows + steps for mask in row_masks(shares)])
    valid_rows = (slots[:local_rows] < length).astype(F32)[:, None]
    seq_len = slots.shape[0]

    def relative(values):
        return to_relative(values, me, members)

    def absolute(values):
        return to_absolute(values, me, members)

    attn_gain, mlp_gain = relative(attn_gain), relative(mlp_gain)

    qkv_full = gather_blocks(
        jnp.concatenate([query_weight, key_weight, value_weight], axis=1), members, 0
    )
    gate_full = gather_blocks(output_gate, members, 0)
    out_full = gather_blocks(out_weight, members, 1)

    residual = relative(hidden_in).astype(F32)
    unit_one, root_one = normalize(residual)
    normed_one = rows_in((unit_one * attn_gain).astype(BF16), shares)
    cosine, sine_table = rope_tables(slots, head_size)
    qkv_raw = matmul(normed_one, qkv_full)
    query_raw = qkv_raw[:, :query_width].reshape(seq_len, head_count, head_size)
    key_raw = qkv_raw[:, query_width : query_width + key_width].reshape(
        seq_len, kv_heads, head_size
    )
    value_b = qkv_raw[:, query_width + key_width :].astype(BF16)
    value_b = value_b.reshape(seq_len, kv_heads, head_size)
    gate_pre = matmul(normed_one, gate_full)
    query_b, query_unit, query_root = head_forward(query_raw, query_gain, cosine, sine_table)
    key_b, key_unit, key_root = head_forward(key_raw, key_gain, cosine, sine_table)
    attended, log_total = attend_forward(query_b, key_b, value_b, slots, length, score_scale)
    gate_sig = jax.nn.sigmoid(gate_pre)
    gated_out = (attended * gate_sig).astype(BF16)
    middle = residual + rows_out(matmul(gated_out, out_full), shares)
    unit_two, root_two = normalize(middle)
    normed_two = rows_in((unit_two * mlp_gain).astype(BF16), shares)

    gate_weights = gather_blocks(gate_weight, members, 0)
    up_weights = gather_blocks(up_weight, members, 0)
    down_weights = gather_blocks(down_weight, members, 1)
    grad_rows = relative(cotangent).astype(F32) * valid_rows
    branch_full = rows_in(grad_rows.astype(BF16), shares)

    ffn_gate = matmul(normed_two, gate_weights)
    ffn_up = matmul(normed_two, up_weights)
    ffn_sig = jax.nn.sigmoid(ffn_gate)
    ffn_act = ffn_gate * ffn_sig
    ffn_mid = (ffn_act * ffn_up).astype(BF16)

    def scatter_rows(acts, grads):
        half = acts.shape[1] // 2
        far = matmul_tn(acts[:, half:], grads).astype(BF16)
        near = matmul_tn(acts[:, :half], grads)
        return scatter_blocks(near, far, members, 0)

    def scatter_cols(acts, grads):
        half = grads.shape[1] // 2
        far = matmul_tn(acts, grads[:, half:]).astype(BF16)
        near = matmul_tn(acts, grads[:, :half])
        return scatter_blocks(near, far, members, 1)

    down_shard = scatter_cols(ffn_mid, branch_full)
    mid_grad = matmul_nt(branch_full, down_weights)
    gate_grad = (mid_grad * ffn_up * ffn_sig * (1.0 + ffn_gate * (1.0 - ffn_sig))).astype(BF16)
    up_grad = (mid_grad * ffn_act).astype(BF16)
    norm_two_grad = rows_out(
        matmul_nt(gate_grad, gate_weights) + matmul_nt(up_grad, up_weights), shares
    )
    gate_shard = scatter_rows(normed_two, gate_grad)
    up_shard = scatter_rows(normed_two, up_grad)
    ffn_branch = rows_out(matmul(ffn_mid, down_weights), shares)
    output = absolute(((middle + ffn_branch) * valid_rows).astype(BF16))

    mlp_gain_part = jnp.sum(norm_two_grad * unit_two, axis=0)
    middle_grad = grad_rows + norm_back(norm_two_grad, unit_two, root_two, mlp_gain)
    attn_full_grad = rows_in(middle_grad.astype(BF16), shares)
    gated_grad = matmul_nt(attn_full_grad, out_full)
    out_shard = scatter_cols(gated_out, attn_full_grad)
    attended_grad = (gated_grad * gate_sig).astype(BF16)
    gate_pre_grad = (gated_grad * attended * gate_sig * (1.0 - gate_sig)).astype(BF16)
    gate_attn_shard = scatter_rows(normed_one, gate_pre_grad)
    query_grad, key_grad, value_grad = attend_backward(
        query_b,
        key_b,
        value_b,
        attended_grad.reshape(seq_len, head_count, head_size),
        log_total,
        slots,
        length,
        score_scale,
    )
    query_back, query_gain_part = head_backward(
        query_grad, query_unit, query_root, query_gain, cosine, sine_table
    )
    key_back, key_gain_part = head_backward(
        key_grad, key_unit, key_root, key_gain, cosine, sine_table
    )
    qkv_send = jnp.concatenate(
        [
            query_back.reshape(seq_len, query_width).astype(BF16),
            key_back.reshape(seq_len, key_width).astype(BF16),
            value_grad.reshape(seq_len, key_width).astype(BF16),
        ],
        axis=1,
    )
    qkv_shard = scatter_rows(normed_one, qkv_send)
    norm_one_grad = rows_out(
        matmul_nt(qkv_send, qkv_full) + matmul_nt(gate_pre_grad, gate_full), shares
    )
    attn_gain_part = jnp.sum(norm_one_grad * unit_one, axis=0)
    grad_hidden = absolute(
        middle_grad + norm_back(norm_one_grad, unit_one, root_one, attn_gain)
    )
    width = hidden_in.shape[1]
    gain_totals = sum_everywhere(
        jnp.concatenate(
            [absolute(attn_gain_part), absolute(mlp_gain_part), query_gain_part, key_gain_part]
        ),
        (("tensor", shares), ("fsdp", members)),
    )
    return (
        output,
        grad_hidden,
        gain_totals[:width],
        qkv_shard[:, :query_width],
        qkv_shard[:, query_width : query_width + key_width],
        qkv_shard[:, query_width + key_width :],
        gate_attn_shard,
        gain_totals[2 * width : 2 * width + head_size],
        gain_totals[2 * width + head_size :],
        out_shard,
        gain_totals[width : 2 * width],
        gate_shard,
        up_shard,
        down_shard,
    )


def solution(mesh):
    members, shares = mesh.shape["fsdp"], mesh.shape["tensor"]

    def layer(*operands):
        return body(members, shares, *operands)

    tokens = P(("fsdp", "tensor"), None)
    return jax.shard_map(
        layer,
        mesh=mesh,
        in_specs=(
            tokens,
            P("fsdp"),
            P(),
            P("fsdp", "tensor"),
            P("fsdp", "tensor"),
            P("fsdp", "tensor"),
            P("fsdp", "tensor"),
            P(),
            P(),
            P("tensor", "fsdp"),
            P(),
            P("fsdp", "tensor"),
            P("fsdp", "tensor"),
            P("tensor", "fsdp"),
            tokens,
        ),
        out_specs=(
            tokens,
            tokens,
            P(),
            P("fsdp", "tensor"),
            P("fsdp", "tensor"),
            P("fsdp", "tensor"),
            P("fsdp", "tensor"),
            P(),
            P(),
            P("tensor", "fsdp"),
            P(),
            P("fsdp", "tensor"),
            P("fsdp", "tensor"),
            P("tensor", "fsdp"),
        ),
        check_vma=False,
    )
```

time: 1800 us -> 1160 us (0.64)
  waiting for transfers between devices: 1360 us -> 570 us
  starting transfers between devices: 1.39 us -> 151 us
  local copies, waits for them, and re-layouts: 71.1 us -> 144 us
  blocking collectives: 39.8 us -> 0 us
    reduce_scatter x12 -> x0, waiting for transfers between devices: 820 us -> none  [the longest x4 270 us: rows_out(): return lax.psum_scatter(values, 'tensor', scatter_dimension=0, tiled=True)]
    ppermute x0 -> x95, waiting for transfers between devices: none -> 570 us  [exchange(): return lax.ppermute(values, axis, [(i, i ^ mask) for i in range(size)])]
    all_gather x12 -> x0, waiting for transfers between devices: 535 us -> none  [the longest x1 102 us: body(): lax.all_gather(down_weight, 'fsdp', axis=1, tiled=True)]
    ppermute x0 -> x95, starting transfers between devices: none -> 151 us  [exchange(): return lax.ppermute(values, axis, [(i, i ^ mask) for i in range(size)])]
    unnamed x134 -> x314, local copies, waits for them, and re-layouts: 16.1 us -> 71.4 us
    psum x1 -> x0, blocking collectives: 39.8 us -> none  [body(): lax.psum((attn_gain_part, query_gain_part, key_gain_part, mlp_gain_part),...]
    dot_general x8 -> x12, matrix products: 54.2 us -> 48.8 us  [matmul_tn(): lax.dot_general(first_op, second_op, (((0,), (0,)), ((), ())), preferred_...]
    dot_general x20 -> x18, matrix products: 93.9 us -> 90.1 us  [the longest x6 59.4 us: matmul(): return jnp.dot(first_op, second_op, preferred_element_type=F32)]
  transfers between devices with their start and end apart: 24 -> 95, of which waited for: 22 -> 35; matrix products, arithmetic and copies ran while one was open for 16% -> 26% of each run, Pallas kernels for 0% -> 0%
where the time goes in v1:
time: 1160 us
  waiting for transfers between devices  570 us (49%)
  matrix products  207 us (18%)
  starting transfers between devices  151 us (13%)
  local copies, waits for them, and re-layouts  144 us (12%)
  other arithmetic  83.5 us (7%)
    ppermute x95, waiting for transfers between devices, exchange(): return lax.ppermute(values, axis, [(i, i ^ mask) for i in range(size)])  570 us
    ppermute x95, starting transfers between devices, exchange(): return lax.ppermute(values, axis, [(i, i ^ mask) for i in range(size)])  151 us
    unnamed x314, local copies, waits for them, and re-layouts  71.4 us
    dot_general x6, matrix products, matmul_nt(): lax.dot_general(first_op, second_op, (((1,), (1,)), ((), ())), preferred_...  61.3 us
    dot_general x6, matrix products, matmul(): return jnp.dot(first_op, second_op, preferred_element_type=F32)  59.4 us
    dot_general x12, matrix products, matmul_tn(): lax.dot_general(first_op, second_op, (((0,), (0,)), ((), ())), preferred_...  48.8 us
  transfers between devices with their start and end apart: 95, of which 35 were waited for; matrix products, arithmetic and copies ran while one was open for 26% of the time, Pallas kernels for 0%

profile of v1, /device:TPU:0, one launch (start us, length us, event | category | flops | bytes accessed | tf_op | source)
XLA Modules:
  0.0 1159.0 jit_solution(1445112941656033465)
XLA Ops:
  100.2 14.9 %collective-permute-start.37 = (bf16[256,1536]{1,0:T(8,128)(2,1)S(1)}, bf16[256,1536]{1,0:T(8,128)(2,1)S(1)}, u32[]{:S(2)}, u32[]{:S(2)}) collective-permute-start(bf16[256,1536]{1,0:T(8,128)(2,1)S(1)} %copy-done.57), channel_id=1, source_target_pairs={{0,8},{4,12},{8,0},{12,4},{16,24},{20,28},{24,16},{28,20},{1,9},{5... | collective-permute-start | bytes 2359304 | tf_op jit(solution)/shard_map/ppermute | solution.py:15
  146.9 24.0 %collective-permute-done.38 = bf16[256,1536]{1,0:T(8,128)(2,1)S(1)} collective-permute-done((bf16[256,1536]{1,0:T(8,128)(2,1)S(1)}, bf16[256,1536]{1,0:T(8,128)(2,1)S(1)}, u32[]{:S(2)}, u32[]{:S(2)}) %collective-permute-start.38) | collective-permute-done | bytes 786464 | tf_op jit(solution)/shard_map/ppermute | solution.py:15
  184.5 27.4 %collective-permute-done.45 = bf16[1536,256]{1,0:T(8,128)(2,1)S(1)} collective-permute-done((bf16[1536,256]{1,0:T(8,128)(2,1)}, bf16[1536,256]{1,0:T(8,128)(2,1)S(1)}, u32[]{:S(2)}, u32[]{:S(2)}) %collective-permute-start.45) | collective-permute-done | bytes 786464 | tf_op jit(solution)/shard_map/ppermute | solution.py:15
  280.4 20.9 %while.27 = (s32[]{:T(128)}, f32[2,512,2,2,128]{4,3,2,1,0:T(2,128)}, f32[2,2,2,512,1]{3,2,1,4,0:T(2,128)S(1)}, s32[1024]{0:T(1024)S(1)}, s32[2,512]{1,0:T(2,128)...) while((s32[]{:T(128)}, ...), condition=%wide.region_6.7_spmd, body=%wide.region_3.6_spmd.sunk | while | flops 1099955200 | bytes 32064116 | solution.py:189
  341.1 16.8 %collective-permute-done.41 = bf16[256,1536]{1,0:T(8,128)(2,1)S(1)} collective-permute-done((bf16[256,1536]{1,0:T(8,128)(2,1)S(1)}, bf16[256,1536]{1,0:T(8,128)(2,1)S(1)}, u32[]{:S(2)}, u32[]{:S(2)}) %collective-permute-start.41) | collective-permute-done | bytes 786464 | tf_op jit(solution)/shard_map/ppermute | solution.py:15
  377.3 14.4 %collective-permute-done.43 = bf16[256,1536]{1,0:T(8,128)(2,1)S(1)} collective-permute-done((bf16[256,1536]{1,0:T(8,128)(2,1)S(1)}, bf16[256,1536]{1,0:T(8,128)(2,1)S(1)}, u32[]{:S(2)}, u32[]{:S(2)}) %collective-permute-start.43) | collective-permute-done | bytes 786464 | tf_op jit(solution)/shard_map/ppermute | solution.py:15
  394.2 14.4 %collective-permute-done.48 = bf16[1536,256]{1,0:T(8,128)(2,1)S(1)} collective-permute-done((bf16[1536,256]{1,0:T(8,128)(2,1)S(1)}, bf16[1536,256]{1,0:T(8,128)(2,1)S(1)}, u32[]{:S(2)}, u32[]{:S(2)}) %collective-permute-start.48) | collective-permute-done | bytes 786464 | tf_op jit(solution)/shard_map/ppermute | solution.py:15
  426.9 15.3 %collective-permute-done.50 = bf16[1536,256]{1,0:T(8,128)(2,1)S(1)} collective-permute-done((bf16[1536,256]{1,0:T(8,128)(2,1)}, bf16[1536,256]{1,0:T(8,128)(2,1)S(1)}, u32[]{:S(2)}, u32[]{:S(2)}) %collective-permute-start.50) | collective-permute-done | bytes 786464 | tf_op jit(solution)/shard_map/ppermute | solution.py:15
  442.2 16.8 %collective-permute-done.34 = bf16[256,1536]{1,0:T(8,128)(2,1)S(1)} collective-permute-done((bf16[256,1536]{1,0:T(8,128)(2,1)}, bf16[256,1536]{1,0:T(8,128)(2,1)S(1)}, u32[]{:S(2)}, u32[]{:S(2)}) %collective-permute-start.34) | collective-permute-done | bytes 786464 | tf_op jit(solution)/shard_map/ppermute | solution.py:15
  476.9 15.3 %collective-permute-done.36 = bf16[256,1536]{1,0:T(8,128)(2,1)S(1)} collective-permute-done((bf16[256,1536]{1,0:T(8,128)(2,1)}, bf16[256,1536]{1,0:T(8,128)(2,1)S(1)}, u32[]{:S(2)}, u32[]{:S(2)}) %collective-permute-start.36) | collective-permute-done | bytes 786464 | tf_op jit(solution)/shard_map/ppermute | solution.py:15
  493.7 14.9 %fusion.108 = f32[1024,1536]{1,0:T(8,128)} fusion(bf16[1536,2048]{1,0:T(8,128)(2,1)} %constant_dynamic-update-slice_fusion.55, bf16[256,2048]{1,0:T(8,128)(2,1)S(1)} %collective-permute-done.56, bf16[256,2048]{1,0:T(8,128)(2,1)S(1)} %collective-permute-done.55, bf16[256,2048]{1,0:T(8,128)(2,1)S(1)} %collective-permute-done.54, ...), kind=kOutput, calls=%fused_computation.332 | convolution fusion | flops 6459228160 | bytes 16777216 | tf_op jit(solution)/shard_map/dot_general | solution.py:117
  528.3 17.6 %multiply_convert_fusion.1 = (bf16[1024,1536]{1,0:T(8,128)(2,1)}, bf16[1024,1536]{1,0:T(8,128)(2,1)}, bf16[1024,1536]{1,0:T(8,128)(2,1)}) fusion(f32[1024,1536]{1,0:T(8,128)} %fusion.108, f32[1024,1536]{1,0:T(8,128)} %fusion.109, bf16[2048,1536]{1,0:T(8,128)(2,1)} %constant_dynamic-update-slice_fusion.39, bf16[256,2048]{1,0:T(8,128)(2,1)} %collective-permute-done.29, ...), kind=kOutput, calls=%fused_computation.57 | convolution fusion | flops 6482821120 | bytes 32505856 | tf_op jit(solution)/shard_map/dot_general | solution.py:107
  609.9 15.7 %collective-permute-done.59 = bf16[256,2048]{1,0:T(8,128)(2,1)S(1)} collective-permute-done((bf16[256,2048]{1,0:T(8,128)(2,1)S(1)}, bf16[256,2048]{1,0:T(8,128)(2,1)S(1)}, u32[]{:S(2)}, u32[]{:S(2)}) %collective-permute-start.59) | collective-permute-done | bytes 1048608 | tf_op jit(solution)/shard_map/ppermute | solution.py:15
  627.8 19.7 %collective-permute-done.53 = bf16[256,2048]{1,0:T(8,128)(2,1)S(1)} collective-permute-done((bf16[256,2048]{1,0:T(8,128)(2,1)S(1)}, bf16[256,2048]{1,0:T(8,128)(2,1)S(1)}, u32[]{:S(2)}, u32[]{:S(2)}) %collective-permute-start.53) | collective-permute-done | bytes 1048608 | tf_op jit(solution)/shard_map/ppermute | solution.py:15
  663.0 39.1 %collective-permute-done.87 = bf16[1024,1536]{1,0:T(8,128)(2,1)} collective-permute-done((bf16[1024,1536]{1,0:T(8,128)(2,1)}, bf16[1024,1536]{1,0:T(8,128)(2,1)}, u32[]{:S(2)}, u32[]{:S(2)}) %collective-permute-start.87) | collective-permute-done | bytes 3145760 | tf_op jit(solution)/shard_map/ppermute | solution.py:15
  709.3 59.6 %collective-permute-done.83 = bf16[1024,1536]{1,0:T(8,128)(2,1)} collective-permute-done((bf16[1024,1536]{1,0:T(8,128)(2,1)}, bf16[1024,1536]{1,0:T(8,128)(2,1)}, u32[]{:S(2)}, u32[]{:S(2)}) %collective-permute-start.83) | collective-permute-done | bytes 3145760 | tf_op jit(solution)/shard_map/ppermute | solution.py:15
  782.5 15.7 %collective-permute-done.88 = bf16[256,1536]{1,0:T(8,128)(2,1)S(1)} collective-permute-done((bf16[256,1536]{1,0:T(8,128)(2,1)S(1)}, bf16[256,1536]{1,0:T(8,128)(2,1)S(1)}, u32[]{:S(2)}, u32[]{:S(2)}) %collective-permute-start.88) | collective-permute-done | bytes 786464 | tf_op jit(solution)/shard_map/ppermute | solution.py:15
  803.8 28.2 %collective-permute-done.89 = bf16[256,1536]{1,0:T(8,128)(2,1)S(1)} collective-permute-done((bf16[256,1536]{1,0:T(8,128)(2,1)S(1)}, bf16[256,1536]{1,0:T(8,128)(2,1)S(1)}, u32[]{:S(2)}, u32[]{:S(2)}) %collective-permute-start.89) | collective-permute-done | bytes 786464 | tf_op jit(solution)/shard_map/ppermute | solution.py:15
  838.7 60.7 %collective-permute-done.85 = bf16[256,1536]{1,0:T(8,128)(2,1)S(1)} collective-permute-done((bf16[256,1536]{1,0:T(8,128)(2,1)S(1)}, bf16[256,1536]{1,0:T(8,128)(2,1)S(1)}, u32[]{:S(2)}, u32[]{:S(2)}) %collective-permute-start.85) | collective-permute-done | bytes 786464 | tf_op jit(solution)/shard_map/ppermute | solution.py:15
  913.6 45.6 %while.28 = (s32[]{:T(128)}, f32[1024,2,128]{0,2,1:T(8,128)S(1)}, f32[1024,2,128]{0,2,1:T(8,128)S(1)}, f32[2,512,2,2,128]{4,1,3,2,0:T(8,128)}, bf16[2,512,2,2,12...) while((s32[]{:T(128)}, f32[1024,2,128]{0,2,1:T(8,128)S(1)}, ...), condition=%wide.region_11.12_spmd.clone, body=%wide.region_9.11_spmd.clone.sunk | while | flops 2709519360 | bytes 162587936 | solution.py:223
  1025.2 15.7 %collective-permute-start.80 = (bf16[512,256]{1,0:T(8,128)(2,1)S(1)}, bf16[512,256]{1,0:T(8,128)(2,1)S(1)}, u32[]{:S(2)}, u32[]{:S(2)}) collective-permute-start(bf16[512,256]{1,0:T(8,128)(2,1)S(1)} %get-tuple-element.301), channel_id=1, source_target_pairs={{0,8},{4,12},{8,0},{12,4},{16,24},{20,28},{24,16},{28,20},{1,9},{5... | collective-permute-start | bytes 786440 | tf_op jit(solution)/shard_map/ppermute | solution.py:15
  1065.2 19.2 %collective-permute-done.77 = bf16[256,512]{1,0:T(8,128)(2,1)S(1)} collective-permute-done((bf16[256,512]{1,0:T(8,128)(2,1)S(1)}, bf16[256,512]{1,0:T(8,128)(2,1)S(1)}, u32[]{:S(2)}, u32[]{:S(2)}) %collective-permute-start.77) | collective-permute-done | bytes 262176 | tf_op jit(solution)/shard_map/ppermute | solution.py:15
  1093.6 14.1 %collective-permute-done.71 = bf16[1024,1024]{1,0:T(8,128)(2,1)S(1)} collective-permute-done((bf16[1024,1024]{1,0:T(8,128)(2,1)S(1)}, bf16[1024,1024]{1,0:T(8,128)(2,1)S(1)}, u32[]{:S(2)}, u32[]{:S(2)}) %collective-permute-start.71) | collective-permute-done | bytes 2097184 | tf_op jit(solution)/shard_map/ppermute | solution.py:15
  1121.8 33.7 %collective-permute-done.70 = f32[4352]{0:T(1024)S(1)} collective-permute-done((f32[4352]{0:T(1024)S(1)}, f32[4352]{0:T(1024)S(1)}, u32[]{:S(2)}, u32[]{:S(2)}) %collective-permute-start.70) | collective-permute-done | bytes 17440 | tf_op jit(solution)/shard_map/ppermute | solution.py:15
  (686 shorter events, 641.7 us)
Async XLA Ops:
  5.7 77.3 %collective-permute-start.3 = (bf16[256,1024]{1,0:T(8,128)(2,1)}, bf16[256,1024]{1,0:T(8,128)(2,1)}, u32[]{:S(2)}, u32[]{:S(2)}) collective-permute-start(bf16[256,1024]{1,0:T(8,128)(2,1)} %get-tuple-element.315), channel_id=1, source_target_pairs={{0,8},{4,12},{8,0},{12,4},{16,24},{20,28},{24,16},{28,20},{1,9},{5... | collective-permute-start | bytes 1572872 | tf_op jit(solution)/shard_map/ppermute | solution.py:15
  8.8 77.7 %collective-permute-start.4 = (bf16[256,1024]{1,0:T(8,128)(2,1)}, bf16[256,1024]{1,0:T(8,128)(2,1)}, u32[]{:S(2)}, u32[]{:S(2)}) collective-permute-start(bf16[256,1024]{1,0:T(8,128)(2,1)} %get-tuple-element.315), channel_id=1, source_target_pairs={{0,16},{4,20},{8,24},{12,28},{16,0},{20,4},{24,8},{28,12},{1,17},{... | collective-permute-start | bytes 1572872 | tf_op jit(solution)/shard_map/ppermute | solution.py:15
  172.9 68.3 %collective-permute-start.1 = (bf16[256,2048]{1,0:T(8,128)(2,1)S(1)}, bf16[256,2048]{1,0:T(8,128)(2,1)S(1)}, u32[]{:S(2)}, u32[]{:S(2)}) collective-permute-start(bf16[256,2048]{1,0:T(8,128)(2,1)S(1)} %copy-done.31), channel_id=1, source_target_pairs={{0,1},{1,0},{2,3},{3,2},{4,5},{5,4},{6,7},{7,6},{8,9},{9,8},{10,11... | collective-permute-start | bytes 3145736 | tf_op jit(solution)/shard_map/ppermute | solution.py:15
  215.5 102.7 %collective-permute-start.46 = (bf16[1536,256]{1,0:T(8,128)(2,1)}, bf16[1536,256]{1,0:T(8,128)(2,1)}, u32[]{:S(2)}, u32[]{:S(2)}) collective-permute-start(bf16[1536,256]{1,0:T(8,128)(2,1)} %param.32), channel_id=1, source_target_pairs={{0,24},{4,28},{8,16},{12,20},{16,8},{20,12},{24,0},{28,4},{1,25},{... | collective-permute-start | bytes 2359304 | tf_op jit(solution)/shard_map/ppermute | solution.py:15
  217.5 103.1 %collective-permute-start.47 = (bf16[1536,256]{1,0:T(8,128)(2,1)}, bf16[1536,256]{1,0:T(8,128)(2,1)}, u32[]{:S(2)}, u32[]{:S(2)}) collective-permute-start(bf16[1536,256]{1,0:T(8,128)(2,1)} %param.32), channel_id=1, source_target_pairs={{0,4},{4,0},{8,12},{12,8},{16,20},{20,16},{24,28},{28,24},{1,5},{5... | collective-permute-start | bytes 2359304 | tf_op jit(solution)/shard_map/ppermute | solution.py:15
  226.8 97.4 %collective-permute-start.30 = (bf16[256,1536]{1,0:T(8,128)(2,1)}, bf16[256,1536]{1,0:T(8,128)(2,1)}, u32[]{:S(2)}, u32[]{:S(2)}) collective-permute-start(bf16[256,1536]{1,0:T(8,128)(2,1)} %param.30), channel_id=1, source_target_pairs={{0,8},{4,12},{8,0},{12,4},{16,24},{20,28},{24,16},{28,20},{1,9},{5... | collective-permute-start | bytes 2359304 | tf_op jit(solution)/shard_map/ppermute | solution.py:15
  241.3 85.5 %collective-permute-start.31 = (bf16[256,1536]{1,0:T(8,128)(2,1)}, bf16[256,1536]{1,0:T(8,128)(2,1)}, u32[]{:S(2)}, u32[]{:S(2)}) collective-permute-start(bf16[256,1536]{1,0:T(8,128)(2,1)} %param.30), channel_id=1, source_target_pairs={{0,16},{4,20},{8,24},{12,28},{16,0},{20,4},{24,8},{28,12},{1,17},{... | collective-permute-start | bytes 2359304 | tf_op jit(solution)/shard_map/ppermute | solution.py:15
  241.3 89.1 %collective-permute-start.32 = (bf16[256,1536]{1,0:T(8,128)(2,1)}, bf16[256,1536]{1,0:T(8,128)(2,1)}, u32[]{:S(2)}, u32[]{:S(2)}) collective-permute-start(bf16[256,1536]{1,0:T(8,128)(2,1)} %param.30), channel_id=1, source_target_pairs={{0,24},{4,28},{8,16},{12,20},{16,8},{20,12},{24,0},{28,4},{1,25},{... | collective-permute-start | bytes 2359304 | tf_op jit(solution)/shard_map/ppermute | solution.py:15
  333.1 75.5 %collective-permute-start.48 = (bf16[1536,256]{1,0:T(8,128)(2,1)S(1)}, bf16[1536,256]{1,0:T(8,128)(2,1)S(1)}, u32[]{:S(2)}, u32[]{:S(2)}) collective-permute-start(bf16[1536,256]{1,0:T(8,128)(2,1)S(1)} %copy-done.67), channel_id=1, source_target_pairs={{0,4},{4,0},{8,12},{12,8},{16,20},{20,16},{24,28},{28,24},{1,5},{5... | collective-permute-start | bytes 2359304 | tf_op jit(solution)/shard_map/ppermute | solution.py:15
  341.1 69.9 %collective-permute-start.24 = (bf16[256,2048]{1,0:T(8,128)(2,1)S(1)}, bf16[256,2048]{1,0:T(8,128)(2,1)S(1)}, u32[]{:S(2)}, u32[]{:S(2)}) collective-permute-start(bf16[256,2048]{1,0:T(8,128)(2,1)S(1)} %get-tuple-element.282), channel_id=1, source_target_pairs={{0,1},{1,0},{2,3},{3,2},{4,5},{5,4},{6,7},{7,6},{8,9},{9,8},{10,11... | collective-permute-start | bytes 3145736 | tf_op jit(solution)/shard_map/ppermute | solution.py:15
  414.1 79.6 %collective-permute-start.55 = (bf16[256,2048]{1,0:T(8,128)(2,1)S(1)}, bf16[256,2048]{1,0:T(8,128)(2,1)S(1)}, u32[]{:S(2)}, u32[]{:S(2)}) collective-permute-start(bf16[256,2048]{1,0:T(8,128)(2,1)S(1)} %copy-done.33), channel_id=1, source_target_pairs={{0,1},{1,0},{2,3},{3,2},{4,5},{5,4},{6,7},{7,6},{8,9},{9,8},{10,11... | collective-permute-start | bytes 3145736 | tf_op jit(solution)/shard_map/ppermute | solution.py:15
  425.4 66.8 %collective-permute-start.36 = (bf16[256,1536]{1,0:T(8,128)(2,1)}, bf16[256,1536]{1,0:T(8,128)(2,1)S(1)}, u32[]{:S(2)}, u32[]{:S(2)}) collective-permute-start(bf16[256,1536]{1,0:T(8,128)(2,1)} %collective-permute-done.32), channel_id=1, source_target_pairs={{0,4},{4,0},{8,12},{12,8},{16,20},{20,16},{24,28},{28,24},{1,5},{5... | collective-permute-start | bytes 2359304 | tf_op jit(solution)/shard_map/ppermute | solution.py:15
  563.4 90.0 %collective-permute-start.91 = (bf16[1536,1024]{1,0:T(8,128)(2,1)}, bf16[1536,1024]{1,0:T(8,128)(2,1)}, u32[]{:S(2)}, u32[]{:S(2)}) collective-permute-start(bf16[1536,1024]{1,0:T(8,128)(2,1)} %convolution_convert_fusion), channel_id=1, source_target_pairs={{0,4},{4,0},{8,12},{12,8},{16,20},{20,16},{24,28},{28,24},{1,5},{5... | collective-permute-start | bytes 9437192 | tf_op jit(solution)/shard_map/ppermute | solution.py:15
  609.2 92.9 %collective-permute-start.87 = (bf16[1024,1536]{1,0:T(8,128)(2,1)}, bf16[1024,1536]{1,0:T(8,128)(2,1)}, u32[]{:S(2)}, u32[]{:S(2)}) collective-permute-start(bf16[1024,1536]{1,0:T(8,128)(2,1)} %convolution_convert_fusion.1), channel_id=1, source_target_pairs={{0,4},{4,0},{8,12},{12,8},{16,20},{20,16},{24,28},{28,24},{1,5},{5... | collective-permute-start | bytes 9437192 | tf_op jit(solution)/shard_map/ppermute | solution.py:15
  625.6 143.3 %collective-permute-start.83 = (bf16[1024,1536]{1,0:T(8,128)(2,1)}, bf16[1024,1536]{1,0:T(8,128)(2,1)}, u32[]{:S(2)}, u32[]{:S(2)}) collective-permute-start(bf16[1024,1536]{1,0:T(8,128)(2,1)} %convolution_convert_fusion.2), channel_id=1, source_target_pairs={{0,4},{4,0},{8,12},{12,8},{16,20},{20,16},{24,28},{28,24},{1,5},{5... | collective-permute-start | bytes 9437192 | tf_op jit(solution)/shard_map/ppermute | solution.py:15
  651.7 125.2 %collective-permute-start.60 = (bf16[256,2048]{1,0:T(8,128)(2,1)S(1)}, bf16[256,2048]{1,0:T(8,128)(2,1)S(1)}, u32[]{:S(2)}, u32[]{:S(2)}) collective-permute-start(bf16[256,2048]{1,0:T(8,128)(2,1)S(1)} %get-tuple-element.263), channel_id=1, source_target_pairs={{0,2},{1,3},{2,0},{3,1},{4,6},{5,7},{6,4},{7,5},{8,10},{9,11},{10,... | collective-permute-start | bytes 3145736 | tf_op jit(solution)/shard_map/ppermute | solution.py:15
  660.8 117.0 %collective-permute-start.92 = (bf16[1536,256]{1,0:T(8,128)(2,1)S(1)}, bf16[1536,256]{1,0:T(8,128)(2,1)S(1)}, u32[]{:S(2)}, u32[]{:S(2)}) collective-permute-start(bf16[1536,256]{1,0:T(8,128)(2,1)S(1)} %get-tuple-element.284), channel_id=1, source_target_pairs={{0,8},{4,12},{8,0},{12,4},{16,24},{20,28},{24,16},{28,20},{1,9},{5... | collective-permute-start | bytes 2359304 | tf_op jit(solution)/shard_map/ppermute | solution.py:15
  662.0 118.3 %collective-permute-start.93 = (bf16[1536,256]{1,0:T(8,128)(2,1)S(1)}, bf16[1536,256]{1,0:T(8,128)(2,1)S(1)}, u32[]{:S(2)}, u32[]{:S(2)}) collective-permute-start(bf16[1536,256]{1,0:T(8,128)(2,1)S(1)} %get-tuple-element.286), channel_id=1, source_target_pairs={{0,16},{4,20},{8,24},{12,28},{16,0},{20,4},{24,8},{28,12},{1,17},{... | collective-permute-start | bytes 2359304 | tf_op jit(solution)/shard_map/ppermute | solution.py:15
  702.1 78.5 %collective-permute-start.94 = (bf16[1536,256]{1,0:T(8,128)(2,1)S(1)}, bf16[1536,256]{1,0:T(8,128)(2,1)S(1)}, u32[]{:S(2)}, u32[]{:S(2)}) collective-permute-start(bf16[1536,256]{1,0:T(8,128)(2,1)S(1)} %get-tuple-element.285), channel_id=1, source_target_pairs={{0,24},{4,28},{8,16},{12,20},{16,8},{20,12},{24,0},{28,4},{1,25},{... | collective-permute-start | bytes 2359304 | tf_op jit(solution)/shard_map/ppermute | solution.py:15
  780.6 118.8 %collective-permute-start.85 = (bf16[256,1536]{1,0:T(8,128)(2,1)S(1)}, bf16[256,1536]{1,0:T(8,128)(2,1)S(1)}, u32[]{:S(2)}, u32[]{:S(2)}) collective-permute-start(bf16[256,1536]{1,0:T(8,128)(2,1)S(1)} %get-tuple-element.292), channel_id=1, source_target_pairs={{0,16},{4,20},{8,24},{12,28},{16,0},{20,4},{24,8},{28,12},{1,17},{... | collective-permute-start | bytes 2359304 | tf_op jit(solution)/shard_map/ppermute | solution.py:15
  798.2 101.2 %collective-permute-start.86 = (bf16[256,1536]{1,0:T(8,128)(2,1)S(1)}, bf16[256,1536]{1,0:T(8,128)(2,1)S(1)}, u32[]{:S(2)}, u32[]{:S(2)}) collective-permute-start(bf16[256,1536]{1,0:T(8,128)(2,1)S(1)} %get-tuple-element.291), channel_id=1, source_target_pairs={{0,24},{4,28},{8,16},{12,20},{16,8},{20,12},{24,0},{28,4},{1,25},{... | collective-permute-start | bytes 2359304 | tf_op jit(solution)/shard_map/ppermute | solution.py:15
  832.0 70.3 %collective-permute-start.61 = (bf16[256,2048]{1,0:T(8,128)(2,1)S(1)}, bf16[256,2048]{1,0:T(8,128)(2,1)S(1)}, u32[]{:S(2)}, u32[]{:S(2)}) collective-permute-start(bf16[256,2048]{1,0:T(8,128)(2,1)S(1)} %get-tuple-element.263), channel_id=1, source_target_pairs={{0,1},{1,0},{2,3},{3,2},{4,5},{5,4},{6,7},{7,6},{8,9},{9,8},{10,11... | collective-permute-start | bytes 3145736 | tf_op jit(solution)/shard_map/ppermute | solution.py:15
  832.0 70.3 %collective-permute-start.62 = (bf16[256,2048]{1,0:T(8,128)(2,1)S(1)}, bf16[256,2048]{1,0:T(8,128)(2,1)S(1)}, u32[]{:S(2)}, u32[]{:S(2)}) collective-permute-start(bf16[256,2048]{1,0:T(8,128)(2,1)S(1)} %collective-permute-done.60), channel_id=1, source_target_pairs={{0,1},{1,0},{2,3},{3,2},{4,5},{5,4},{6,7},{7,6},{8,9},{9,8},{10,11... | collective-permute-start | bytes 3145736 | tf_op jit(solution)/shard_map/ppermute | solution.py:15
  1018.3 67.1 %collective-permute-start.63 = (bf16[256,2048]{1,0:T(8,128)(2,1)S(1)}, bf16[256,2048]{1,0:T(8,128)(2,1)S(1)}, u32[]{:S(2)}, u32[]{:S(2)}) collective-permute-start(bf16[256,2048]{1,0:T(8,128)(2,1)S(1)} %get-tuple-element.274), channel_id=1, source_target_pairs={{0,1},{1,0},{2,3},{3,2},{4,5},{5,4},{6,7},{7,6},{8,9},{9,8},{10,11... | collective-permute-start | bytes 3145736 | tf_op jit(solution)/shard_map/ppermute | solution.py:15
  (187 other events, 5293.1 us)

commit v2 on v1

v2 whole, which is shorter than its diff:
```python
import functools

import jax
import jax.numpy as jnp
from jax import lax
from jax.experimental import pallas as pl
from jax.experimental.pallas import tpu as pltpu
from jax.sharding import PartitionSpec as P

NORM_EPSILON = 1e-06
ROPE_THETA = 1000000.0
MASKED_LOGIT = -1e30
F32 = jnp.float32
BF16 = jnp.bfloat16


def exchange(values, axis, size, mask):
    return lax.ppermute(values, axis, [(i, i ^ mask) for i in range(size)])


def lines(count):
    return [list(range(0, count, 2)), list(range(1, count, 2))]


def gather_line(shard, count):
    return lax.all_gather(shard, "fsdp", axis=0, tiled=True, axis_index_groups=lines(count))


def gather_pair(near, count, *before):
    far = exchange(near, "fsdp", count, 1)
    if before:
        far = hold(far, *before)
    return jnp.concatenate([near, far], axis=0)


def scatter_line(total, count):
    return lax.psum_scatter(
        total, "fsdp", scatter_dimension=0, tiled=True, axis_index_groups=lines(count)
    )


def add_low(first, second):
    return (first.astype(F32) + second.astype(F32)).astype(BF16)


def hold(value, *others):
    return lax.optimization_barrier((value,) + others)[0]


def to_pairs(values, me, count):
    blocks = values.reshape(values.shape[:-1] + (count // 2, 2, values.shape[-1] // count))
    even = blocks[..., 0, :].reshape(values.shape[:-1] + (-1,))
    odd = blocks[..., 1, :].reshape(values.shape[:-1] + (-1,))
    first = me % 2 == 0
    return jnp.concatenate([jnp.where(first, even, odd), jnp.where(first, odd, even)], axis=-1)


def to_index_order(values, me, count):
    width = values.shape[-1]
    shape = values.shape[:-1] + (count // 2, 1, width // count)
    near = values[..., : width // 2].reshape(shape)
    far = values[..., width // 2 :].reshape(shape)
    first = me % 2 == 0
    even, odd = jnp.where(first, near, far), jnp.where(first, far, near)
    return jnp.concatenate([even, odd], axis=-2).reshape(values.shape)


def row_masks(count):
    half = count // 2
    return [((p % half) << 1) | (p // half) for p in range(count)]


def place_of(mask, count):
    return (mask & 1) * (count // 2) + (mask >> 1)


def rows_in(values, count, *before):
    half = count // 2
    moved = [exchange(values, "tensor", count, step << 1) for step in range(1, half)]
    if before:
        moved = [hold(piece, *before) for piece in moved]
    near = [values] + moved
    far = [exchange(piece, "tensor", count, 1) for piece in near]
    return jnp.concatenate(near + far, axis=0)


def rows_out(near, far, count, *before):
    half = count // 2
    rows = near.shape[0] // half
    arrived = exchange(far.astype(BF16), "tensor", count, 1)

    def block(step):
        piece = slice(step * rows, (step + 1) * rows)
        return near[piece].astype(F32) + arrived[piece].astype(F32)

    moved = [
        exchange(block(step).astype(BF16), "tensor", count, step << 1) for step in range(1, half)
    ]
    result = block(0)
    for piece in moved:
        result = result + (hold(piece, *before) if before else piece).astype(F32)
    return result


def sum_everywhere(values, axes):
    for axis, count in axes:
        mask = 1
        while mask < count:
            values = values + exchange(values, axis, count, mask)
            mask <<= 1
    return values


def matmul(first_op, second_op):
    return jnp.dot(first_op, second_op, preferred_element_type=F32)


def matmul_tn(first_op, second_op):
    return lax.dot_general(
        first_op, second_op, (((0,), (0,)), ((), ())), preferred_element_type=F32
    )


def matmul_nt(first_op, second_op):
    return lax.dot_general(
        first_op, second_op, (((1,), (1,)), ((), ())), preferred_element_type=F32
    )


def normalize(values):
    inv_root = lax.rsqrt(jnp.mean(values * values, axis=-1, keepdims=True) + NORM_EPSILON)
    return (values * inv_root, inv_root)


def norm_back(gradient, unit_rows, inv_root, gain_vec):
    scaled = gradient * gain_vec
    return inv_root * (scaled - unit_rows * jnp.mean(scaled * unit_rows, axis=-1, keepdims=True))


def rope_tables(slot_count, head_size):
    half_width = head_size // 2
    inverse = ROPE_THETA ** (-(jnp.arange(half_width, dtype=F32) * 2.0 / head_size))
    angles = jnp.arange(slot_count, dtype=F32)[:, None] * inverse[None, :]
    cosine = jnp.concatenate([jnp.cos(angles), jnp.cos(angles)], axis=-1)
    signed_sine = jnp.concatenate([-jnp.sin(angles), jnp.sin(angles)], axis=-1)
    return (cosine, signed_sine)


def allowed_block(block, rows, width, length):
    row_slot = block * rows + lax.broadcasted_iota(jnp.int32, (rows, width), 0)
    col_slot = lax.broadcasted_iota(jnp.int32, (rows, width), 1)
    return (col_slot <= row_slot) & (col_slot < length)


def turn(unit_rows, gain_vec, cosine, signed_sine):
    normed = unit_rows * gain_vec
    half = normed.shape[-1] // 2
    return normed * cosine + pltpu.roll(normed, half, 1) * signed_sine


def turn_back(gradient, cosine, signed_sine):
    half = gradient.shape[-1] // 2
    return gradient * cosine - pltpu.roll(gradient, half, 1) * signed_sine


def attend_forward_kernel(
    masks,
    head_size,
    score_scale,
    share_ref,
    length_ref,
    query_ref,
    key_ref,
    value_ref,
    query_gain_ref,
    key_gain_ref,
    cosine_ref,
    sine_ref,
    attended_ref,
    log_ref,
    query_rot_ref,
    key_rot_ref,
    value_low_ref,
):
    blocks = len(masks)
    rows = query_ref.shape[0] // blocks
    group = query_ref.shape[1] // head_size
    share, length = share_ref[0], length_ref[0]
    for place, mask in enumerate(masks):
        here = pl.ds(place * rows, rows)
        there = pl.ds(pl.multiple_of((share ^ mask) * rows, rows), rows)
        cosine, signed_sine = cosine_ref[there, :], sine_ref[there, :]
        for head in range(group):
            cols = pl.ds(head * head_size, head_size)
            unit_rows, _ = normalize(query_ref[here, cols])
            turned = turn(unit_rows, query_gain_ref[...], cosine, signed_sine)
            query_rot_ref[there, cols] = turned.astype(BF16)
        unit_rows, _ = normalize(key_ref[here, :])
        turned = turn(unit_rows, key_gain_ref[...], cosine, signed_sine)
        key_rot_ref[there, :] = turned.astype(BF16)
        value_low_ref[there, :] = value_ref[here, :].astype(BF16)

    for block in range(blocks):
        width = (block + 1) * rows
        here = pl.ds(block * rows, rows)
        allowed = allowed_block(block, rows, width, length)
        back = pl.ds(pl.multiple_of(place_of(share ^ block, blocks) * rows, rows), rows)

        def one_head(head, carry, width=width, here=here, allowed=allowed, back=back):
            cols = pl.ds(pl.multiple_of(head * head_size, head_size), head_size)
            scores = matmul_nt(query_rot_ref[here, cols], key_rot_ref[:width, :])
            logits = jnp.where(allowed, scores * score_scale, MASKED_LOGIT)
            highest = jnp.max(logits, axis=-1, keepdims=True)
            weights_raw = jnp.exp(logits - highest)
            row_total = jnp.sum(weights_raw, axis=-1, keepdims=True)
            probabilities = (weights_raw * (1.0 / row_total)).astype(BF16)
            attended_ref[back, cols] = matmul(probabilities, value_low_ref[:width, :])
            log_ref[here, cols] = jnp.broadcast_to(highest + jnp.log(row_total), (rows, head_size))
            return carry

        lax.fori_loop(0, group, one_head, 0)


def attend_backward_kernel(
    masks,
    head_size,
    score_scale,
    share_ref,
    length_ref,
    grad_ref,
    query_ref,
    key_ref,
    query_rot_ref,
    key_rot_ref,
    value_low_ref,
    log_ref,
    query_gain_ref,
    key_gain_ref,
    cosine_ref,
    sine_ref,
    send_ref,
    gain_ref,
    query_grad_ref,
    key_grad_ref,
    value_grad_ref,
):
    blocks = len(masks)
    rows = query_ref.shape[0] // blocks
    group = query_ref.shape[1] // head_size
    kv_heads = pl.num_programs(0)
    kv_head = pl.program_id(0)
    share, length = share_ref[0], length_ref[0]
    key_grad_ref[...] = jnp.zeros_like(key_grad_ref)
    value_grad_ref[...] = jnp.zeros_like(value_grad_ref)

    @pl.when(kv_head == 0)
    def _():
        gain_ref[...] = jnp.zeros_like(gain_ref)

    for block in range(blocks):
        width = (block + 1) * rows
        here = pl.ds(block * rows, rows)
        allowed = allowed_block(block, rows, width, length)
        back = pl.ds(pl.multiple_of(place_of(share ^ block, blocks) * rows, rows), rows)

        def one_head(head, carry, width=width, here=here, allowed=allowed, back=back):
            cols = pl.ds(pl.multiple_of(head * head_size, head_size), head_size)
            queries, grads = query_rot_ref[here, cols], grad_ref[back, cols]
            scores = matmul_nt(queries, key_rot_ref[:width, :])
            logits = jnp.where(allowed, scores * score_scale, MASKED_LOGIT)
            soft = jnp.where(allowed, jnp.exp(logits - log_ref[here, cols][:, :1]), 0.0)
            prob_grad = matmul_nt(grads, value_low_ref[:width, :])
            centre = jnp.sum(soft * prob_grad, axis=-1, keepdims=True)
            score_grad = (score_scale * soft * (prob_grad - centre)).astype(BF16)
            query_grad_ref[here, cols] = matmul(score_grad, key_rot_ref[:width, :])
            key_grad_ref[:width, :] += matmul_tn(score_grad, queries)
            value_grad_ref[:width, :] += matmul_tn(soft.astype(BF16), grads)
            return carry

        lax.fori_loop(0, group, one_head, 0)

    key_base, value_base = kv_heads * group * head_size, kv_heads * (group + 1) * head_size
    for place, mask in enumerate(masks):
        here = pl.ds(place * rows, rows)
        there = pl.ds(pl.multiple_of((share ^ mask) * rows, rows), rows)
        cosine, signed_sine = cosine_ref[there, :], sine_ref[there, :]

        def through_norm(gradient, raw, gain_vec):
            normed_grad = turn_back(gradient, cosine, signed_sine)
            unit_rows, inv_root = normalize(raw)
            gain_part = jnp.sum(normed_grad * unit_rows, axis=0, keepdims=True)
            return norm_back(normed_grad, unit_rows, inv_root, gain_vec).astype(BF16), gain_part

        for head in range(group):
            cols = pl.ds(head * head_size, head_size)
            sent, gain_part = through_norm(
                query_grad_ref[there, cols], query_ref[here, cols], query_gain_ref[...]
            )
            offset = pl.multiple_of((kv_head * group + head) * head_size, head_size)
            send_ref[here, pl.ds(offset, head_size)] = sent
            gain_ref[0:1, :] += gain_part
        sent, gain_part = through_norm(key_grad_ref[there, :], key_ref[here, :], key_gain_ref[...])
        offset = pl.multiple_of(key_base + kv_head * head_size, head_size)
        send_ref[here, pl.ds(offset, head_size)] = sent
        gain_ref[1:2, :] += gain_part
        offset = pl.multiple_of(value_base + kv_head * head_size, head_size)
        send_ref[here, pl.ds(offset, head_size)] = value_grad_ref[there, :].astype(BF16)


def head_specs(seq_len, group, kv_heads, head_size):
    query_spec = pl.BlockSpec((seq_len, group * head_size), lambda c: (0, c))
    key_spec = pl.BlockSpec((seq_len, head_size), lambda c: (0, kv_heads * group + c))
    value_spec = pl.BlockSpec((seq_len, head_size), lambda c: (0, kv_heads * (group + 1) + c))
    one_spec = pl.BlockSpec((seq_len, head_size), lambda c: (0, c))
    gain_spec = pl.BlockSpec((1, head_size), lambda c: (0, 0))
    table_spec = pl.BlockSpec((seq_len, head_size), lambda c: (0, 0))
    scalar_spec = pl.BlockSpec(memory_space=pltpu.SMEM)
    return query_spec, key_spec, value_spec, one_spec, gain_spec, table_spec, scalar_spec


def attend_forward(qkv_raw, share, length, gains, tables, masks, sizes):
    kv_heads, group, head_size = sizes
    seq_len = qkv_raw.shape[0]
    query, key, value, one, gain, table, scalar = head_specs(seq_len, group, kv_heads, head_size)
    wide, narrow = kv_heads * group * head_size, kv_heads * head_size
    return pl.pallas_call(
        functools.partial(attend_forward_kernel, masks, head_size, head_size ** (-0.5)),
        grid=(kv_heads,),
        in_specs=[scalar, scalar, query, key, value, gain, gain, table, table],
        out_specs=[query, query, query, one, one],
        out_shape=[
            jax.ShapeDtypeStruct((seq_len, wide), F32),
            jax.ShapeDtypeStruct((seq_len, wide), F32),
            jax.ShapeDtypeStruct((seq_len, wide), BF16),
            jax.ShapeDtypeStruct((seq_len, narrow), BF16),
            jax.ShapeDtypeStruct((seq_len, narrow), BF16),
        ],
        cost_estimate=pl.CostEstimate(
            flops=seq_len,
            bytes_accessed=seq_len,
            transcendentals=0,
        ),
        name="attend_forward",
    )(share, length, qkv_raw, qkv_raw, qkv_raw, *gains, *tables)


def attend_backward(grads, qkv_raw, kept, share, length, gains, tables, masks, sizes):
    kv_heads, group, head_size = sizes
    seq_len = qkv_raw.shape[0]
    query, key, value, one, gain, table, scalar = head_specs(seq_len, group, kv_heads, head_size)
    wide = kv_heads * group * head_size
    log_total, query_rot, key_rot, value_low = kept
    return pl.pallas_call(
        functools.partial(attend_backward_kernel, masks, head_size, head_size ** (-0.5)),
        grid=(kv_heads,),
        in_specs=[scalar, scalar, query, query, key, query, one, one, query]
        + [gain, gain, table, table],
        out_specs=[
            pl.BlockSpec(qkv_raw.shape, lambda c: (0, 0)),
            pl.BlockSpec((8, head_size), lambda c: (0, 0)),
        ],
        out_shape=[
            jax.ShapeDtypeStruct(qkv_raw.shape, BF16),
            jax.ShapeDtypeStruct((8, head_size), F32),
        ],
        scratch_shapes=[
            pltpu.VMEM((seq_len, group * head_size), F32),
            pltpu.VMEM((seq_len, head_size), F32),
            pltpu.VMEM((seq_len, head_size), F32),
        ],
        cost_estimate=pl.CostEstimate(
            flops=seq_len,
            bytes_accessed=seq_len,
            transcendentals=0,
        ),
        name="attend_backward",
    )(
        share,
        length,
        grads,
        qkv_raw,
        qkv_raw,
        query_rot,
        key_rot,
        value_low,
        log_total,
        *gains,
        *tables,
    )


def body(
    members,
    shares,
    hidden_in,
    lengths,
    attn_gain,
    query_weight,
    key_weight,
    value_weight,
    output_gate,
    query_gain,
    key_gain,
    out_weight,
    mlp_gain,
    gate_weight,
    up_weight,
    down_weight,
    cotangent,
):
    me = lax.axis_index("fsdp")
    share = lax.axis_index("tensor")
    local_rows = hidden_in.shape[0]
    length = lengths[0]
    head_size = query_gain.shape[0]
    query_width = query_weight.shape[1]
    key_width = key_weight.shape[1]
    sizes = (key_width // head_size, query_width // key_width, head_size)
    masks = row_masks(shares)
    slots = share * local_rows + jnp.arange(local_rows)
    valid_rows = (slots < length).astype(F32)[:, None]
    seq_len = local_rows * shares
    share_at, length_at = share.astype(jnp.int32)[None], lengths
    gains = (query_gain[None, :], key_gain[None, :])

    def relative(values):
        return to_pairs(values, me, members)

    def absolute(values):
        return to_index_order(values, me, members)

    attn_gain, mlp_gain = relative(attn_gain), relative(mlp_gain)

    qkv_near = gather_line(
        jnp.concatenate([query_weight, key_weight, value_weight], axis=1), members
    )
    gate_out_near = gather_line(
        jnp.concatenate([output_gate, out_weight.T], axis=1), members
    )
    down_own = down_weight.T
    down_pair = exchange(down_own, "fsdp", members, 1)
    gate_near = gather_line(hold(gate_weight, qkv_near, down_pair), members)
    up_near = gather_line(hold(up_weight, gate_out_near), members)
    down_near = gather_line(hold(down_own, gate_near), members)
    down_far = gather_line(hold(down_pair, up_near), members)

    residual = relative(hidden_in).astype(F32)
    unit_one, root_one = normalize(residual)
    normed_one = rows_in((unit_one * attn_gain).astype(BF16), shares)
    grad_rows = relative(cotangent).astype(F32) * valid_rows
    tables = rope_tables(seq_len, head_size)
    qkv_full = gather_pair(qkv_near, members)
    branch_full = rows_in(hold(grad_rows.astype(BF16), qkv_full), shares)
    qkv_raw = matmul(normed_one, qkv_full)
    qkv_raw = hold(qkv_raw, gate_out_near)
    attended, *kept = attend_forward(qkv_raw, share_at, length_at, gains, tables, masks, sizes)
    gate_out_full = gather_pair(gate_out_near, members, attended)
    gate_full, out_full = gate_out_full[:, :query_width], gate_out_full[:, query_width:]
    gate_pre = matmul(hold(normed_one, attended, branch_full), gate_full)
    gate_sig = jax.nn.sigmoid(gate_pre)
    gated_out = (attended * gate_sig).astype(BF16)
    half_rows = seq_len // 2
    attn_far = matmul_nt(gated_out[half_rows:], out_full).astype(BF16)
    attn_near = matmul_nt(gated_out[:half_rows], out_full).astype(BF16)
    attn_near = hold(attn_near, gate_near)
    gate_weights = gather_pair(gate_near, members)
    middle = residual + rows_out(attn_near, attn_far, shares)
    unit_two, root_two = normalize(middle)
    normed_two = rows_in((unit_two * mlp_gain).astype(BF16), shares)
    normed_two = hold(normed_two, up_near)
    up_weights = gather_pair(up_near, members)
    ffn_gate = matmul(normed_two, gate_weights)
    ffn_gate = hold(ffn_gate, down_near)
    ffn_up = matmul(normed_two, up_weights)
    ffn_sig = jax.nn.sigmoid(ffn_gate)
    ffn_act = ffn_gate * ffn_sig
    ffn_mid = (ffn_act * ffn_up).astype(BF16)

    def weight_grads(acts, grads):
        half = acts.shape[1] // 2
        far = matmul_tn(acts[:, half:], grads).astype(BF16)
        near = matmul_tn(acts[:, :half], grads).astype(BF16)
        return near, far

    down_near_part, down_far_part = weight_grads(branch_full, ffn_mid)
    down_far_sum = scatter_line(down_far_part, members)
    down_near_sum = scatter_line(down_near_part, members)
    down_arrived = exchange(down_far_sum, "fsdp", members, 1)
    down_shard = (down_near_sum.astype(F32) + down_arrived.astype(F32)).T

    down_far = hold(down_far, down_near_part, down_far_part)
    down_weights = jnp.concatenate([down_near, down_far], axis=0)
    mid_grad = matmul(branch_full, down_weights)
    gate_grad = (mid_grad * ffn_up * ffn_sig * (1.0 + ffn_gate * (1.0 - ffn_sig))).astype(BF16)
    up_grad = (mid_grad * ffn_act).astype(BF16)

    gate_near_sum, gate_far_sum = weight_grads(normed_two, gate_grad)
    gate_arrived = exchange(gate_far_sum, "fsdp", members, 1)

    gate_back, up_back = hold((gate_grad, up_grad), gate_far_sum)

    def ffn_back(rows):
        return matmul_nt(rows(gate_back), gate_weights) + matmul_nt(rows(up_back), up_weights)

    back_far = ffn_back(lambda g: g[half_rows:]).astype(BF16)
    back_near = ffn_back(lambda g: g[:half_rows]).astype(BF16)
    up_near_sum, up_far_sum = weight_grads(normed_two, up_grad)
    gate_total = add_low(gate_near_sum, gate_arrived)
    norm_two_grad = rows_out(back_near, back_far, shares, up_far_sum, gate_total)
    up_arrived = exchange(up_far_sum, "fsdp", members, 1)

    mlp_gain_part = jnp.sum(norm_two_grad * unit_two, axis=0)
    middle_grad = grad_rows + norm_back(norm_two_grad, unit_two, root_two, mlp_gain)
    mid_late = hold(ffn_mid, norm_two_grad)
    branch_far = matmul_nt(mid_late[half_rows:], down_weights).astype(BF16)
    branch_near = matmul_nt(mid_late[:half_rows], down_weights).astype(BF16)
    attn_full_grad = rows_in(middle_grad.astype(BF16), shares, branch_near, branch_far)
    gate_shard = scatter_line(gate_total, members)

    gated_grad = matmul(attn_full_grad, out_full)
    attended_grad = hold((gated_grad * gate_sig).astype(BF16), down_far_sum)
    gate_pre_grad = (gated_grad * attended * gate_sig * (1.0 - gate_sig)).astype(BF16)
    gate_attn_near_sum, gate_attn_far_sum = weight_grads(normed_one, gate_pre_grad)
    out_near_sum, out_far_sum = weight_grads(attn_full_grad, gated_out)
    gate_out_near_sum = jnp.concatenate([gate_attn_near_sum, out_near_sum], axis=1)
    gate_out_far_sum = jnp.concatenate([gate_attn_far_sum, out_far_sum], axis=1)
    gate_out_arrived = exchange(gate_out_far_sum, "fsdp", members, 1)
    ffn_branch = rows_out(branch_near, hold(branch_far, attn_full_grad), shares)
    output = absolute(((middle + ffn_branch) * valid_rows).astype(BF16))
    qkv_send, gain_parts = attend_backward(
        attended_grad, qkv_raw, kept, share_at, length_at, gains, tables, masks, sizes
    )
    qkv_near_sum, qkv_far_sum = weight_grads(normed_one, qkv_send)
    qkv_arrived = exchange(qkv_far_sum, "fsdp", members, 1)
    one_send, one_gate = hold((qkv_send, gate_pre_grad), qkv_far_sum)

    def attn_back(rows):
        return matmul_nt(rows(one_send), qkv_full) + matmul_nt(rows(one_gate), gate_full)

    one_far = attn_back(lambda g: g[half_rows:]).astype(BF16)
    one_near = attn_back(lambda g: g[:half_rows]).astype(BF16)
    up_total = add_low(up_near_sum, hold(up_arrived, one_near, one_far, down_near_sum))
    up_shard = scatter_line(up_total, members)
    norm_one_grad = rows_out(one_near, one_far, shares)
    attn_gain_part = jnp.sum(norm_one_grad * unit_one, axis=0)
    grad_hidden = absolute(
        middle_grad + norm_back(norm_one_grad, unit_one, root_one, attn_gain)
    )
    gain_totals = sum_everywhere(
        jnp.concatenate(
            [absolute(attn_gain_part), absolute(mlp_gain_part), gain_parts[0], gain_parts[1]]
        ),
        (("tensor", shares), ("fsdp", members)),
    )
    gate_out_total = add_low(
        gate_out_near_sum, hold(gate_out_arrived, gate_shard, norm_one_grad, ffn_branch)
    )
    gate_out_shard = scatter_line(gate_out_total, members)
    qkv_total = add_low(qkv_near_sum, hold(qkv_arrived, gate_out_total, up_shard))
    qkv_shard = scatter_line(qkv_total, members)
    gate_shard = gate_shard.astype(F32)
    up_shard = up_shard.astype(F32)
    gate_out_shard = gate_out_shard.astype(F32)
    qkv_shard = hold(
        qkv_shard, gain_totals, grad_hidden, output, gate_shard, up_shard, gate_out_shard, down_shard
    ).astype(F32)
    width = hidden_in.shape[1]
    return (
        output,
        grad_hidden,
        gain_totals[:width],
        qkv_shard[:, :query_width],
        qkv_shard[:, query_width : query_width + key_width],
        qkv_shard[:, query_width + key_width :],
        gate_out_shard[:, :query_width],
        gain_totals[2 * width : 2 * width + head_size],
        gain_totals[2 * width + head_size :],
        gate_out_shard[:, query_width:].T,
        gain_totals[width : 2 * width],
        gate_shard,
        up_shard,
        down_shard,
    )


def solution(mesh):
    members, shares = mesh.shape["fsdp"], mesh.shape["tensor"]

    def layer(*operands):
        return body(members, shares, *operands)

    tokens = P(("fsdp", "tensor"), None)
    return jax.shard_map(
        layer,
        mesh=mesh,
        in_specs=(
            tokens,
            P("fsdp"),
            P(),
            P("fsdp", "tensor"),
            P("fsdp", "tensor"),
            P("fsdp", "tensor"),
            P("fsdp", "tensor"),
            P(),
            P(),
            P("tensor", "fsdp"),
            P(),
            P("fsdp", "tensor"),
            P("fsdp", "tensor"),
            P("tensor", "fsdp"),
            tokens,
        ),
        out_specs=(
            tokens,
            tokens,
            P(),
            P("fsdp", "tensor"),
            P("fsdp", "tensor"),
            P("fsdp", "tensor"),
            P("fsdp", "tensor"),
            P(),
            P(),
            P("tensor", "fsdp"),
            P(),
            P("fsdp", "tensor"),
            P("fsdp", "tensor"),
            P("tensor", "fsdp"),
        ),
        check_vma=False,
    )
```

time: 1160 us -> 795 us (0.69)
  waiting for transfers between devices: 570 us -> 402 us
  starting transfers between devices: 151 us -> 32.8 us
  local copies, waits for them, and re-layouts: 144 us -> 74.4 us
  Pallas kernels: 0 us -> 41.7 us
  matrix products: 207 us -> 168 us
  other arithmetic: 83.5 us -> 53 us
  between operations: 3.68 us -> 16.5 us
    ppermute x95 -> x35, waiting for transfers between devices: 570 us -> 323 us  [exchange(): return lax.ppermute(values, axis, [(i, i ^ mask) for i in range(size)])]
    ppermute x95 -> x35, starting transfers between devices: 151 us -> 30.7 us  [exchange(): return lax.ppermute(values, axis, [(i, i ^ mask) for i in range(size)])]
    all_gather x0 -> x6, waiting for transfers between devices: none -> 78.8 us  [gather_line(): lax.all_gather(shard, 'fsdp', axis=0, tiled=True, axis_index_groups=lines...]
    pallas_call x0 -> x2, Pallas kernels: none -> 41.7 us  [the longest x1 23.6 us: attend_backward(): pl.pallas_call(functools.partial(attend_backward_kernel, masks, head_size...]
    unnamed x314 -> x137, local copies, waits for them, and re-layouts: 71.4 us -> 31.3 us
    dot_general x14 -> x0, matrix products: 37.2 us -> none  [the longest x4 12.7 us: one_block(): jnp.einsum('qkgd,skd->kgqs', qblock, keys_b, preferred_element_type=F32)]
    while x21 -> x0, local copies, waits for them, and re-layouts: 23.2 us -> none
    dot_general x6 -> x12, matrix products: 61.3 us -> 52.3 us  [matmul_nt(): lax.dot_general(first_op, second_op, (((1,), (1,)), ((), ())), preferred_...]
  transfers between devices with their start and end apart: 95 -> 47, of which waited for: 35 -> 22; matrix products, arithmetic and copies ran while one was open for 26% -> 35% of each run, Pallas kernels for 0% -> 5%
where the time goes in v2:
time: 795 us; the launch traced here: 788 us
  waiting for transfers between devices  402 us (51%)
  matrix products  168 us (21%)
  local copies, waits for them, and re-layouts  74.4 us (9%)
  other arithmetic  53 us (7%)
  Pallas kernels  41.7 us (5%)
  starting transfers between devices  32.8 us (4%)
  between operations  16.5 us (2%)
    ppermute x35, waiting for transfers between devices, exchange(): return lax.ppermute(values, axis, [(i, i ^ mask) for i in range(size)])  323 us
    all_gather x6, waiting for transfers between devices, gather_line(): lax.all_gather(shard, 'fsdp', axis=0, tiled=True, axis_index_groups=lines...  78.8 us
    dot_general x12, matrix products, matmul_tn(): lax.dot_general(first_op, second_op, (((0,), (0,)), ((), ())), preferred_...  59.5 us
    dot_general x6, matrix products, matmul(): return jnp.dot(first_op, second_op, preferred_element_type=F32)  56 us
    dot_general x12, matrix products, matmul_nt(): lax.dot_general(first_op, second_op, (((1,), (1,)), ((), ())), preferred_...  52.3 us
    unnamed x137, local copies, waits for them, and re-layouts  31.3 us
    ppermute x35, starting transfers between devices, exchange(): return lax.ppermute(values, axis, [(i, i ^ mask) for i in range(size)])  30.7 us
    pallas_call x1, Pallas kernels, attend_backward(): pl.pallas_call(functools.partial(attend_backward_kernel, masks, head_size...  23.6 us
  transfers between devices with their start and end apart: 47, of which 22 were waited for; matrix products, arithmetic and copies ran while one was open for 35% of the time, Pallas kernels for 5%

profile of v2, /device:TPU:0, one launch (start us, length us, event | category | flops | bytes accessed | tf_op | source)
XLA Modules:
  0.0 787.7 jit_solution(712879767011165055)
XLA Ops:
  15.4 17.6 %collective-permute-done.8 = bf16[256,1536]{0,1:T(8,128)(2,1)} collective-permute-done((bf16[256,1536]{0,1:T(8,128)(2,1)S(1)}, bf16[256,1536]{0,1:T(8,128)(2,1)}, u32[]{:S(2)}, u32[]{:S(2)}) %collective-permute-start.8) | collective-permute-done | bytes 786464 | tf_op jit(solution)/shard_map/ppermute | solution.py:18
  33.1 25.8 %all-gather.7.cloned.1.call-done = bf16[1024,1024]{1,0:T(8,128)(2,1)} async-done(((bf16[256,1024]{1,0:T(8,128)(2,1)}), bf16[1024,1024]{1,0:T(8,128)(2,1)}) %all-gather.7.cloned.1.call-update) | async-done | bytes 2097168 | tf_op jit(solution)/shard_map/all_gather | solution.py:26
  70.5 22.5 %collective-permute-done = bf16[256,2048]{1,0:T(8,128)(2,1)} collective-permute-done((bf16[256,2048]{1,0:T(8,128)(2,1)}, bf16[256,2048]{1,0:T(8,128)(2,1)}, u32[]{:S(2)}, u32[]{:S(2)}) %collective-permute-start) | collective-permute-done | bytes 1048608 | tf_op jit(solution)/shard_map/ppermute | solution.py:18
  93.3 12.6 %all-gather.9.cloned.1.call-done = bf16[1024,1024]{0,1:T(8,128)(2,1)} async-done(((bf16[256,1024]{0,1:T(8,128)(2,1)}), bf16[1024,1024]{0,1:T(8,128)(2,1)}) %all-gather.9.cloned.1.call-update) | async-done | bytes 2097168 | tf_op jit(solution)/shard_map/all_gather | solution.py:26
  127.2 11.9 %collective-permute-done.4 = bf16[256,2048]{1,0:T(8,128)(2,1)S(1)} collective-permute-done((bf16[256,2048]{1,0:T(8,128)(2,1)S(1)}, bf16[256,2048]{1,0:T(8,128)(2,1)S(1)}, u32[]{:S(2)}, u32[]{:S(2)}) %collective-permute-start.4) | collective-permute-done | bytes 1048608 | tf_op jit(solution)/shard_map/ppermute | solution.py:18
  139.1 8.6 %fusion.70.query_ref.key_ref.value_ref = f32[1024,1024]{1,0:T(8,128)} fusion(bf16[2048,1024]{1,0:T(8,128)(2,1)S(1)} %copy-done.26, bf16[256,2048]{1,0:T(8,128)(2,1)} %collective-permute-done.2, bf16[256,2048]{1,0:T(8,128)(2,1)} %collective-permute-done.1, bf16[256,2048]{1,0:T(8,128)(2,1)} %collective-permute-done, bf16[256,2048]{1,0:T(8,128)(2,1)} %fusion.5), kind=kOutput, calls=%fused_computation.162 | convolution fusion | flops 4311744512 | bytes 12582912 | tf_op jit(solution)/shard_map/dot_general | solution.py:115
  147.8 18.1 %attend_forward.1 = (f32[1024,512]{1,0:T(8,128)}, f32[1024,512]{1,0:T(8,128)}, bf16[1024,512]{1,0:T(8,128)(2,1)}, bf16[1024,256]{1,0:T(8,128)(2,1)}, bf16[1024,256]{1,0:T(8,128)(2,1)}) custom-call(s32[1]{0:T(128)} %bitcast.share_ref, s32[1]{0:T(128)} %copy.64.length_ref, f32[1024,1024]{1,0:T(8,128)} %fusion.70.query_ref.key_ref.value_ref, ...), custom_call_target="tpu_custom_call" | custom-call | flops 1024 | bytes 1024 | tf_op jit(solution)/shard_map/attend_forward/pallas_call | solution.py:326
  192.6 40.3 %all-gather.13.cloned.1.call-done = bf16[1024,1536]{1,0:T(8,128)(2,1)} async-done(((bf16[256,1536]{1,0:T(8,128)(2,1)}), bf16[1024,1536]{1,0:T(8,128)(2,1)}) %all-gather.13.cloned.1.call-update) | async-done | bytes 3145744 | tf_op jit(solution)/shard_map/all_gather | solution.py:26
  239.4 22.6 %collective-permute-done.11 = bf16[256,2048]{1,0:T(8,128)(2,1)} collective-permute-done((bf16[256,2048]{1,0:T(8,128)(2,1)S(1)}, bf16[256,2048]{1,0:T(8,128)(2,1)}, u32[]{:S(2)}, u32[]{:S(2)}) %collective-permute-start.11) | collective-permute-done | bytes 1048608 | tf_op jit(solution)/shard_map/ppermute | solution.py:18
  266.5 62.1 %collective-permute-done.15 = bf16[1024,1536]{1,0:T(8,128)(2,1)} collective-permute-done((bf16[1024,1536]{1,0:T(8,128)(2,1)}, bf16[1024,1536]{1,0:T(8,128)(2,1)}, u32[]{:S(2)}, u32[]{:S(2)}) %collective-permute-start.15) | collective-permute-done | bytes 3145760 | tf_op jit(solution)/shard_map/ppermute | solution.py:18
  337.0 8.7 %fusion.77 = f32[1024,1536]{1,0:T(8,128)} fusion(bf16[1024,2048]{1,0:T(8,128)(2,1)S(1)} %pad_maximum_fusion.1, bf16[2048,1536]{1,0:T(8,128)(2,1)S(1)} %constant_dynamic-update-slice_fusion.8), kind=kOutput, calls=%fused_computation.169 | convolution fusion | flops 6442450944 | bytes 16777216 | tf_op jit(solution)/shard_map/dot_general | solution.py:115
  345.7 13.1 %multiply_convert_fusion.2 = (bf16[1024,1536]{1,0:T(8,128)(2,1)S(1)}, f32[1024,1536]{1,0:T(8,128)}) fusion(f32[1024,1536]{1,0:T(8,128)} %fusion.77, bf16[1024,2048]{1,0:T(8,128)(2,1)} %copy-done.13, bf16[2048,1536]{1,0:T(8,128)(2,1)} %copy-done.23), kind=kOutput, calls=%fused_computation.4 | convolution fusion | flops 6451888128 | bytes 26214400 | tf_op jit(solution)/shard_map/dot_general | solution.py:115
  367.1 7.7 convolution_convert_fusion.5
  383.0 16.2 %multiply_convert_fusion = (bf16[1024,1536]{1,0:T(8,128)(2,1)}, bf16[1024,1536]{1,0:T(8,128)(2,1)}) fusion(f32[1024,1536]{1,0:T(8,128)} %fusion.77, f32[1024,1536]{1,0:T(8,128)} %get-tuple-element.142, bf16[1024,2048]{1,0:T(8,128)(2,1)} %constant_dynamic-update-slice_fusion.2, bf16[2048,1536]{0,1:T(8,128)(2,1)} %constant_dynamic-update-slice_fusion.12), kind=kOutput, calls=%fused_computation.2 | convolution fusion | flops 6462898176 | bytes 29360128 | tf_op jit(solution)/shard_map/dot_general | solution.py:115
  440.5 47.9 %collective-permute-done.18 = bf16[1024,1536]{1,0:T(8,128)(2,1)S(1)} collective-permute-done((bf16[1024,1536]{1,0:T(8,128)(2,1)}, bf16[1024,1536]{1,0:T(8,128)(2,1)S(1)}, u32[]{:S(2)}, u32[]{:S(2)}) %collective-permute-start.18) | collective-permute-done | bytes 3145760 | tf_op jit(solution)/shard_map/ppermute | solution.py:18
  505.1 8.1 %convolution_convert_fusion.6 = bf16[512,2048]{1,0:T(8,128)(2,1)} fusion(bf16[2048,1536]{0,1:T(8,128)(2,1)} %constant_dynamic-update-slice_fusion.12, bf16[1024,1536]{1,0:T(8,128)(2,1)} %copy-done.54), kind=kOutput, calls=%fused_computation.29 | convolution fusion | flops 3222274048 | bytes 9961472 | tf_op jit(solution)/shard_map/dot_general | solution.py:125
  513.2 10.2 %collective-permute-done.19 = bf16[256,2048]{1,0:T(8,128)(2,1)} collective-permute-done((bf16[256,2048]{1,0:T(8,128)(2,1)S(1)}, bf16[256,2048]{1,0:T(8,128)(2,1)}, u32[]{:S(2)}, u32[]{:S(2)}) %collective-permute-start.19) | collective-permute-done | bytes 1048608 | tf_op jit(solution)/shard_map/ppermute | solution.py:18
  532.7 23.6 %attend_backward.1 = (bf16[1024,1024]{1,0:T(8,128)(2,1)}, f32[8,128]{1,0:T(8,128)}) custom-call(s32[1]{0:T(128)} %bitcast.share_ref, s32[1]{0:T(128)} %copy.64.length_ref, bf16[1024,512]{1,0:T(8,128)(2,1)} %get-tuple-element.65.grad_ref, f32[1024,1024]{1,0:T(8,128)} %fusion.70.query_ref.key_ref.value_ref, f32[1024,1024]{1,0:T(8,128)} %fusion.70.query_ref.key_ref.value_ref, ...), custom_call_target="tpu_custom_call" | custom-call | flops 1024 | bytes 1024 | tf_op jit(solution)/shard_map/attend_backward/pallas_call | solution.py:353
  573.9 20.3 %collective-permute-done.33 = bf16[1024,1536]{1,0:T(8,128)(2,1)} collective-permute-done((bf16[1024,1536]{1,0:T(8,128)(2,1)}, bf16[1024,1536]{1,0:T(8,128)(2,1)}, u32[]{:S(2)}, u32[]{:S(2)}) %collective-permute-start.33) | collective-permute-done | bytes 3145760 | tf_op jit(solution)/shard_map/ppermute | solution.py:18
  594.3 8.6 %add_convert_fusion = bf16[1024,1536]{1,0:T(8,128)(2,1)} fusion(bf16[1024,1536]{1,0:T(8,128)(2,1)} %collective-permute-done.33, bf16[1024,1536]{1,0:T(8,128)(2,1)} %get-tuple-element.60, bf16[1024,2048]{1,0:T(8,128)(2,1)} %copy-done.13), kind=kOutput, calls=%fused_computation | convolution fusion | flops 3229089792 | bytes 11534336 | tf_op jit(solution)/shard_map/dot_general | solution.py:119
  619.3 19.0 %collective-permute-done.23 = bf16[256,2048]{1,0:T(8,128)(2,1)S(1)} collective-permute-done((bf16[256,2048]{1,0:T(8,128)(2,1)S(1)}, bf16[256,2048]{1,0:T(8,128)(2,1)S(1)}, u32[]{:S(2)}, u32[]{:S(2)}) %collective-permute-start.23) | collective-permute-done | bytes 1048608 | tf_op jit(solution)/shard_map/ppermute | solution.py:18
  640.0 20.0 %collective-permute-done.25 = bf16[256,2048]{1,0:T(8,128)(2,1)S(1)} collective-permute-done((bf16[256,2048]{1,0:T(8,128)(2,1)S(1)}, bf16[256,2048]{1,0:T(8,128)(2,1)S(1)}, u32[]{:S(2)}, u32[]{:S(2)}) %collective-permute-start.25) | collective-permute-done | bytes 1048608 | tf_op jit(solution)/shard_map/ppermute | solution.py:18
  668.1 46.9 %collective-permute-done.31 = bf16[1024,1024]{1,0:T(8,128)(2,1)} collective-permute-done((bf16[1024,1024]{1,0:T(8,128)(2,1)}, bf16[1024,1024]{1,0:T(8,128)(2,1)}, u32[]{:S(2)}, u32[]{:S(2)}) %collective-permute-start.31) | collective-permute-done | bytes 2097184 | tf_op jit(solution)/shard_map/ppermute | solution.py:18
  722.3 7.9 collective-permute-done.34
  (331 shorter events, 270.9 us)
Async XLA Ops:
  7.2 51.6 %all-gather.7.cloned.1.call-start = ((), (), s32[]{:S(2)}) async-start(), calls=%async_computation.6 | async-start | bytes 2621440 | tf_op jit(solution)/shard_map/all_gather | solution.py:26
  9.4 96.6 %all-gather.9.cloned.1.call-start = ((), (), s32[]{:S(2)}) async-start(), calls=%async_computation.7 | async-start | bytes 2621440 | tf_op jit(solution)/shard_map/all_gather | solution.py:26
  12.3 171.2 %all-gather.11.cloned.1.call-start = ((), (), s32[]{:S(2)}) async-start(), calls=%async_computation.8 | async-start | bytes 3932160 | tf_op jit(solution)/shard_map/all_gather | solution.py:26
  58.9 174.1 %all-gather.13.cloned.1.call-start = ((), (), s32[]{:S(2)}) async-start(), calls=%async_computation.9 | async-start | bytes 3932160 | tf_op jit(solution)/shard_map/all_gather | solution.py:26
  69.6 52.1 %collective-permute-start.1 = (bf16[256,2048]{1,0:T(8,128)(2,1)}, bf16[256,2048]{1,0:T(8,128)(2,1)}, u32[]{:S(2)}, u32[]{:S(2)}) collective-permute-start(bf16[256,2048]{1,0:T(8,128)(2,1)} %fusion.5), channel_id=1, source_target_pairs={{0,1},{1,0},{2,3},{3,2},{4,5},{5,4},{6,7},{7,6},{8,9},{9,8},{10,11... | collective-permute-start | bytes 3145736 | tf_op jit(solution)/shard_map/ppermute | solution.py:18
  106.0 59.8 %collective-permute-start.7 = (bf16[1024,1024]{0,1:T(8,128)(2,1)}, bf16[1024,1024]{0,1:T(8,128)(2,1)}, u32[]{:S(2)}, u32[]{:S(2)}) collective-permute-start(bf16[1024,1024]{0,1:T(8,128)(2,1)} %all-gather.9.cloned.1.call-done), channel_id=1, source_target_pairs={{0,4},{4,0},{8,12},{12,8},{16,20},{20,16},{24,28},{28,24},{1,5},{5... | collective-permute-start | bytes 6291464 | tf_op jit(solution)/shard_map/ppermute | solution.py:18
  121.5 224.3 %all-gather.15.cloned.1.call-start = ((), (), s32[]{:S(2)}) async-start(), calls=%async_computation.10 | async-start | bytes 3932160 | tf_op jit(solution)/shard_map/all_gather | solution.py:26
  183.6 195.3 %all-gather.17.cloned.1.call-start = ((), (), s32[]{:S(2)}) async-start(), calls=%async_computation.11 | async-start | bytes 3932160 | tf_op jit(solution)/shard_map/all_gather | solution.py:26
  191.2 73.2 %collective-permute-start.14 = (bf16[1024,1536]{1,0:T(8,128)(2,1)}, bf16[1024,1536]{1,0:T(8,128)(2,1)}, u32[]{:S(2)}, u32[]{:S(2)}) collective-permute-start(bf16[1024,1536]{1,0:T(8,128)(2,1)} %all-gather.11.cloned.1.call-done), channel_id=1, source_target_pairs={{0,4},{4,0},{8,12},{12,8},{16,20},{20,16},{24,28},{28,24},{1,5},{5... | collective-permute-start | bytes 9437192 | tf_op jit(solution)/shard_map/ppermute | solution.py:18
  232.9 95.7 %collective-permute-start.15 = (bf16[1024,1536]{1,0:T(8,128)(2,1)}, bf16[1024,1536]{1,0:T(8,128)(2,1)}, u32[]{:S(2)}, u32[]{:S(2)}) collective-permute-start(bf16[1024,1536]{1,0:T(8,128)(2,1)} %all-gather.13.cloned.1.call-done), channel_id=1, source_target_pairs={{0,4},{4,0},{8,12},{12,8},{16,20},{20,16},{24,28},{28,24},{1,5},{5... | collective-permute-start | bytes 9437192 | tf_op jit(solution)/shard_map/ppermute | solution.py:18
  238.8 293.9 %reduce-scatter.7.cloned.1.call-start = ((), (), s32[]{:S(2)}) async-start(), calls=%async_computation.12 | async-start | bytes 3932160 | tf_op jit(solution)/shard_map/reduce_scatter | solution.py:37
  239.3 91.5 %collective-permute-start.12 = (bf16[256,2048]{1,0:T(8,128)(2,1)S(1)}, bf16[256,2048]{1,0:T(8,128)(2,1)S(1)}, u32[]{:S(2)}, u32[]{:S(2)}) collective-permute-start(bf16[256,2048]{1,0:T(8,128)(2,1)S(1)} %multiply_convert_fusion.6), channel_id=1, source_target_pairs={{0,1},{1,0},{2,3},{3,2},{4,5},{5,4},{6,7},{7,6},{8,9},{9,8},{10,11... | collective-permute-start | bytes 3145736 | tf_op jit(solution)/shard_map/ppermute | solution.py:18
  262.0 71.4 %collective-permute-start.13 = (bf16[256,2048]{1,0:T(8,128)(2,1)}, bf16[256,2048]{1,0:T(8,128)(2,1)S(1)}, u32[]{:S(2)}, u32[]{:S(2)}) collective-permute-start(bf16[256,2048]{1,0:T(8,128)(2,1)} %collective-permute-done.11), channel_id=1, source_target_pairs={{0,1},{1,0},{2,3},{3,2},{4,5},{5,4},{6,7},{7,6},{8,9},{9,8},{10,11... | collective-permute-start | bytes 3145736 | tf_op jit(solution)/shard_map/ppermute | solution.py:18
  374.7 219.5 %reduce-scatter.11.cloned.1.call-start = ((), (), s32[]{:S(2)}) async-start(), calls=%async_computation.14 | async-start | bytes 3932160 | tf_op jit(solution)/shard_map/reduce_scatter | solution.py:37
  417.4 243.8 %reduce-scatter.9.cloned.1.call-start = ((), (), s32[]{:S(2)}) async-start(), calls=%async_computation.13 | async-start | bytes 3932160 | tf_op jit(solution)/shard_map/reduce_scatter | solution.py:37
  417.6 70.8 %collective-permute-start.18 = (bf16[1024,1536]{1,0:T(8,128)(2,1)}, bf16[1024,1536]{1,0:T(8,128)(2,1)S(1)}, u32[]{:S(2)}, u32[]{:S(2)}) collective-permute-start(bf16[1024,1536]{1,0:T(8,128)(2,1)} %convolution_convert_fusion.3), channel_id=1, source_target_pairs={{0,4},{4,0},{8,12},{12,8},{16,20},{20,16},{24,28},{28,24},{1,5},{5... | collective-permute-start | bytes 9437192 | tf_op jit(solution)/shard_map/ppermute | solution.py:18
  434.6 58.8 %collective-permute-start.17 = (bf16[256,2048]{1,0:T(8,128)(2,1)S(1)}, bf16[256,2048]{1,0:T(8,128)(2,1)}, u32[]{:S(2)}, u32[]{:S(2)}) collective-permute-start(bf16[256,2048]{1,0:T(8,128)(2,1)S(1)} %add_convert_fusion.10), channel_id=1, source_target_pairs={{0,2},{1,3},{2,0},{3,1},{4,6},{5,7},{6,4},{7,5},{8,10},{9,11},{10,... | collective-permute-start | bytes 3145736 | tf_op jit(solution)/shard_map/ppermute | solution.py:18
  504.6 210.3 %reduce-scatter.13.cloned.1.call-start = ((), (), s32[]{:S(2)}) async-start(), calls=%async_computation.15 | async-start | bytes 3932160 | tf_op jit(solution)/shard_map/reduce_scatter | solution.py:37
  523.4 70.8 %collective-permute-start.33 = (bf16[1024,1536]{1,0:T(8,128)(2,1)}, bf16[1024,1536]{1,0:T(8,128)(2,1)}, u32[]{:S(2)}, u32[]{:S(2)}) collective-permute-start(bf16[1024,1536]{1,0:T(8,128)(2,1)} %convolution_convert_fusion.2), channel_id=1, source_target_pairs={{0,4},{4,0},{8,12},{12,8},{16,20},{20,16},{24,28},{28,24},{1,5},{5... | collective-permute-start | bytes 9437192 | tf_op jit(solution)/shard_map/ppermute | solution.py:18
  602.9 170.0 %reduce-scatter.17.cloned.1.call-start = ((), (), s32[]{:S(2)}) async-start(), calls=%async_computation.17 | async-start | bytes 2621440 | tf_op jit(solution)/shard_map/reduce_scatter | solution.py:37
  609.8 51.4 %collective-permute-start.32 = (bf16[1024,1024]{0,1:T(8,128)(2,1)S(1)}, bf16[1024,1024]{0,1:T(8,128)(2,1)}, u32[]{:S(2)}, u32[]{:S(2)}) collective-permute-start(bf16[1024,1024]{0,1:T(8,128)(2,1)S(1)} %pad_maximum_fusion.4), channel_id=1, source_target_pairs={{0,4},{4,0},{8,12},{12,8},{16,20},{20,16},{24,28},{28,24},{1,5},{5... | collective-permute-start | bytes 6291464 | tf_op jit(solution)/shard_map/ppermute | solution.py:18
  665.7 111.1 %reduce-scatter.15.cloned.1.call-start = ((), (), s32[]{:S(2)}) async-start(), calls=%async_computation.16 | async-start | bytes 2621440 | tf_op jit(solution)/shard_map/reduce_scatter | solution.py:37
  666.0 48.9 %collective-permute-start.31 = (bf16[1024,1024]{1,0:T(8,128)(2,1)}, bf16[1024,1024]{1,0:T(8,128)(2,1)}, u32[]{:S(2)}, u32[]{:S(2)}) collective-permute-start(bf16[1024,1024]{1,0:T(8,128)(2,1)} %convolution_convert_fusion.10), channel_id=1, source_target_pairs={{0,4},{4,0},{8,12},{12,8},{16,20},{20,16},{24,28},{28,24},{1,5},{5... | collective-permute-start | bytes 6291464 | tf_op jit(solution)/shard_map/ppermute | solution.py:18
  667.6 62.5 %collective-permute-start.34 = (bf16[256,1536]{1,0:T(8,128)(2,1)}, bf16[256,1536]{1,0:T(8,128)(2,1)}, u32[]{:S(2)}, u32[]{:S(2)}) collective-permute-start(bf16[256,1536]{1,0:T(8,128)(2,1)} %reduce-scatter.7.cloned.1.call-done), channel_id=1, source_target_pairs={{0,4},{4,0},{8,12},{12,8},{16,20},{20,16},{24,28},{28,24},{1,5},{5... | collective-permute-start | bytes 2359304 | tf_op jit(solution)/shard_map/ppermute | solution.py:18
  (83 other events, 1696.8 us)
Sparse Core Ops, SparseCore 0:
  10.2 48.6 all-gather.6
  61.0 44.9 all-gather.8
  107.6 61.7 all-gather.10
  170.8 62.1 all-gather.12
  234.3 62.0 all-gather.14
  297.9 61.5 all-gather.16
  374.9 58.2 reduce-scatter.6
  435.5 60.2 reduce-scatter.10
  504.7 58.5 reduce-scatter.8
  603.0 58.1 reduce-scatter.12
  665.8 41.8 reduce-scatter.16
  721.6 42.3 reduce-scatter.14

commit v3 on v2

--- a/solution.py
+++ b/solution.py
@@ -53,6 +53,12 @@
     odd = blocks[..., 1, :].reshape(values.shape[:-1] + (-1,))
     first = me % 2 == 0
     return jnp.concatenate([jnp.where(first, even, odd), jnp.where(first, odd, even)], axis=-1)
+
+
+def swap_pairs(values, me, count):
+    blocks = values.reshape(values.shape[0], count // 2, 2, values.shape[1] // count)
+    swapped = jnp.concatenate([blocks[:, :, 1:], blocks[:, :, :1]], axis=2)
+    return jnp.where(me % 2 == 0, values, swapped.reshape(values.shape))
 
 
 def to_index_order(values, me, count):
@@ -441,8 +447,8 @@
     down_pair = exchange(down_own, "fsdp", members, 1)
     gate_near = gather_line(hold(gate_weight, qkv_near, down_pair), members)
     up_near = gather_line(hold(up_weight, gate_out_near), members)
-    down_near = gather_line(hold(down_own, gate_near), members)
-    down_far = gather_line(hold(down_pair, up_near), members)
+    down_both = jnp.concatenate([down_own, down_pair], axis=0)
+    down_weights = gather_line(hold(down_both, gate_near), members)
 
     residual = relative(hidden_in).astype(F32)
     unit_one, root_one = normalize(residual)
@@ -450,10 +456,11 @@
     grad_rows = relative(cotangent).astype(F32) * valid_rows
     tables = rope_tables(seq_len, head_size)
     qkv_full = gather_pair(qkv_near, members)
-    branch_full = rows_in(hold(grad_rows.astype(BF16), qkv_full), shares)
     qkv_raw = matmul(normed_one, qkv_full)
     qkv_raw = hold(qkv_raw, gate_out_near)
     attended, *kept = attend_forward(qkv_raw, share_at, length_at, gains, tables, masks, sizes)
+    branch_rows = swap_pairs(cotangent.astype(F32) * valid_rows, me, members).astype(BF16)
+    branch_full = rows_in(hold(branch_rows, qkv_full), shares, attended)
     gate_out_full = gather_pair(gate_out_near, members, attended)
     gate_full, out_full = gate_out_full[:, :query_width], gate_out_full[:, query_width:]
     gate_pre = matmul(hold(normed_one, attended, branch_full), gate_full)
@@ -468,10 +475,13 @@
     unit_two, root_two = normalize(middle)
     normed_two = rows_in((unit_two * mlp_gain).astype(BF16), shares)
     normed_two = hold(normed_two, up_near)
-    up_weights = gather_pair(up_near, members)
+    half_width = normed_two.shape[1] // 2
+    up_far = exchange(up_near, "fsdp", members, 1)
     ffn_gate = matmul(normed_two, gate_weights)
-    ffn_gate = hold(ffn_gate, down_near)
-    ffn_up = matmul(normed_two, up_weights)
+    up_part = matmul(normed_two[:, :half_width], up_near)
+    up_far = hold(up_far, up_part, ffn_gate)
+    up_weights = jnp.concatenate([up_near, up_far], axis=0)
+    ffn_up = up_part + matmul(normed_two[:, half_width:], up_far)
     ffn_sig = jax.nn.sigmoid(ffn_gate)
     ffn_act = ffn_gate * ffn_sig
     ffn_mid = (ffn_act * ffn_up).astype(BF16)
@@ -482,15 +492,13 @@
         near = matmul_tn(acts[:, :half], grads).astype(BF16)
         return near, far
 
-    down_near_part, down_far_part = weight_grads(branch_full, ffn_mid)
-    down_far_sum = scatter_line(down_far_part, members)
-    down_near_sum = scatter_line(down_near_part, members)
-    down_arrived = exchange(down_far_sum, "fsdp", members, 1)
-    down_shard = (down_near_sum.astype(F32) + down_arrived.astype(F32)).T
-
-    down_far = hold(down_far, down_near_part, down_far_part)
-    down_weights = jnp.concatenate([down_near, down_far], axis=0)
-    mid_grad = matmul(branch_full, down_weights)
+    down_part = matmul_tn(branch_full, ffn_mid).astype(BF16)
+    down_sum = scatter_line(down_part, members)
+    own_rows = down_sum.shape[0] // 2
+    down_arrived = exchange(down_sum[own_rows:], "fsdp", members, 1)
+    down_shard = (down_sum[:own_rows].astype(F32) + down_arrived.astype(F32)).T
+
+    mid_grad = matmul(branch_full, hold(down_weights, down_part))
     gate_grad = (mid_grad * ffn_up * ffn_sig * (1.0 + ffn_gate * (1.0 - ffn_sig))).astype(BF16)
     up_grad = (mid_grad * ffn_act).astype(BF16)
 
@@ -518,7 +526,7 @@
     gate_shard = scatter_line(gate_total, members)
 
     gated_grad = matmul(attn_full_grad, out_full)
-    attended_grad = hold((gated_grad * gate_sig).astype(BF16), down_far_sum)
+    attended_grad = hold((gated_grad * gate_sig).astype(BF16), down_sum)
     gate_pre_grad = (gated_grad * attended * gate_sig * (1.0 - gate_sig)).astype(BF16)
     gate_attn_near_sum, gate_attn_far_sum = weight_grads(normed_one, gate_pre_grad)
     out_near_sum, out_far_sum = weight_grads(attn_full_grad, gated_out)
@@ -526,11 +534,14 @@
     gate_out_far_sum = jnp.concatenate([gate_attn_far_sum, out_far_sum], axis=1)
     gate_out_arrived = exchange(gate_out_far_sum, "fsdp", members, 1)
     ffn_branch = rows_out(branch_near, hold(branch_far, attn_full_grad), shares)
-    output = absolute(((middle + ffn_branch) * valid_rows).astype(BF16))
+    ffn_branch = swap_pairs(ffn_branch, me, members)
+    output = ((absolute(middle) + ffn_branch) * valid_rows).astype(BF16)
     qkv_send, gain_parts = attend_backward(
         attended_grad, qkv_raw, kept, share_at, length_at, gains, tables, masks, sizes
     )
-    qkv_near_sum, qkv_far_sum = weight_grads(normed_one, qkv_send)
+    up_total = add_low(up_near_sum, hold(up_arrived, qkv_send))
+    up_shard = scatter_line(up_total, members)
+    qkv_near_sum, qkv_far_sum = weight_grads(normed_one, hold(qkv_send, up_total))
     qkv_arrived = exchange(qkv_far_sum, "fsdp", members, 1)
     one_send, one_gate = hold((qkv_send, gate_pre_grad), qkv_far_sum)
 
@@ -539,9 +550,11 @@
 
     one_far = attn_back(lambda g: g[half_rows:]).astype(BF16)
     one_near = attn_back(lambda g: g[:half_rows]).astype(BF16)
-    up_total = add_low(up_near_sum, hold(up_arrived, one_near, one_far, down_near_sum))
-    up_shard = scatter_line(up_total, members)
-    norm_one_grad = rows_out(one_near, one_far, shares)
+    gate_out_total = add_low(
+        gate_out_near_sum, hold(gate_out_arrived, gate_shard, one_near, one_far)
+    )
+    gate_out_shard = scatter_line(gate_out_total, members)
+    norm_one_grad = rows_out(one_near, one_far, shares, gate_out_total)
     attn_gain_part = jnp.sum(norm_one_grad * unit_one, axis=0)
     grad_hidden = absolute(
         middle_grad + norm_back(norm_one_grad, unit_one, root_one, attn_gain)
@@ -552,11 +565,7 @@
         ),
         (("tensor", shares), ("fsdp", members)),
     )
-    gate_out_total = add_low(
-        gate_out_near_sum, hold(gate_out_arrived, gate_shard, norm_one_grad, ffn_branch)
-    )
-    gate_out_shard = scatter_line(gate_out_total, members)
-    qkv_total = add_low(qkv_near_sum, hold(qkv_arrived, gate_out_total, up_shard))
+    qkv_total = add_low(qkv_near_sum, hold(qkv_arrived, up_shard, grad_hidden, ffn_branch))
     qkv_shard = scatter_line(qkv_total, members)
     gate_shard = gate_shard.astype(F32)
     up_shard = up_shard.astype(F32)

time: 795 us -> 711 us (0.89)
  waiting for transfers between devices: 402 us -> 311 us
  other arithmetic: 53 us -> 69.4 us
    ppermute x35, waiting for transfers between devices: 323 us -> 257 us  [exchange(): return lax.ppermute(values, axis, [(i, i ^ mask) for i in range(size)])]
    all_gather x6 -> x5, waiting for transfers between devices: 78.8 us -> 45.3 us  [gather_line(): lax.all_gather(shard, 'fsdp', axis=0, tiled=True, axis_index_groups=lines...]
    reshape x0 -> x4, local copies, waits for them, and re-layouts: none -> 10.2 us  [the longest x2 5.5 us: swap_pairs(): return jnp.where(me % 2 == 0, values, swapped.reshape(values.shape))]
    concatenate x0 -> x3, other arithmetic: none -> 8.26 us  [the longest x2 5.64 us: swap_pairs(): swapped = jnp.concatenate([blocks[:, :, 1:], blocks[:, :, :1]], axis=2)]
    reduce_scatter x6 -> x5, waiting for transfers between devices: 0.03 us -> 8.28 us  [scatter_line(): lax.psum_scatter(total, 'fsdp', scatter_dimension=0, tiled=True, axis_ind...]
    dot_general x6 -> x7, matrix products: 56 us -> 47.9 us  [matmul(): return jnp.dot(first_op, second_op, preferred_element_type=F32)]
    unnamed x137 -> x146, local copies, waits for them, and re-layouts: 31.3 us -> 26 us
    dot_general x12 -> x11, matrix products: 59.5 us -> 56.2 us  [matmul_tn(): lax.dot_general(first_op, second_op, (((0,), (0,)), ((), ())), preferred_...]
  transfers between devices with their start and end apart: 47 -> 45, of which waited for: 22 -> 24; matrix products, arithmetic and copies ran while one was open for 35% -> 42% of each run, Pallas kernels for 5% -> 6%
where the time goes in v3:
time: 711 us; the launch traced here: 702 us
  waiting for transfers between devices  311 us (44%)
  matrix products  161 us (23%)
  local copies, waits for them, and re-layouts  73.9 us (10%)
  other arithmetic  69.4 us (10%)
  Pallas kernels  41.6 us (6%)
  starting transfers between devices  28.7 us (4%)
  between operations  16.1 us (2%)
    ppermute x35, waiting for transfers between devices, exchange(): return lax.ppermute(values, axis, [(i, i ^ mask) for i in range(size)])  257 us
    dot_general x12, matrix products, matmul_nt(): lax.dot_general(first_op, second_op, (((1,), (1,)), ((), ())), preferred_...  57.2 us
    dot_general x11, matrix products, matmul_tn(): lax.dot_general(first_op, second_op, (((0,), (0,)), ((), ())), preferred_...  56.2 us
    dot_general x7, matrix products, matmul(): return jnp.dot(first_op, second_op, preferred_element_type=F32)  47.9 us
    all_gather x5, waiting for transfers between devices, gather_line(): lax.all_gather(shard, 'fsdp', axis=0, tiled=True, axis_index_groups=lines...  45.3 us
    ppermute x35, starting transfers between devices, exchange(): return lax.ppermute(values, axis, [(i, i ^ mask) for i in range(size)])  27.9 us
    unnamed x146, local copies, waits for them, and re-layouts  26 us
    pallas_call x1, Pallas kernels, attend_backward(): pl.pallas_call(functools.partial(attend_backward_kernel, masks, head_size...  23.6 us
  transfers between devices with their start and end apart: 45, of which 24 were waited for; matrix products, arithmetic and copies ran while one was open for 42% of the time, Pallas kernels for 6%

profile of v3, /device:TPU:0, one launch (start us, length us, event | category | flops | bytes accessed | tf_op | source)
XLA Modules:
  0.0 702.0 jit_solution(6084809429183819869)
XLA Ops:
  19.3 14.0 %collective-permute-done.8 = bf16[256,1536]{0,1:T(8,128)(2,1)} collective-permute-done((bf16[256,1536]{0,1:T(8,128)(2,1)}, bf16[256,1536]{0,1:T(8,128)(2,1)}, u32[]{:S(2)}, u32[]{:S(2)}) %collective-permute-start.8) | collective-permute-done | bytes 786464 | tf_op jit(solution)/shard_map/ppermute | solution.py:18
  33.2 25.6 %all-gather.6.cloned.1.call-done = bf16[1024,1024]{1,0:T(8,128)(2,1)} async-done(((bf16[256,1024]{1,0:T(8,128)(2,1)}), bf16[1024,1024]{1,0:T(8,128)(2,1)}) %all-gather.6.cloned.1.call-update) | async-done | bytes 2097168 | tf_op jit(solution)/shard_map/all_gather | solution.py:26
  76.7 12.9 %collective-permute-done = bf16[256,2048]{1,0:T(8,128)(2,1)} collective-permute-done((bf16[256,2048]{1,0:T(8,128)(2,1)}, bf16[256,2048]{1,0:T(8,128)(2,1)}, u32[]{:S(2)}, u32[]{:S(2)}) %collective-permute-start) | collective-permute-done | bytes 1048608 | tf_op jit(solution)/shard_map/ppermute | solution.py:18
  90.0 15.9 %all-gather.8.cloned.1.call-done = bf16[1024,1024]{0,1:T(8,128)(2,1)} async-done(((bf16[256,1024]{0,1:T(8,128)(2,1)}), bf16[1024,1024]{0,1:T(8,128)(2,1)}) %all-gather.8.cloned.1.call-update) | async-done | bytes 2097168 | tf_op jit(solution)/shard_map/all_gather | solution.py:26
  123.7 9.9 %fusion.70.query_ref.key_ref.value_ref = f32[1024,1024]{1,0:T(8,128)} fusion(bf16[2048,1024]{1,0:T(8,128)(2,1)} %constant_dynamic-update-slice_fusion, bf16[256,2048]{1,0:T(8,128)(2,1)} %collective-permute-done.2, bf16[256,2048]{1,0:T(8,128)(2,1)} %collective-permute-done.1, bf16[256,2048]{1,0:T(8,128)(2,1)} %collective-permute-done, ...), kind=kOutput, calls=%fused_computation.164 | convolution fusion | flops 4311744512 | bytes 12582912 | tf_op jit(solution)/shard_map/dot_general | solution.py:121
  133.6 18.0 %attend_forward.1 = (f32[1024,512]{1,0:T(8,128)}, f32[1024,512]{1,0:T(8,128)}, bf16[1024,512]{1,0:T(8,128)(2,1)}, bf16[1024,256]{1,0:T(8,128)(2,1)}, bf16[1024,256]{1,0:T(8,128)(2,1)}) custom-call(s32[1]{0:T(128)} %bitcast.share_ref, s32[1]{0:T(128)} %copy.63.length_ref, f32[1024,1024]{1,0:T(8,128)} %fusion.70.query_ref.key_ref.value_ref, ...), custom_call_target="tpu_custom_call" | custom-call | flops 1024 | bytes 1024 | tf_op jit(solution)/shard_map/attend_forward/pallas_call | solution.py:332
  187.9 20.8 %collective-permute-done.10 = bf16[256,2048]{1,0:T(8,128)(2,1)} collective-permute-done((bf16[256,2048]{1,0:T(8,128)(2,1)}, bf16[256,2048]{1,0:T(8,128)(2,1)}, u32[]{:S(2)}, u32[]{:S(2)}) %collective-permute-start.10) | collective-permute-done | bytes 1048608 | tf_op jit(solution)/shard_map/ppermute | solution.py:18
  212.1 23.9 %collective-permute-done.11 = bf16[256,2048]{1,0:T(8,128)(2,1)} collective-permute-done((bf16[256,2048]{1,0:T(8,128)(2,1)S(1)}, bf16[256,2048]{1,0:T(8,128)(2,1)}, u32[]{:S(2)}, u32[]{:S(2)}) %collective-permute-start.11) | collective-permute-done | bytes 1048608 | tf_op jit(solution)/shard_map/ppermute | solution.py:18
  239.6 15.4 %collective-permute-done.14 = bf16[1024,1536]{1,0:T(8,128)(2,1)} collective-permute-done((bf16[1024,1536]{1,0:T(8,128)(2,1)}, bf16[1024,1536]{1,0:T(8,128)(2,1)}, u32[]{:S(2)}, u32[]{:S(2)}) %collective-permute-start.14) | collective-permute-done | bytes 3145760 | tf_op jit(solution)/shard_map/ppermute | solution.py:18
  272.3 48.9 %collective-permute-done.15 = bf16[1024,1536]{1,0:T(8,128)(2,1)S(1)} collective-permute-done((bf16[1024,1536]{1,0:T(8,128)(2,1)}, bf16[1024,1536]{1,0:T(8,128)(2,1)S(1)}, u32[]{:S(2)}, u32[]{:S(2)}) %collective-permute-start.15) | collective-permute-done | bytes 3145760 | tf_op jit(solution)/shard_map/ppermute | solution.py:18
  328.4 11.0 %convolution_convert_fusion = bf16[2048,1536]{1,0:T(8,128)(2,1)} fusion(bf16[1024,2048]{1,0:T(8,128)(2,1)} %constant_dynamic-update-slice_fusion.2, bf16[1024,1536]{1,0:T(8,128)(2,1)S(1)} %get-tuple-element.64), kind=kOutput, calls=%fused_computation | convolution fusion | flops 6445596672 | bytes 13631488 | tf_op jit(solution)/shard_map/dot_general | solution.py:125
  348.9 14.6 %multiply_convert_fusion = (bf16[1024,1536]{1,0:T(8,128)(2,1)S(1)}, bf16[1024,1536]{1,0:T(8,128)(2,1)S(1)}) fusion(f32[1024,1536]{1,0:T(8,128)} %copy-done.60, f32[1024,1536]{1,0:T(8,128)} %get-tuple-element.149, bf16[1024,2048]{1,0:T(8,128)(2,1)} %constant_dynamic-update-slice_fusion.2, bf16[2048,1536]{0,1:T(8,128)(2,1)} %all-gather.14.cloned.1.call-done), kind=kOutput, calls=%fused_computation.3 | convolution fusion | flops 6462898176 | bytes 29360128 | tf_op jit(solution)/shard_map/dot_general | solution.py:121
  375.6 6.9 add_convert_fusion.6
  382.9 8.9 %fusion.45 = f32[512,2048]{1,0:T(8,128)} fusion(bf16[2048,1536]{1,0:T(8,128)(2,1)} %constant_dynamic-update-slice_fusion.10, bf16[1024,1536]{1,0:T(8,128)(2,1)} %copy-done.56), kind=kOutput, calls=%fused_computation.98 | convolution fusion | flops 3221225472 | bytes 12058624 | tf_op jit(solution)/shard_map/dot_general | solution.py:131
  402.2 36.7 %collective-permute-done.18 = bf16[1024,1536]{1,0:T(8,128)(2,1)} collective-permute-done((bf16[1024,1536]{1,0:T(8,128)(2,1)}, bf16[1024,1536]{1,0:T(8,128)(2,1)}, u32[]{:S(2)}, u32[]{:S(2)}) %collective-permute-start.18) | collective-permute-done | bytes 3145760 | tf_op jit(solution)/shard_map/ppermute | solution.py:18
  445.3 7.8 %convolution_convert_fusion.3 = bf16[1024,1536]{1,0:T(8,128)(2,1)} fusion(bf16[1024,1536]{1,0:T(8,128)(2,1)} %copy-done.56, bf16[1024,2048]{1,0:T(8,128)(2,1)} %copy-done.14), kind=kOutput, calls=%fused_computation.20 | convolution fusion | flops 3222798336 | bytes 8388608 | tf_op jit(solution)/shard_map/dot_general | solution.py:125
  470.9 12.1 %collective-permute-done.19 = bf16[256,2048]{1,0:T(8,128)(2,1)S(1)} collective-permute-done((bf16[256,2048]{1,0:T(8,128)(2,1)S(1)}, bf16[256,2048]{1,0:T(8,128)(2,1)S(1)}, u32[]{:S(2)}, u32[]{:S(2)}) %collective-permute-start.19) | collective-permute-done | bytes 1048608 | tf_op jit(solution)/shard_map/ppermute | solution.py:18
  490.5 23.6 %attend_backward.1 = (bf16[1024,1024]{1,0:T(8,128)(2,1)}, f32[8,128]{1,0:T(8,128)}) custom-call(s32[1]{0:T(128)} %bitcast.share_ref, s32[1]{0:T(128)} %copy.63.length_ref, bf16[1024,512]{1,0:T(8,128)(2,1)} %get-tuple-element.67.grad_ref, f32[1024,1024]{1,0:T(8,128)} %fusion.70.query_ref.key_ref.value_ref, f32[1024,1024]{1,0:T(8,128)} %fusion.70.query_ref.key_ref.value_ref, ...), custom_call_target="tpu_custom_call" | custom-call | flops 1024 | bytes 1024 | tf_op jit(solution)/shard_map/attend_backward/pallas_call | solution.py:359
  514.1 8.6 %collective-permute-done.24 = bf16[1024,1536]{1,0:T(8,128)(2,1)} collective-permute-done((bf16[1024,1536]{1,0:T(8,128)(2,1)}, bf16[1024,1536]{1,0:T(8,128)(2,1)}, u32[]{:S(2)}, u32[]{:S(2)}) %collective-permute-start.24) | collective-permute-done | bytes 3145760 | tf_op jit(solution)/shard_map/ppermute | solution.py:18
  522.7 8.6 %add_convert_fusion = bf16[1024,1536]{1,0:T(8,128)(2,1)} fusion(bf16[1024,1536]{1,0:T(8,128)(2,1)} %collective-permute-done.24, bf16[1024,1536]{1,0:T(8,128)(2,1)} %copy-done.56, bf16[1024,2048]{1,0:T(8,128)(2,1)} %copy-done.14), kind=kOutput, calls=%fused_computation.1 | convolution fusion | flops 3229089792 | bytes 11534336 | tf_op jit(solution)/shard_map/dot_general | solution.py:125
  574.7 22.6 %collective-permute-done.27 = bf16[1024,1024]{0,1:T(8,128)(2,1)S(1)} collective-permute-done((bf16[1024,1024]{0,1:T(8,128)(2,1)S(1)}, bf16[1024,1024]{0,1:T(8,128)(2,1)S(1)}, u32[]{:S(2)}, u32[]{:S(2)}) %collective-permute-start.27) | collective-permute-done | bytes 2097184 | tf_op jit(solution)/shard_map/ppermute | solution.py:18
  622.4 8.5 %collective-permute-done.26 = bf16[256,2048]{1,0:T(8,128)(2,1)S(1)} collective-permute-done((bf16[256,2048]{1,0:T(8,128)(2,1)}, bf16[256,2048]{1,0:T(8,128)(2,1)S(1)}, u32[]{:S(2)}, u32[]{:S(2)}) %collective-permute-start.26) | collective-permute-done | bytes 1048608 | tf_op jit(solution)/shard_map/ppermute | solution.py:18
  656.4 9.1 %collective-permute-done.30 = f32[4352]{0:T(1024)S(1)} collective-permute-done((f32[4352]{0:T(1024)S(1)}, f32[4352]{0:T(1024)S(1)}, u32[]{:S(2)}, u32[]{:S(2)}) %collective-permute-start.30) | collective-permute-done | bytes 17440 | tf_op jit(solution)/shard_map/ppermute | solution.py:18
  683.0 8.3 %reduce-scatter.12.cloned.1.call-done = bf16[256,1024]{1,0:T(8,128)(2,1)} async-done(((bf16[1024,1024]{1,0:T(8,128)(2,1)}), bf16[256,1024]{1,0:T(8,128)(2,1)}) %reduce-scatter.12.cloned.1.call-update) | async-done | bytes 524304 | tf_op jit(solution)/shard_map/reduce_scatter | solution.py:37
  (345 shorter events, 293.2 us)
Async XLA Ops:
  7.2 51.6 %all-gather.6.cloned.1.call-start = ((), (), s32[]{:S(2)}) async-start(), calls=%async_computation.5 | async-start | bytes 2621440 | tf_op jit(solution)/shard_map/all_gather | solution.py:26
  9.3 96.6 %all-gather.8.cloned.1.call-start = ((), (), s32[]{:S(2)}) async-start(), calls=%async_computation.6 | async-start | bytes 2621440 | tf_op jit(solution)/shard_map/all_gather | solution.py:26
  12.3 165.8 %all-gather.10.cloned.1.call-start = ((), (), s32[]{:S(2)}) async-start(), calls=%async_computation.7 | async-start | bytes 3932160 | tf_op jit(solution)/shard_map/all_gather | solution.py:26
  58.9 177.2 %all-gather.12.cloned.1.call-start = ((), (), s32[]{:S(2)}) async-start(), calls=%async_computation.8 | async-start | bytes 3932160 | tf_op jit(solution)/shard_map/all_gather | solution.py:26
  65.9 53.4 %collective-permute-start.1 = (bf16[256,2048]{1,0:T(8,128)(2,1)}, bf16[256,2048]{1,0:T(8,128)(2,1)}, u32[]{:S(2)}, u32[]{:S(2)}) collective-permute-start(bf16[256,2048]{1,0:T(8,128)(2,1)} %fusion.5), channel_id=1, source_target_pairs={{0,1},{1,0},{2,3},{3,2},{4,5},{5,4},{6,7},{7,6},{8,9},{9,8},{10,11... | collective-permute-start | bytes 3145736 | tf_op jit(solution)/shard_map/ppermute | solution.py:18
  66.6 48.8 %collective-permute-start.3 = (bf16[1024,1024]{1,0:T(8,128)(2,1)}, bf16[1024,1024]{1,0:T(8,128)(2,1)}, u32[]{:S(2)}, u32[]{:S(2)}) collective-permute-start(bf16[1024,1024]{1,0:T(8,128)(2,1)} %all-gather.6.cloned.1.call-done), channel_id=1, source_target_pairs={{0,4},{4,0},{8,12},{12,8},{16,20},{20,16},{24,28},{28,24},{1,5},{5... | collective-permute-start | bytes 6291464 | tf_op jit(solution)/shard_map/ppermute | solution.py:18
  106.0 54.0 %collective-permute-start.7 = (bf16[1024,1024]{0,1:T(8,128)(2,1)}, bf16[1024,1024]{0,1:T(8,128)(2,1)}, u32[]{:S(2)}, u32[]{:S(2)}) collective-permute-start(bf16[1024,1024]{0,1:T(8,128)(2,1)} %all-gather.8.cloned.1.call-done), channel_id=1, source_target_pairs={{0,4},{4,0},{8,12},{12,8},{16,20},{20,16},{24,28},{28,24},{1,5},{5... | collective-permute-start | bytes 6291464 | tf_op jit(solution)/shard_map/ppermute | solution.py:18
  123.1 225.9 %all-gather.14.cloned.1.call-start = ((), (), s32[]{:S(2)}) async-start(), calls=%async_computation.9 | async-start | bytes 7864320 | tf_op jit(solution)/shard_map/all_gather | solution.py:26
  123.6 40.3 %collective-permute-start.5 = (bf16[256,2048]{1,0:T(8,128)(2,1)S(1)}, bf16[256,2048]{1,0:T(8,128)(2,1)}, u32[]{:S(2)}, u32[]{:S(2)}) collective-permute-start(bf16[256,2048]{1,0:T(8,128)(2,1)S(1)} %select_convert_fusion), channel_id=1, source_target_pairs={{0,1},{1,0},{2,3},{3,2},{4,5},{5,4},{6,7},{7,6},{8,9},{9,8},{10,11... | collective-permute-start | bytes 3145736 | tf_op jit(solution)/shard_map/ppermute | solution.py:18
  183.7 71.3 %collective-permute-start.14 = (bf16[1024,1536]{1,0:T(8,128)(2,1)}, bf16[1024,1536]{1,0:T(8,128)(2,1)}, u32[]{:S(2)}, u32[]{:S(2)}) collective-permute-start(bf16[1024,1536]{1,0:T(8,128)(2,1)} %all-gather.10.cloned.1.call-done), channel_id=1, source_target_pairs={{0,4},{4,0},{8,12},{12,8},{16,20},{20,16},{24,28},{28,24},{1,5},{5... | collective-permute-start | bytes 9437192 | tf_op jit(solution)/shard_map/ppermute | solution.py:18
  187.8 302.6 %reduce-scatter.6.cloned.1.call-start = ((), (), s32[]{:S(2)}) async-start(), calls=%async_computation.10 | async-start | bytes 7864320 | tf_op jit(solution)/shard_map/reduce_scatter | solution.py:37
  212.1 45.0 %collective-permute-start.12 = (bf16[256,2048]{1,0:T(8,128)(2,1)S(1)}, bf16[256,2048]{1,0:T(8,128)(2,1)}, u32[]{:S(2)}, u32[]{:S(2)}) collective-permute-start(bf16[256,2048]{1,0:T(8,128)(2,1)S(1)} %multiply_convert_fusion.6), channel_id=1, source_target_pairs={{0,1},{1,0},{2,3},{3,2},{4,5},{5,4},{6,7},{7,6},{8,9},{9,8},{10,11... | collective-permute-start | bytes 3145736 | tf_op jit(solution)/shard_map/ppermute | solution.py:18
  236.0 85.1 %collective-permute-start.15 = (bf16[1024,1536]{1,0:T(8,128)(2,1)}, bf16[1024,1536]{1,0:T(8,128)(2,1)S(1)}, u32[]{:S(2)}, u32[]{:S(2)}) collective-permute-start(bf16[1024,1536]{1,0:T(8,128)(2,1)} %all-gather.12.cloned.1.call-done), channel_id=1, source_target_pairs={{0,4},{4,0},{8,12},{12,8},{16,20},{20,16},{24,28},{28,24},{1,5},{5... | collective-permute-start | bytes 9437192 | tf_op jit(solution)/shard_map/ppermute | solution.py:18
  339.5 257.8 %reduce-scatter.8.cloned.1.call-start = ((), (), s32[]{:S(2)}) async-start(), calls=%async_computation.11 | async-start | bytes 3932160 | tf_op jit(solution)/shard_map/reduce_scatter | solution.py:37
  368.5 70.4 %collective-permute-start.18 = (bf16[1024,1536]{1,0:T(8,128)(2,1)}, bf16[1024,1536]{1,0:T(8,128)(2,1)}, u32[]{:S(2)}, u32[]{:S(2)}) collective-permute-start(bf16[1024,1536]{1,0:T(8,128)(2,1)} %convolution_convert_fusion.4), channel_id=1, source_target_pairs={{0,4},{4,0},{8,12},{12,8},{16,20},{20,16},{24,28},{28,24},{1,5},{5... | collective-permute-start | bytes 9437192 | tf_op jit(solution)/shard_map/ppermute | solution.py:18
  400.8 53.8 %collective-permute-start.17 = (bf16[256,2048]{1,0:T(8,128)(2,1)}, bf16[256,2048]{1,0:T(8,128)(2,1)}, u32[]{:S(2)}, u32[]{:S(2)}) collective-permute-start(bf16[256,2048]{1,0:T(8,128)(2,1)} %add_convert_fusion.10), channel_id=1, source_target_pairs={{0,2},{1,3},{2,0},{3,1},{4,6},{5,7},{6,4},{7,5},{8,10},{9,11},{10,... | collective-permute-start | bytes 3145736 | tf_op jit(solution)/shard_map/ppermute | solution.py:18
  445.2 196.3 %reduce-scatter.10.cloned.1.call-start = ((), (), s32[]{:S(2)}) async-start(), calls=%async_computation.12 | async-start | bytes 3932160 | tf_op jit(solution)/shard_map/reduce_scatter | solution.py:37
  453.1 69.5 %collective-permute-start.24 = (bf16[1024,1536]{1,0:T(8,128)(2,1)}, bf16[1024,1536]{1,0:T(8,128)(2,1)}, u32[]{:S(2)}, u32[]{:S(2)}) collective-permute-start(bf16[1024,1536]{1,0:T(8,128)(2,1)} %convolution_convert_fusion.3), channel_id=1, source_target_pairs={{0,4},{4,0},{8,12},{12,8},{16,20},{20,16},{24,28},{28,24},{1,5},{5... | collective-permute-start | bytes 9437192 | tf_op jit(solution)/shard_map/ppermute | solution.py:18
  531.3 146.5 %reduce-scatter.14.cloned.1.call-start = ((), (), s32[]{:S(2)}) async-start(), calls=%async_computation.14 | async-start | bytes 2621440 | tf_op jit(solution)/shard_map/reduce_scatter | solution.py:37
  548.6 48.6 %collective-permute-start.27 = (bf16[1024,1024]{0,1:T(8,128)(2,1)S(1)}, bf16[1024,1024]{0,1:T(8,128)(2,1)S(1)}, u32[]{:S(2)}, u32[]{:S(2)}) collective-permute-start(bf16[1024,1024]{0,1:T(8,128)(2,1)S(1)} %pad_maximum_fusion.6), channel_id=1, source_target_pairs={{0,4},{4,0},{8,12},{12,8},{16,20},{20,16},{24,28},{28,24},{1,5},{5... | collective-permute-start | bytes 6291464 | tf_op jit(solution)/shard_map/ppermute | solution.py:18
  563.5 42.6 %collective-permute-start.25 = (bf16[512,2048]{1,0:T(8,128)(2,1)}, bf16[512,2048]{1,0:T(8,128)(2,1)}, u32[]{:S(2)}, u32[]{:S(2)}) collective-permute-start(bf16[512,2048]{1,0:T(8,128)(2,1)} %add_convert_fusion.4), channel_id=1, source_target_pairs={{0,1},{1,0},{2,3},{3,2},{4,5},{5,4},{6,7},{7,6},{8,9},{9,8},{10,11... | collective-permute-start | bytes 6291464 | tf_op jit(solution)/shard_map/ppermute | solution.py:18
  565.2 36.0 %collective-permute-start.23 = (bf16[256,2048]{1,0:T(8,128)(2,1)}, bf16[256,2048]{1,0:T(8,128)(2,1)S(1)}, u32[]{:S(2)}, u32[]{:S(2)}) collective-permute-start(bf16[256,2048]{1,0:T(8,128)(2,1)} %add_convert_fusion.9), channel_id=1, source_target_pairs={{0,2},{1,3},{2,0},{3,1},{4,6},{5,7},{6,4},{7,5},{8,10},{9,11},{10,... | collective-permute-start | bytes 3145736 | tf_op jit(solution)/shard_map/ppermute | solution.py:18
  566.7 74.9 %collective-permute-start.33 = (bf16[1024,1024]{1,0:T(8,128)(2,1)}, bf16[1024,1024]{1,0:T(8,128)(2,1)}, u32[]{:S(2)}, u32[]{:S(2)}) collective-permute-start(bf16[1024,1024]{1,0:T(8,128)(2,1)} %convolution_convert_fusion.9), channel_id=1, source_target_pairs={{0,4},{4,0},{8,12},{12,8},{16,20},{20,16},{24,28},{28,24},{1,5},{5... | collective-permute-start | bytes 6291464 | tf_op jit(solution)/shard_map/ppermute | solution.py:18
  601.1 90.2 %reduce-scatter.12.cloned.1.call-start = ((), (), s32[]{:S(2)}) async-start(), calls=%async_computation.13 | async-start | bytes 2621440 | tf_op jit(solution)/shard_map/reduce_scatter | solution.py:37
  (86 other events, 1291.9 us)
Sparse Core Ops, SparseCore 0:
  10.2 48.6 all-gather.5
  61.0 44.9 all-gather.7
  107.5 61.7 all-gather.9
  170.7 62.1 all-gather.11
  234.9 113.9 all-gather.13
  351.1 108.9 reduce-scatter.5
  462.4 60.7 reduce-scatter.7
  531.4 58.4 reduce-scatter.9
  601.3 42.0 reduce-scatter.13
  648.4 42.8 reduce-scatter.11

commit v4 on v2

v4 whole, which is shorter than its diff:
```python
import functools

import jax
import jax.numpy as jnp
from jax import lax
from jax.experimental import pallas as pl
from jax.experimental.pallas import tpu as pltpu
from jax.sharding import PartitionSpec as P

NORM_EPSILON = 1e-06
ROPE_THETA = 1000000.0
MASKED_LOGIT = -1e30
F32 = jnp.float32
BF16 = jnp.bfloat16


def exchange(values, axis, size, mask):
    return lax.ppermute(values, axis, [(i, i ^ mask) for i in range(size)])


def lines(count):
    return [list(range(0, count, 2)), list(range(1, count, 2))]


def to_partner(values, count):
    return exchange(values, "fsdp", count, 1)


def halves(values, odd):
    width = values.shape[-1] // 2
    left, right = values[..., :width], values[..., width:]
    return jnp.where(odd, right, left), jnp.where(odd, left, right)


def in_order(own, other, odd, axis):
    first, second = jnp.where(odd, other, own), jnp.where(odd, own, other)
    return jnp.concatenate([first, second], axis=axis)


def pair_rows(shards, odd, count, *before):
    split = [halves(shard, odd) for shard in shards]
    own = jnp.concatenate([piece[0] for piece in split], axis=1)
    other = jnp.concatenate([piece[1] for piece in split], axis=1)
    arrived = to_partner(other, count)
    if before:
        arrived = hold(arrived, *before)
    return in_order(own, arrived, odd, 0)


def gather_line(rows, count):
    return lax.all_gather(rows, "fsdp", axis=0, tiled=True, axis_index_groups=lines(count))


def scatter_line(total, count):
    return lax.psum_scatter(
        total, "fsdp", scatter_dimension=0, tiled=True, axis_index_groups=lines(count)
    )


def swap_rows(rows, odd, count):
    height = rows.shape[0] // 2
    top, bottom = rows[:height], rows[height:]
    return jnp.where(odd, bottom, top), to_partner(jnp.where(odd, top, bottom), count)


def own_shard(own, other, odd, widths):
    shards, start = [], 0
    for width in widths:
        piece = slice(start, start + width)
        shards.append(in_order(own[:, piece], other[:, piece], odd, 1).astype(F32))
        start += width
    return shards


def hold(value, *others):
    return lax.optimization_barrier((value,) + others)[0]


def row_masks(count):
    half = count // 2
    return [((p % half) << 1) | (p // half) for p in range(count)]


def across(values, count):
    return exchange(values, "tensor", count, 2)


def core(values, count):
    return exchange(values, "tensor", count, 1)


def rows_in(values, members, shares, *before):
    half = values.shape[0] // 2
    side = across(values, shares)
    partner = to_partner(values, members)
    if before and before[0] is not None:
        side, partner = hold((side, partner), before[0])
    upper = to_partner(side[:half], members)
    lower = across(partner[half:], shares)
    if before[1:]:
        upper, lower = hold((upper, lower), *before[1:])
    near = [values, side, partner, upper, lower]
    return stack_rows(near + [core(piece, shares) for piece in near])


def stack_kernel(count, *refs):
    pieces, out, held, in_sems, out_sems = refs[:count], *refs[count:]
    incoming, outgoing, start = [], [], 0
    for i, piece in enumerate(pieces):
        place = pl.ds(start, piece.shape[0])
        incoming.append(pltpu.make_async_copy(piece, held.at[place], in_sems.at[i]))
        outgoing.append(pltpu.make_async_copy(held.at[place], out.at[place], out_sems.at[i]))
        incoming[-1].start()
        start += piece.shape[0]
    for arrive, leave in zip(incoming, outgoing):
        arrive.wait()
        leave.start()
    for leave in outgoing:
        leave.wait()


def stack_rows(pieces):
    count, (_, width), kind = len(pieces), pieces[0].shape, pieces[0].dtype
    rows = sum(piece.shape[0] for piece in pieces)
    anywhere = pl.BlockSpec(memory_space=pl.ANY)
    return pl.pallas_call(
        functools.partial(stack_kernel, count),
        in_specs=[anywhere] * count,
        out_specs=anywhere,
        out_shape=jax.ShapeDtypeStruct((rows, width), kind),
        scratch_shapes=[
            pltpu.VMEM((rows, width), kind),
            pltpu.SemaphoreType.DMA((count,)),
            pltpu.SemaphoreType.DMA((count,)),
        ],
        compiler_params=pltpu.CompilerParams(vmem_limit_bytes=(rows * width * 2) + (1 << 20)),
        cost_estimate=light_cost(),
        name="stack_rows",
    )(*pieces)


def light_cost():
    return pl.CostEstimate(flops=1024, bytes_accessed=1024, transcendentals=0)


def corner_kernel(near_ref, arrived_ref, upper_ref, lower_ref):
    half = upper_ref.shape[0]
    total = (near_ref[...].astype(F32) + arrived_ref[...].astype(F32)).astype(BF16)
    upper_ref[...] = total[:half]
    lower_ref[...] = total[half:]


def add_corner(near, arrived):
    rows, width = arrived.shape
    tile = width // 2
    half = pl.BlockSpec((rows // 2, tile), lambda i: (0, i))
    return pl.pallas_call(
        corner_kernel,
        grid=(2,),
        in_specs=[
            pl.BlockSpec((rows, tile), lambda i: (3, i)),
            pl.BlockSpec((rows, tile), lambda i: (0, i)),
        ],
        out_specs=[half, half],
        out_shape=[jax.ShapeDtypeStruct((rows // 2, width), BF16)] * 2,
        compiler_params=pltpu.CompilerParams(vmem_limit_bytes=16 << 20),
        cost_estimate=light_cost(),
        name="add_corner",
    )(near, arrived)


def main_kernel(near_ref, arrived_ref, own_ref, side_a, side_b, partner_a, partner_b):
    rows = own_ref.shape[0]
    half = rows // 2

    def total(start, size):
        piece = pl.ds(start, size)
        return near_ref[piece, :].astype(F32) + arrived_ref[piece, :].astype(F32)

    own_ref[...] = total(0, rows)
    side_a[...] = total(rows, half).astype(BF16)
    side_b[...] = total(rows + half, half)
    partner_a[...] = total(2 * rows, half)
    partner_b[...] = total(2 * rows + half, half).astype(BF16)


def add_main(near, arrived):
    rows, width = arrived.shape[0] // 3, arrived.shape[1]
    tile = width // 4
    whole = pl.BlockSpec((rows, tile), lambda i: (0, i))
    half = pl.BlockSpec((rows // 2, tile), lambda i: (0, i))
    three = pl.BlockSpec((3 * rows, tile), lambda i: (0, i))

    def shape(kind):
        return jax.ShapeDtypeStruct((rows // 2, width), kind)

    return pl.pallas_call(
        main_kernel,
        grid=(4,),
        in_specs=[three, three],
        out_specs=[whole, half, half, half, half],
        out_shape=[
            jax.ShapeDtypeStruct((rows, width), F32),
            shape(BF16),
            shape(F32),
            shape(F32),
            shape(BF16),
        ],
        compiler_params=pltpu.CompilerParams(vmem_limit_bytes=24 << 20),
        cost_estimate=light_cost(),
        name="add_main",
    )(near, arrived)


def open_sum(parts, members, shares, *before):
    near, far, far_corner = parts
    arrived_corner, arrived = core(far_corner, shares), core(far, shares)
    if before:
        arrived_corner, arrived = hold((arrived_corner, arrived), *before)
    upper, lower = add_corner(near, arrived_corner)
    corners = across(upper, shares), to_partner(lower, members)
    own, side_a, side_b, partner_a, partner_b = add_main(near, arrived)
    return corners, (own, side_b, partner_a, across(side_a, shares), to_partner(partner_b, members))


def close_sum(corners, opened, members, shares, *before):
    corner_side, corner_partner = corners
    own, side, partner, side_first, partner_first = opened
    side_second = across((side + corner_partner.astype(F32)).astype(BF16), shares)
    partner_second = to_partner((partner + corner_side.astype(F32)).astype(BF16), members)
    if before:
        side_second, partner_second = hold((side_second, partner_second), *before)
    from_side = jnp.concatenate([side_first, side_second], axis=0).astype(F32)
    from_partner = jnp.concatenate([partner_second, partner_first], axis=0).astype(F32)
    return own + from_side + from_partner


def sum_everywhere(values, axes):
    for axis, count in axes:
        mask = 1
        while mask < count:
            values = values + exchange(values, axis, count, mask)
            mask <<= 1
    return values


def matmul(first_op, second_op):
    return jnp.dot(first_op, second_op, preferred_element_type=F32)


def matmul_tn(first_op, second_op):
    return lax.dot_general(
        first_op, second_op, (((0,), (0,)), ((), ())), preferred_element_type=F32
    )


def matmul_nt(first_op, second_op):
    return lax.dot_general(
        first_op, second_op, (((1,), (1,)), ((), ())), preferred_element_type=F32
    )


def normalize(values):
    inv_root = lax.rsqrt(jnp.mean(values * values, axis=-1, keepdims=True) + NORM_EPSILON)
    return (values * inv_root, inv_root)


def norm_back(gradient, unit_rows, inv_root, gain_vec):
    scaled = gradient * gain_vec
    return inv_root * (scaled - unit_rows * jnp.mean(scaled * unit_rows, axis=-1, keepdims=True))


def rope_tables(slot_count, head_size):
    half_width = head_size // 2
    inverse = ROPE_THETA ** (-(jnp.arange(half_width, dtype=F32) * 2.0 / head_size))
    angles = jnp.arange(slot_count, dtype=F32)[:, None] * inverse[None, :]
    cosine = jnp.concatenate([jnp.cos(angles), jnp.cos(angles)], axis=-1)
    signed_sine = jnp.concatenate([-jnp.sin(angles), jnp.sin(angles)], axis=-1)
    return (cosine, signed_sine)


def piece_of(mask, rows):
    return mask & 1, pl.ds(pl.multiple_of((mask >> 1) * rows, rows), rows)


def allowed_block(block, rows, width, length):
    row_slot = block * rows + lax.broadcasted_iota(jnp.int32, (rows, width), 0)
    col_slot = lax.broadcasted_iota(jnp.int32, (rows, width), 1)
    return (col_slot <= row_slot) & (col_slot < length)


def turn(unit_rows, gain_vec, cosine, signed_sine):
    normed = unit_rows * gain_vec
    half = normed.shape[-1] // 2
    return normed * cosine + pltpu.roll(normed, half, 1) * signed_sine


def turn_back(gradient, cosine, signed_sine):
    half = gradient.shape[-1] // 2
    return gradient * cosine - pltpu.roll(gradient, half, 1) * signed_sine


def attend_forward_kernel(
    masks,
    head_size,
    score_scale,
    share_ref,
    length_ref,
    query_ref,
    key_ref,
    value_ref,
    query_gain_ref,
    key_gain_ref,
    cosine_ref,
    sine_ref,
    attended_ref,
    log_ref,
    query_rot_ref,
    key_rot_ref,
    value_low_ref,
):
    blocks = len(masks)
    rows = 2 * query_ref.shape[1] // blocks
    group = query_ref.shape[2] // head_size
    share, length = share_ref[0], length_ref[pl.program_id(0)]
    for mask in masks:
        side, here = mask & 1, pl.ds((mask >> 1) * rows, rows)
        there = pl.ds(pl.multiple_of((share ^ mask) * rows, rows), rows)
        cosine, signed_sine = cosine_ref[there, :], sine_ref[there, :]
        for head in range(group):
            cols = pl.ds(head * head_size, head_size)
            unit_rows, _ = normalize(query_ref[side, here, cols])
            turned = turn(unit_rows, query_gain_ref[...], cosine, signed_sine)
            query_rot_ref[there, cols] = turned.astype(BF16)
        unit_rows, _ = normalize(key_ref[side, here, :])
        turned = turn(unit_rows, key_gain_ref[...], cosine, signed_sine)
        key_rot_ref[there, :] = turned.astype(BF16)
        value_low_ref[there, :] = value_ref[side, here, :].astype(BF16)

    for block in range(blocks):
        width = (block + 1) * rows
        here = pl.ds(block * rows, rows)
        allowed = allowed_block(block, rows, width, length)
        side, back = piece_of(share ^ block, rows)

        def one_head(head, carry, width=width, here=here, allowed=allowed, side=side, back=back):
            cols = pl.ds(pl.multiple_of(head * head_size, head_size), head_size)
            scores = matmul_nt(query_rot_ref[here, cols], key_rot_ref[:width, :])
            logits = jnp.where(allowed, scores * score_scale, MASKED_LOGIT)
            highest = jnp.max(logits, axis=-1, keepdims=True)
            weights_raw = jnp.exp(logits - highest)
            row_total = jnp.sum(weights_raw, axis=-1, keepdims=True)
            probabilities = (weights_raw * (1.0 / row_total)).astype(BF16)
            attended_ref[side, back, cols] = matmul(probabilities, value_low_ref[:width, :])
            log_ref[here, cols] = jnp.broadcast_to(highest + jnp.log(row_total), (rows, head_size))
            return carry

        lax.fori_loop(0, group, one_head, 0)


def attend_backward_kernel(
    masks,
    head_size,
    score_scale,
    share_ref,
    length_ref,
    grad_ref,
    gate_grad_ref,
    query_ref,
    key_ref,
    query_rot_ref,
    key_rot_ref,
    value_low_ref,
    log_ref,
    query_gain_ref,
    key_gain_ref,
    cosine_ref,
    sine_ref,
    send_ref,
    gain_ref,
    query_grad_ref,
    key_grad_ref,
    value_grad_ref,
):
    blocks = len(masks)
    rows = 2 * query_ref.shape[1] // blocks
    group = query_ref.shape[2] // head_size
    kv_heads = pl.num_programs(1)
    kv_head = pl.program_id(1)
    share, length = share_ref[0], length_ref[pl.program_id(0)]
    key_grad_ref[...] = jnp.zeros_like(key_grad_ref)
    value_grad_ref[...] = jnp.zeros_like(value_grad_ref)

    @pl.when((pl.program_id(0) == 0) & (kv_head == 0))
    def _():
        gain_ref[...] = jnp.zeros_like(gain_ref)

    for block in range(blocks):
        width = (block + 1) * rows
        here = pl.ds(block * rows, rows)
        allowed = allowed_block(block, rows, width, length)
        side, back = piece_of(share ^ block, rows)

        def one_head(head, carry, width=width, here=here, allowed=allowed, side=side, back=back):
            cols = pl.ds(pl.multiple_of(head * head_size, head_size), head_size)
            queries, grads = query_rot_ref[here, cols], grad_ref[side, back, cols]
            scores = matmul_nt(queries, key_rot_ref[:width, :])
            logits = jnp.where(allowed, scores * score_scale, MASKED_LOGIT)
            soft = jnp.where(allowed, jnp.exp(logits - log_ref[here, cols][:, :1]), 0.0)
            prob_grad = matmul_nt(grads, value_low_ref[:width, :])
            centre = jnp.sum(soft * prob_grad, axis=-1, keepdims=True)
            score_grad = (score_scale * soft * (prob_grad - centre)).astype(BF16)
            query_grad_ref[here, cols] = matmul(score_grad, key_rot_ref[:width, :])
            key_grad_ref[:width, :] += matmul_tn(score_grad, queries)
            value_grad_ref[:width, :] += matmul_tn(soft.astype(BF16), grads)
            return carry

        lax.fori_loop(0, group, one_head, 0)

    key_base, value_base = kv_heads * group * head_size, kv_heads * (group + 1) * head_size
    gate_base = kv_heads * (group + 2) * head_size
    for mask in masks:
        side, here = mask & 1, pl.ds((mask >> 1) * rows, rows)
        there = pl.ds(pl.multiple_of((share ^ mask) * rows, rows), rows)
        cosine, signed_sine = cosine_ref[there, :], sine_ref[there, :]

        def through_norm(gradient, raw, gain_vec):
            normed_grad = turn_back(gradient, cosine, signed_sine)
            unit_rows, inv_root = normalize(raw)
            gain_part = jnp.sum(normed_grad * unit_rows, axis=0, keepdims=True)
            return norm_back(normed_grad, unit_rows, inv_root, gain_vec).astype(BF16), gain_part

        for head in range(group):
            cols = pl.ds(head * head_size, head_size)
            sent, gain_part = through_norm(
                query_grad_ref[there, cols], query_ref[side, here, cols], query_gain_ref[...]
            )
            offset = pl.multiple_of((kv_head * group + head) * head_size, head_size)
            send_ref[side, here, pl.ds(offset, head_size)] = sent
            gain_ref[0:1, :] += gain_part
        sent, gain_part = through_norm(
            key_grad_ref[there, :], key_ref[side, here, :], key_gain_ref[...]
        )
        offset = pl.multiple_of(key_base + kv_head * head_size, head_size)
        send_ref[side, here, pl.ds(offset, head_size)] = sent
        gain_ref[1:2, :] += gain_part
        offset = pl.multiple_of(value_base + kv_head * head_size, head_size)
        send_ref[side, here, pl.ds(offset, head_size)] = value_grad_ref[there, :].astype(BF16)
        offset = pl.multiple_of(gate_base + kv_head * group * head_size, head_size)
        send_ref[side, here, pl.ds(offset, group * head_size)] = gate_grad_ref[side, here, :]


def head_specs(slots, group, kv_heads, head_size):
    half = slots // 2
    wide = group * head_size

    def piece(width, base):
        return pl.BlockSpec((2, None, half, width), lambda s, c: (0, s, 0, base + c))

    def ordered(width):
        return pl.BlockSpec((None, slots, width), lambda s, c: (s, 0, c))

    raw = [piece(wide, 0), piece(head_size, kv_heads * group)]
    value = piece(head_size, kv_heads * (group + 1))
    gain = pl.BlockSpec((1, head_size), lambda s, c: (0, 0))
    table = pl.BlockSpec((slots, head_size), lambda s, c: (0, 0))
    scalar = pl.BlockSpec(memory_space=pltpu.SMEM)
    return raw, value, ordered(wide), ordered(head_size), gain, table, scalar


def attend_forward(qkv_raw, share, lengths, gains, tables, masks, sizes):
    kv_heads, group, head_size = sizes
    slots = qkv_raw.shape[0] // 2
    raw, value, wide, narrow, gain, table, scalar = head_specs(slots, group, kv_heads, head_size)
    split = qkv_raw.reshape(2, 2, slots // 2, qkv_raw.shape[1])
    width, key_width = kv_heads * group * head_size, kv_heads * head_size
    attended, *kept = pl.pallas_call(
        functools.partial(attend_forward_kernel, masks, head_size, head_size ** (-0.5)),
        grid=(2, kv_heads),
        in_specs=[scalar, scalar, *raw, value, gain, gain, table, table],
        out_specs=[raw[0], wide, wide, narrow, narrow],
        out_shape=[
            jax.ShapeDtypeStruct((2, 2, slots // 2, width), F32),
            jax.ShapeDtypeStruct((2, slots, width), F32),
            jax.ShapeDtypeStruct((2, slots, width), BF16),
            jax.ShapeDtypeStruct((2, slots, key_width), BF16),
            jax.ShapeDtypeStruct((2, slots, key_width), BF16),
        ],
        cost_estimate=light_cost(),
        name="attend_forward",
    )(share, lengths, split, split, split, *gains, *tables)
    return attended.reshape(2 * slots, width), kept


def attend_backward(grads, gate_grads, qkv_raw, kept, share, lengths, gains, tables, masks, sizes):
    kv_heads, group, head_size = sizes
    slots = qkv_raw.shape[0] // 2
    raw, value, wide, narrow, gain, table, scalar = head_specs(slots, group, kv_heads, head_size)
    split = qkv_raw.reshape(2, 2, slots // 2, qkv_raw.shape[1])
    log_total, query_rot, key_rot, value_low = kept
    width = qkv_raw.shape[1] + gate_grads.shape[1]
    sent, gain_parts = pl.pallas_call(
        functools.partial(attend_backward_kernel, masks, head_size, head_size ** (-0.5)),
        grid=(2, kv_heads),
        in_specs=[scalar, scalar, raw[0], raw[0], *raw, wide, narrow, narrow, wide]
        + [gain, gain, table, table],
        out_specs=[
            pl.BlockSpec((2, None, slots // 2, width), lambda s, c: (0, s, 0, 0)),
            pl.BlockSpec((8, head_size), lambda s, c: (0, 0)),
        ],
        out_shape=[
            jax.ShapeDtypeStruct((2, 2, slots // 2, width), BF16),
            jax.ShapeDtypeStruct((8, head_size), F32),
        ],
        scratch_shapes=[
            pltpu.VMEM((slots, group * head_size), F32),
            pltpu.VMEM((slots, head_size), F32),
            pltpu.VMEM((slots, head_size), F32),
        ],
        cost_estimate=light_cost(),
        name="attend_backward",
    )(
        share,
        lengths,
        grads.reshape(2, 2, slots // 2, grads.shape[1]),
        gate_grads.reshape(2, 2, slots // 2, grads.shape[1]),
        split,
        split,
        query_rot,
        key_rot,
        value_low,
        log_total,
        *gains,
        *tables,
    )
    return sent.reshape(2 * slots, width), gain_parts


def body(
    members,
    shares,
    hidden_in,
    lengths,
    attn_gain,
    query_weight,
    key_weight,
    value_weight,
    output_gate,
    query_gain,
    key_gain,
    out_weight,
    mlp_gain,
    gate_weight,
    up_weight,
    down_weight,
    cotangent,
):
    odd = lax.axis_index("fsdp") % 2 == 1
    share = lax.axis_index("tensor")
    local_rows = hidden_in.shape[0]
    head_size = query_gain.shape[0]
    query_width = query_weight.shape[1] // 2
    key_width = key_weight.shape[1] // 2
    sizes = (key_width // head_size, query_width // key_width, head_size)
    masks = row_masks(shares)
    slots = share * local_rows + jnp.arange(local_rows)
    valid_rows = (slots < lengths[0]).astype(F32)[:, None]
    share_at = share.astype(jnp.int32)[None]
    both_lengths = jnp.concatenate([lengths, to_partner(lengths, members)])
    gains = (query_gain[None, :], key_gain[None, :])
    half_rows = local_rows * shares

    def gather_rows(values, *before):
        return rows_in(values, members, shares, *before)

    def sum_rows(parts, first, last):
        opened = open_sum(parts, members, shares, *first)
        return close_sum(*opened, members, shares, *last)

    def in_parts(function):
        corner = function(slice(2 * half_rows - local_rows, 2 * half_rows)).astype(BF16)
        far = function(slice(half_rows, 2 * half_rows - local_rows)).astype(BF16)
        near = function(slice(0, half_rows)).astype(BF16)
        return near, far, corner

    qkv_rows = pair_rows([query_weight, key_weight, value_weight], odd, members)
    qkv_full = gather_line(qkv_rows, members)
    gate_out_rows = pair_rows([output_gate, out_weight.T], odd, members)
    gate_out_full = gather_line(hold(gate_out_rows, qkv_rows), members)

    residual = hidden_in.astype(F32)
    unit_one, root_one = normalize(residual)
    gate_rows = pair_rows([hold(gate_weight, gate_out_rows)], odd, members)
    normed_one = gather_rows(hold((unit_one * attn_gain).astype(BF16), gate_rows))
    qkv_raw = matmul(normed_one, qkv_full)
    grad_rows = cotangent.astype(F32) * valid_rows
    tables = rope_tables(half_rows, head_size)
    attended, kept = attend_forward(
        qkv_raw, share_at, both_lengths, gains, tables, masks, sizes
    )
    up_in, down_in = hold((up_weight, down_weight), normed_one)
    up_rows = pair_rows([up_in], odd, members, attended)
    down_rows = pair_rows([down_in.T], odd, members, attended)
    gate_weights = gather_line(hold(gate_rows, qkv_full), members)
    up_weights = gather_line(hold(up_rows, gate_out_full), members)
    down_weights = gather_line(hold(down_rows, gate_weights), members)
    gate_full, out_full = gate_out_full[:, :query_width], gate_out_full[:, query_width:]
    gate_pre = matmul(hold(normed_one, attended, up_rows, down_rows), gate_full)
    gate_sig = jax.nn.sigmoid(gate_pre)
    gated_out = (attended * gate_sig).astype(BF16)
    attn_parts = in_parts(lambda rows: matmul_nt(gated_out[rows], out_full))
    middle = residual + sum_rows(attn_parts, (), ())
    unit_two, root_two = normalize(middle)
    normed_two = gather_rows((unit_two * mlp_gain).astype(BF16))
    one_weights = jnp.concatenate([qkv_full, gate_full], axis=1)
    ffn_gate = matmul(normed_two, gate_weights)
    branch_full = gather_rows(hold(grad_rows.astype(BF16), normed_two), ffn_gate, one_weights)
    ffn_up = matmul(normed_two, up_weights)
    ffn_sig = jax.nn.sigmoid(ffn_gate)
    ffn_act = ffn_gate * ffn_sig
    ffn_mid = (ffn_act * ffn_up).astype(BF16)

    down_part = matmul_tn(branch_full, ffn_mid).astype(BF16)
    down_sum = scatter_line(down_part, members)

    mid_grad = matmul(branch_full, hold(down_weights, down_part))
    gate_grad = (mid_grad * ffn_up * ffn_sig * (1.0 + ffn_gate * (1.0 - ffn_sig))).astype(BF16)
    up_grad = (mid_grad * ffn_act).astype(BF16)
    back_parts = in_parts(
        lambda rows: matmul_nt(gate_grad[rows], gate_weights)
        + matmul_nt(up_grad[rows], up_weights)
    )
    gate_part = matmul_tn(normed_two, hold(gate_grad, back_parts)).astype(BF16)
    gate_sum = scatter_line(gate_part, members)
    up_part = matmul_tn(normed_two, hold(up_grad, gate_part)).astype(BF16)
    up_sum = scatter_line(up_part, members)
    norm_two_grad = sum_rows(back_parts, (gate_part,), (down_sum, up_part))

    mlp_gain_part = jnp.sum(norm_two_grad * unit_two, axis=0)
    middle_grad = grad_rows + norm_back(norm_two_grad, unit_two, root_two, mlp_gain)
    mid_late = hold(ffn_mid, norm_two_grad)
    branch_parts = in_parts(lambda rows: matmul_nt(mid_late[rows], down_weights))
    attn_full_grad = gather_rows(middle_grad.astype(BF16), None, branch_parts, gate_sum)
    down_swap = swap_rows(hold(down_sum, attn_full_grad), odd, members)
    gate_swap = swap_rows(hold(gate_sum, attn_full_grad), odd, members)

    gated_grad = matmul(attn_full_grad, out_full)
    attended_grad = (gated_grad * gate_sig).astype(BF16)
    gate_pre_grad = (gated_grad * attended * gate_sig * (1.0 - gate_sig)).astype(BF16)
    gate_out_part = jnp.concatenate(
        [
            matmul_tn(normed_one, gate_pre_grad).astype(BF16),
            matmul_tn(attn_full_grad, gated_out).astype(BF16),
        ],
        axis=1,
    )
    gate_out_sum = scatter_line(gate_out_part, members)
    corners, opened = open_sum(hold(branch_parts, attn_full_grad), members, shares)
    one_send, gain_parts = attend_backward(
        hold(attended_grad, gate_out_part, down_swap, gate_swap),
        gate_pre_grad,
        qkv_raw,
        kept,
        share_at,
        both_lengths,
        gains,
        tables,
        masks,
        sizes,
    )
    ffn_branch = close_sum(corners, opened, members, shares, one_send)
    output = ((middle + ffn_branch) * valid_rows).astype(BF16)
    units = up_sum.shape[1]
    (down_shard,) = own_shard(*down_swap, odd, (units,))
    (gate_shard,) = own_shard(*gate_swap, odd, (units,))
    one_parts = in_parts(lambda rows: matmul_nt(one_send[rows], one_weights))
    qkv_send = hold(one_send, up_sum, one_parts)[:, : qkv_raw.shape[1]]
    qkv_part = matmul_tn(normed_one, qkv_send).astype(BF16)
    qkv_sum = scatter_line(qkv_part, members)
    norm_one_grad = sum_rows(one_parts, (qkv_part, ffn_branch), (gate_out_sum, output, down_shard, gate_shard))
    attn_gain_part = jnp.sum(norm_one_grad * unit_one, axis=0)
    grad_hidden = middle_grad + norm_back(norm_one_grad, unit_one, root_one, attn_gain)
    gain_totals = sum_everywhere(
        jnp.concatenate([attn_gain_part, mlp_gain_part, gain_parts[0], gain_parts[1]]),
        (("tensor", shares), ("fsdp", members)),
    )
    up_swap = swap_rows(hold(up_sum, norm_one_grad), odd, members)
    gate_out_swap = swap_rows(hold(gate_out_sum, norm_one_grad), odd, members)
    (up_shard,) = own_shard(*up_swap, odd, (units,))
    gate_attn_shard, out_shard = own_shard(*gate_out_swap, odd, (query_width,) * 2)
    qkv_sum = hold(
        qkv_sum,
        norm_one_grad,
        output,
        down_shard,
        gate_shard,
        up_shard,
        gate_attn_shard,
        out_shard,
    )
    query_shard, key_shard, value_shard = own_shard(
        *swap_rows(qkv_sum, odd, members), odd, (query_width, key_width, key_width)
    )
    width = hidden_in.shape[1]
    return (
        output,
        grad_hidden,
        gain_totals[:width],
        query_shard,
        key_shard,
        value_shard,
        gate_attn_shard,
        gain_totals[2 * width : 2 * width + head_size],
        gain_totals[2 * width + head_size :],
        out_shard.T,
        gain_totals[width : 2 * width],
        gate_shard,
        up_shard,
        down_shard.T,
    )


def solution(mesh):
    members, shares = mesh.shape["fsdp"], mesh.shape["tensor"]

    def layer(*operands):
        return body(members, shares, *operands)

    tokens = P(("fsdp", "tensor"), None)
    return jax.shard_map(
        layer,
        mesh=mesh,
        in_specs=(
            tokens,
            P("fsdp"),
            P(),
            P("fsdp", "tensor"),
            P("fsdp", "tensor"),
            P("fsdp", "tensor"),
            P("fsdp", "tensor"),
            P(),
            P(),
            P("tensor", "fsdp"),
            P(),
            P("fsdp", "tensor"),
            P("fsdp", "tensor"),
            P("tensor", "fsdp"),
            tokens,
        ),
        out_specs=(
            tokens,
            tokens,
            P(),
            P("fsdp", "tensor"),
            P("fsdp", "tensor"),
            P("fsdp", "tensor"),
            P("fsdp", "tensor"),
            P(),
            P(),
            P("tensor", "fsdp"),
            P(),
            P("fsdp", "tensor"),
            P("fsdp", "tensor"),
            P("tensor", "fsdp"),
        ),
        check_vma=False,
    )
```

time: 795 us -> 660 us (0.83)
  waiting for transfers between devices: 402 us -> 254 us
  starting transfers between devices: 32.8 us -> 64.7 us
  local copies, waits for them, and re-layouts: 74.4 us -> 44.7 us
  Pallas kernels: 41.7 us -> 67.8 us
  matrix products: 168 us -> 159 us
    ppermute x35 -> x84, waiting for transfers between devices: 323 us -> 228 us  [exchange(): return lax.ppermute(values, axis, [(i, i ^ mask) for i in range(size)])]
    all_gather x6 -> x5, waiting for transfers between devices: 78.8 us -> 26.1 us  [gather_line(): lax.all_gather(rows, 'fsdp', axis=0, tiled=True, axis_index_groups=lines(...]
    ppermute x35 -> x84, starting transfers between devices: 30.7 us -> 63.9 us  [exchange(): return lax.ppermute(values, axis, [(i, i ^ mask) for i in range(size)])]
    pallas_call x0 -> x12, Pallas kernels: none -> 26.3 us  [the longest x4 13 us: stack_rows(): pl.pallas_call(functools.partial(stack_kernel, count), in_specs=[anywhere...]
    concatenate x8 -> x0, local copies, waits for them, and re-layouts: 20.2 us -> none  [the longest x4 9.53 us: gather_pair(): return jnp.concatenate([near, far], axis=0)]
    dot_general x12 -> x6, matrix products: 59.5 us -> 42.6 us  [matmul_tn(): lax.dot_general(first_op, second_op, (((0,), (0,)), ((), ())), preferred_...]
    dot_general x12 -> x15, matrix products: 52.3 us -> 54.2 us  [matmul_nt(): lax.dot_general(first_op, second_op, (((1,), (1,)), ((), ())), preferred_...]
    convert_element_type x13 -> x19, other arithmetic: 17.7 us -> 16.6 us  [the longest x1 4.58 us: body(): output = ((middle + ffn_branch) * valid_rows).astype(BF16)]
  transfers between devices with their start and end apart: 47 -> 94, of which waited for: 22 -> 39; matrix products, arithmetic and copies ran while one was open for 35% -> 32% of each run, Pallas kernels for 5% -> 10%
where the time goes in v4:
time: 660 us; the launch traced here: 656 us
  waiting for transfers between devices  254 us (38%)
  matrix products  159 us (24%)
  Pallas kernels  67.8 us (10%)
  starting transfers between devices  64.7 us (10%)
  other arithmetic  49.3 us (7%)
  local copies, waits for them, and re-layouts  44.7 us (7%)
  between operations  16.3 us (2%)
    ppermute x84, waiting for transfers between devices, exchange(): return lax.ppermute(values, axis, [(i, i ^ mask) for i in range(size)])  228 us
    ppermute x84, starting transfers between devices, exchange(): return lax.ppermute(values, axis, [(i, i ^ mask) for i in range(size)])  63.9 us
    dot_general x6, matrix products, matmul(): return jnp.dot(first_op, second_op, preferred_element_type=F32)  62.3 us
    dot_general x15, matrix products, matmul_nt(): lax.dot_general(first_op, second_op, (((1,), (1,)), ((), ())), preferred_...  54.2 us
    dot_general x6, matrix products, matmul_tn(): lax.dot_general(first_op, second_op, (((0,), (0,)), ((), ())), preferred_...  42.6 us
    unnamed x145, local copies, waits for them, and re-layouts  31 us
    all_gather x5, waiting for transfers between devices, gather_line(): lax.all_gather(rows, 'fsdp', axis=0, tiled=True, axis_index_groups=lines(...  26.1 us
    pallas_call x1, Pallas kernels, attend_backward(): pl.pallas_call(functools.partial(attend_backward_kernel, masks, head_size...  23.1 us
  transfers between devices with their start and end apart: 94, of which 39 were waited for; matrix products, arithmetic and copies ran while one was open for 32% of the time, Pallas kernels for 10%

profile of v4, /device:TPU:0, one launch (start us, length us, event | category | flops | bytes accessed | tf_op | source)
XLA Modules:
  0.0 656.2 jit_solution(709142200143401830)
XLA Ops:
  29.0 8.2 %collective-permute-done.2 = bf16[256,768]{1,0:T(8,128)(2,1)S(1)} collective-permute-done((bf16[256,768]{1,0:T(8,128)(2,1)S(1)}, bf16[256,768]{1,0:T(8,128)(2,1)S(1)}, u32[]{:S(2)}, u32[]{:S(2)}) %collective-permute-start.2) | collective-permute-done | bytes 393248 | tf_op jit(solution)/shard_map/ppermute | solution.py:18
  41.1 20.6 %collective-permute-done.3.refs_1_ = bf16[256,2048]{1,0:T(8,128)(2,1)S(1)} collective-permute-done((bf16[256,2048]{1,0:T(8,128)(2,1)S(1)}, bf16[256,2048]{1,0:T(8,128)(2,1)S(1)}, u32[]{:S(2)}, u32[]{:S(2)}) %collective-permute-start.3) | collective-permute-done | bytes 1048608 | tf_op jit(solution)/shard_map/ppermute | solution.py:18
  66.8 7.7 %collective-permute-done = s32[1]{0:T(128)} collective-permute-done((s32[1]{0:T(128)}, s32[1]{0:T(128)}, u32[]{:S(2)}, u32[]{:S(2)}) %collective-permute-start) | collective-permute-done | bytes 36 | tf_op jit(solution)/shard_map/ppermute | solution.py:18
  91.2 10.7 %fusion.54 = f32[2048,512]{1,0:T(8,128)} fusion(bf16[2048,2048]{1,0:T(8,128)(2,1)} %copy-done.5, bf16[2048,512]{0,1:T(8,128)(2,1)} %all-gather.6.cloned.1.call-done), kind=kOutput, calls=%fused_computation.185 | convolution fusion | flops 4294967296 | bytes 14680064 | tf_op jit(solution)/shard_map/dot_general | solution.py:248
  101.9 18.3 %attend_forward.1 = (f32[2,2,512,256]{3,2,1,0:T(8,128)}, f32[2,1024,256]{2,1,0:T(8,128)}, bf16[2,1024,256]{2,1,0:T(8,128)(2,1)}, bf16[2,1024,128]{2,1,0:T(8,128)(2,1)}, bf16[2,1024,128]{2,1,0:T(8,128)(2,1)}) custom-call(s32[1]{0:T(128)} %bitcast.share_ref, s32[2]{0:T(128)} %pad_add_fusion.length_ref, f32[2,2,512,512]{3,2,1,0:T(8,128)} %bitcast.58, ...), custom_call_target="tpu_custom_call" | custom-call | flops 1024 | bytes 1024 | tf_op jit(solution)/shard_map/attend_forward/pallas_call | solution.py:477
  122.3 8.4 %multiply_convert_fusion.7 = (bf16[2048,256]{1,0:T(8,128)(2,1)S(1)}, f32[2048,256]{1,0:T(8,128)}) fusion(f32[2,2,512,256]{3,2,1,0:T(8,128)} %get-tuple-element.93, bf16[2048,2048]{1,0:T(8,128)(2,1)} %copy-done.5, bf16[2048,512]{0,1:T(8,128)(2,1)} %all-gather.8.cloned.1.call-done), kind=kOutput, calls=%fused_computation.58 | convolution fusion | flops 2150105088 | bytes 14680064 | tf_op jit(solution)/shard_map/dot_general | solution.py:248
  144.5 10.5 %collective-permute-done.18 = bf16[128,2048]{1,0:T(8,128)(2,1)S(1)} collective-permute-done((bf16[128,2048]{1,0:T(8,128)(2,1)S(1)}, bf16[128,2048]{1,0:T(8,128)(2,1)S(1)}, u32[]{:S(2)}, u32[]{:S(2)}) %collective-permute-start.18) | collective-permute-done | bytes 524320 | tf_op jit(solution)/shard_map/ppermute | solution.py:18
  159.5 10.6 %collective-permute-done.19 = bf16[128,2048]{1,0:T(8,128)(2,1)S(1)} collective-permute-done((bf16[128,2048]{1,0:T(8,128)(2,1)S(1)}, bf16[128,2048]{1,0:T(8,128)(2,1)S(1)}, u32[]{:S(2)}, u32[]{:S(2)}) %collective-permute-start.19) | collective-permute-done | bytes 524320 | tf_op jit(solution)/shard_map/ppermute | solution.py:18
  171.8 7.9 %collective-permute-done.16 = bf16[128,2048]{1,0:T(8,128)(2,1)S(1)} collective-permute-done((bf16[128,2048]{1,0:T(8,128)(2,1)S(1)}, bf16[128,2048]{1,0:T(8,128)(2,1)S(1)}, u32[]{:S(2)}, u32[]{:S(2)}) %collective-permute-start.16) | collective-permute-done | bytes 524320 | tf_op jit(solution)/shard_map/ppermute | solution.py:18
  185.0 21.6 %collective-permute-done.23.refs_1_ = bf16[256,2048]{1,0:T(8,128)(2,1)S(1)} collective-permute-done((bf16[256,2048]{1,0:T(8,128)(2,1)S(1)}, bf16[256,2048]{1,0:T(8,128)(2,1)S(1)}, u32[]{:S(2)}, u32[]{:S(2)}) %collective-permute-start.23) | collective-permute-done | bytes 1048608 | tf_op jit(solution)/shard_map/ppermute | solution.py:18
  230.1 11.7 %fusion.55 = f32[2048,768]{1,0:T(8,128)} fusion(bf16[2048,2048]{1,0:T(8,128)(2,1)} %copy-done.6, bf16[2048,768]{1,0:T(8,128)(2,1)} %all-gather.10.cloned.1.call-done), kind=kOutput, calls=%fused_computation.186 | convolution fusion | flops 6442450944 | bytes 17825792 | tf_op jit(solution)/shard_map/dot_general | solution.py:248
  241.8 11.4 %collective-permute-done.32.refs_1_ = bf16[256,2048]{1,0:T(8,128)(2,1)S(1)} collective-permute-done((bf16[256,2048]{1,0:T(8,128)(2,1)S(1)}, bf16[256,2048]{1,0:T(8,128)(2,1)S(1)}, u32[]{:S(2)}, u32[]{:S(2)}) %collective-permute-start.32) | collective-permute-done | bytes 1048608 | tf_op jit(solution)/shard_map/ppermute | solution.py:18
  259.0 9.4 %collective-permute-done.34.refs_3_ = bf16[128,2048]{1,0:T(8,128)(2,1)} collective-permute-done((bf16[128,2048]{1,0:T(8,128)(2,1)}, bf16[128,2048]{1,0:T(8,128)(2,1)}, u32[]{:S(2)}, u32[]{:S(2)}) %collective-permute-start.34) | collective-permute-done | bytes 524320 | tf_op jit(solution)/shard_map/ppermute | solution.py:18
  270.3 13.1 %multiply_convert_fusion.2 = (bf16[2048,768]{1,0:T(8,128)(2,1)S(1)}, f32[2048,768]{1,0:T(8,128)}) fusion(f32[2048,768]{1,0:T(8,128)} %fusion.55, bf16[2048,2048]{1,0:T(8,128)(2,1)} %copy-done.6, bf16[2048,768]{1,0:T(8,128)(2,1)} %all-gather.12.cloned.1.call-done), kind=kOutput, calls=%fused_computation.4 | convolution fusion | flops 6451888128 | bytes 27262976 | tf_op jit(solution)/shard_map/dot_general | solution.py:248
  290.7 8.5 %convolution_convert_fusion.8 = bf16[2048,768]{1,0:T(8,128)(2,1)} fusion(bf16[2048,2048]{1,0:T(8,128)(2,1)S(1)} %stack_rows.6, bf16[2048,768]{1,0:T(8,128)(2,1)S(1)} %get-tuple-element.129), kind=kOutput, calls=%fused_computation.15 | convolution fusion | flops 6444023808 | bytes 14680064 | tf_op jit(solution)/shard_map/dot_general | solution.py:252
  299.2 26.1 %all-gather.14.cloned.1.call-done = bf16[2048,768]{1,0:T(8,128)(2,1)} async-done(((bf16[512,768]{1,0:T(8,128)(2,1)}), bf16[2048,768]{1,0:T(8,128)(2,1)}) %all-gather.14.cloned.1.call-update) | async-done | bytes 3145744 | tf_op jit(solution)/shard_map/all_gather | solution.py:51
  325.3 14.6 %multiply_convert_fusion = (bf16[2048,768]{1,0:T(8,128)(2,1)S(1)}, bf16[2048,768]{1,0:T(8,128)(2,1)S(1)}) fusion(f32[2048,768]{1,0:T(8,128)} %fusion.55, f32[2048,768]{1,0:T(8,128)} %get-tuple-element.260, bf16[2048,2048]{1,0:T(8,128)(2,1)} %copy-done.7, bf16[2048,768]{1,0:T(8,128)(2,1)} %all-gather.14.cloned.1.call-done), kind=kOutput, calls=%fused_computation.2 | convolution fusion | flops 6462898176 | bytes 30408704 | tf_op jit(solution)/shard_map/dot_general | solution.py:248
  363.2 8.9 %convolution_convert_fusion.7 = bf16[2048,768]{1,0:T(8,128)(2,1)} fusion(bf16[2048,2048]{1,0:T(8,128)(2,1)S(1)} %bitcast.57, bf16[2048,768]{1,0:T(8,128)(2,1)S(1)} %get-tuple-element.116), kind=kOutput, calls=%fused_computation.14 | convolution fusion | flops 6444023808 | bytes 14680064 | tf_op jit(solution)/shard_map/dot_general | solution.py:252
  397.6 10.4 %convolution_convert_fusion.6 = bf16[2048,768]{1,0:T(8,128)(2,1)} fusion(bf16[2048,2048]{1,0:T(8,128)(2,1)} %copy-done.6, bf16[2048,768]{1,0:T(8,128)(2,1)S(1)} %copy-done.51), kind=kOutput, calls=%fused_computation.13 | convolution fusion | flops 6444023808 | bytes 14680064 | tf_op jit(solution)/shard_map/dot_general | solution.py:252
  408.1 8.0 %collective-permute-done.47 = bf16[128,2048]{1,0:T(8,128)(2,1)} collective-permute-done((bf16[128,2048]{1,0:T(8,128)(2,1)}, bf16[128,2048]{1,0:T(8,128)(2,1)}, u32[]{:S(2)}, u32[]{:S(2)}) %collective-permute-start.47) | collective-permute-done | bytes 524320 | tf_op jit(solution)/shard_map/ppermute | solution.py:18
  430.4 15.2 %collective-permute-done.49.refs_1_ = bf16[256,2048]{1,0:T(8,128)(2,1)S(1)} collective-permute-done((bf16[256,2048]{1,0:T(8,128)(2,1)S(1)}, bf16[256,2048]{1,0:T(8,128)(2,1)S(1)}, u32[]{:S(2)}, u32[]{:S(2)}) %collective-permute-start.49) | collective-permute-done | bytes 1048608 | tf_op jit(solution)/shard_map/ppermute | solution.py:18
  486.7 23.1 %attend_backward.1 = (bf16[2,2,512,768]{3,2,1,0:T(8,128)(2,1)}, f32[8,128]{1,0:T(8,128)}) custom-call(s32[1]{0:T(128)} %bitcast.share_ref, s32[2]{0:T(128)} %pad_add_fusion.length_ref, bf16[2,2,512,256]{3,2,1,0:T(8,128)(2,1)} %bitcast.67, bf16[2,2,512,256]{3,2,1,0:T(8,128)(2,1)} %bitcast.66, f32[2,2,512,512]{3,2,1,0:T(8,128)} %bitcast.61, ...), custom_call_target="tpu_custom_call" | custom-call | flops 1024 | bytes 1024 | tf_op jit(solution)/shard_map/attend_backward/pallas_call | solution.py:502
  550.6 9.9 %convolution_convert_fusion.9 = bf16[2048,512]{0,1:T(8,128)(2,1)} fusion(bf16[2048,2048]{1,0:T(8,128)(2,1)} %copy-done.5, bf16[2048,768]{1,0:T(8,128)(2,1)} %bitcast.68), kind=kOutput, calls=%fused_computation.24 | convolution fusion | flops 4296015872 | bytes 12582912 | tf_op jit(solution)/shard_map/dot_general | solution.py:252
  593.9 15.5 %collective-permute-done.74 = bf16[128,2048]{1,0:T(8,128)(2,1)} collective-permute-done((bf16[128,2048]{1,0:T(8,128)(2,1)}, bf16[128,2048]{1,0:T(8,128)(2,1)}, u32[]{:S(2)}, u32[]{:S(2)}) %collective-permute-start.74) | collective-permute-done | bytes 524320 | tf_op jit(solution)/shard_map/ppermute | solution.py:18
  (453 shorter events, 329.4 us)
Async XLA Ops:
  7.2 84.0 %all-gather.6.cloned.1.call-start = ((), (), s32[]{:S(2)}) async-start(), calls=%async_computation.5 | async-start | bytes 2621440 | tf_op jit(solution)/shard_map/all_gather | solution.py:51
  22.0 100.2 %all-gather.8.cloned.1.call-start = ((), (), s32[]{:S(2)}) async-start(), calls=%async_computation.6 | async-start | bytes 2621440 | tf_op jit(solution)/shard_map/all_gather | solution.py:51
  74.5 155.6 %all-gather.10.cloned.1.call-start = ((), (), s32[]{:S(2)}) async-start(), calls=%async_computation.7 | async-start | bytes 3932160 | tf_op jit(solution)/shard_map/all_gather | solution.py:51
  89.0 31.2 %collective-permute-start.14 = (bf16[256,768]{1,0:T(8,128)(2,1)S(1)}, bf16[256,768]{1,0:T(8,128)(2,1)S(1)}, u32[]{:S(2)}, u32[]{:S(2)}) collective-permute-start(bf16[256,768]{1,0:T(8,128)(2,1)S(1)} %broadcast_select_fusion.15), channel_id=1, source_target_pairs={{0,4},{4,0},{8,12},{12,8},{16,20},{20,16},{24,28},{28,24},{1,5},{5... | collective-permute-start | bytes 1179656 | tf_op jit(solution)/shard_map/ppermute | solution.py:18
  90.3 29.9 %collective-permute-start.13 = (bf16[256,768]{1,0:T(8,128)(2,1)S(1)}, bf16[256,768]{1,0:T(8,128)(2,1)S(1)}, u32[]{:S(2)}, u32[]{:S(2)}) collective-permute-start(bf16[256,768]{1,0:T(8,128)(2,1)S(1)} %broadcast_select_fusion.19), channel_id=1, source_target_pairs={{0,4},{4,0},{8,12},{12,8},{16,20},{20,16},{24,28},{28,24},{1,5},{5... | collective-permute-start | bytes 1179656 | tf_op jit(solution)/shard_map/ppermute | solution.py:18
  133.4 136.9 %all-gather.12.cloned.1.call-start = ((), (), s32[]{:S(2)}) async-start(), calls=%async_computation.8 | async-start | bytes 3932160 | tf_op jit(solution)/shard_map/all_gather | solution.py:51
  185.0 140.3 %all-gather.14.cloned.1.call-start = ((), (), s32[]{:S(2)}) async-start(), calls=%async_computation.9 | async-start | bytes 3932160 | tf_op jit(solution)/shard_map/all_gather | solution.py:51
  227.9 25.2 %collective-permute-start.32 = (bf16[256,2048]{1,0:T(8,128)(2,1)S(1)}, bf16[256,2048]{1,0:T(8,128)(2,1)S(1)}, u32[]{:S(2)}, u32[]{:S(2)}) collective-permute-start(bf16[256,2048]{1,0:T(8,128)(2,1)S(1)} %fusion.17.refs_0_), channel_id=1, source_target_pairs={{0,2},{1,3},{2,0},{3,1},{4,6},{5,7},{6,4},{7,5},{8,10},{9,11},{10,... | collective-permute-start | bytes 3145736 | tf_op jit(solution)/shard_map/ppermute | solution.py:18
  258.3 157.8 %reduce-scatter.6.cloned.1.call-start = ((), (), s32[]{:S(2)}) async-start(), calls=%async_computation.10 | async-start | bytes 3932160 | tf_op jit(solution)/shard_map/reduce_scatter | solution.py:55
  299.2 160.2 %reduce-scatter.8.cloned.1.call-start = ((), (), s32[]{:S(2)}) async-start(), calls=%async_computation.11 | async-start | bytes 3932160 | tf_op jit(solution)/shard_map/reduce_scatter | solution.py:55
  347.0 28.3 %collective-permute-start.42 = (bf16[768,2048]{1,0:T(8,128)(2,1)}, bf16[768,2048]{1,0:T(8,128)(2,1)S(1)}, u32[]{:S(2)}, u32[]{:S(2)}) collective-permute-start(bf16[768,2048]{1,0:T(8,128)(2,1)} %add_convert_fusion.1), channel_id=1, source_target_pairs={{0,1},{1,0},{2,3},{3,2},{4,5},{5,4},{6,7},{7,6},{8,9},{9,8},{10,11... | collective-permute-start | bytes 9437192 | tf_op jit(solution)/shard_map/ppermute | solution.py:18
  372.2 165.7 %reduce-scatter.10.cloned.1.call-start = ((), (), s32[]{:S(2)}) async-start(), calls=%async_computation.12 | async-start | bytes 3932160 | tf_op jit(solution)/shard_map/reduce_scatter | solution.py:55
  384.8 31.3 %collective-permute-start.43 = (bf16[128,2048]{1,0:T(8,128)(2,1)}, bf16[128,2048]{1,0:T(8,128)(2,1)S(1)}, u32[]{:S(2)}, u32[]{:S(2)}) collective-permute-start(bf16[128,2048]{1,0:T(8,128)(2,1)} %get-tuple-element.119), channel_id=1, source_target_pairs={{0,2},{1,3},{2,0},{3,1},{4,6},{5,7},{6,4},{7,5},{8,10},{9,11},{10,... | collective-permute-start | bytes 1572872 | tf_op jit(solution)/shard_map/ppermute | solution.py:18
  385.3 30.8 %collective-permute-start.48 = (bf16[128,2048]{1,0:T(8,128)(2,1)}, bf16[128,2048]{1,0:T(8,128)(2,1)S(1)}, u32[]{:S(2)}, u32[]{:S(2)}) collective-permute-start(bf16[128,2048]{1,0:T(8,128)(2,1)} %get-tuple-element.128), channel_id=1, source_target_pairs={{0,4},{4,0},{8,12},{12,8},{16,20},{20,16},{24,28},{28,24},{1,5},{5... | collective-permute-start | bytes 1572872 | tf_op jit(solution)/shard_map/ppermute | solution.py:18
  408.0 185.9 %reduce-scatter.12.cloned.1.call-start = ((), (), s32[]{:S(2)}) async-start(), calls=%async_computation.13 | async-start | bytes 2621440 | tf_op jit(solution)/shard_map/reduce_scatter | solution.py:55
  421.7 25.4 %collective-permute-start.50 = (bf16[256,2048]{1,0:T(8,128)(2,1)S(1)}, bf16[256,2048]{1,0:T(8,128)(2,1)S(1)}, u32[]{:S(2)}, u32[]{:S(2)}) collective-permute-start(bf16[256,2048]{1,0:T(8,128)(2,1)S(1)} %get-tuple-element.193.refs_0_), channel_id=1, source_target_pairs={{0,4},{4,0},{8,12},{12,8},{16,20},{20,16},{24,28},{28,24},{1,5},{5... | collective-permute-start | bytes 3145736 | tf_op jit(solution)/shard_map/ppermute | solution.py:18
  423.2 39.1 %collective-permute-start.53 = (bf16[256,2048]{1,0:T(8,128)(2,1)S(1)}, bf16[256,2048]{1,0:T(8,128)(2,1)}, u32[]{:S(2)}, u32[]{:S(2)}) collective-permute-start(bf16[256,2048]{1,0:T(8,128)(2,1)S(1)} %get-tuple-element.193.refs_0_), channel_id=1, source_target_pairs={{0,1},{1,0},{2,3},{3,2},{4,5},{5,4},{6,7},{7,6},{8,9},{9,8},{10,11... | collective-permute-start | bytes 3145736 | tf_op jit(solution)/shard_map/ppermute | solution.py:18
  468.9 41.0 %collective-permute-start.60 = (bf16[256,2048]{1,0:T(8,128)(2,1)}, bf16[256,2048]{1,0:T(8,128)(2,1)S(1)}, u32[]{:S(2)}, u32[]{:S(2)}) collective-permute-start(bf16[256,2048]{1,0:T(8,128)(2,1)} %convolution_convert_fusion.14), channel_id=1, source_target_pairs={{0,1},{1,0},{2,3},{3,2},{4,5},{5,4},{6,7},{7,6},{8,9},{9,8},{10,11... | collective-permute-start | bytes 3145736 | tf_op jit(solution)/shard_map/ppermute | solution.py:18
  468.9 55.9 %collective-permute-start.58 = (bf16[768,2048]{1,0:T(8,128)(2,1)}, bf16[768,2048]{1,0:T(8,128)(2,1)}, u32[]{:S(2)}, u32[]{:S(2)}) collective-permute-start(bf16[768,2048]{1,0:T(8,128)(2,1)} %convolution_convert_fusion.4), channel_id=1, source_target_pairs={{0,1},{1,0},{2,3},{3,2},{4,5},{5,4},{6,7},{7,6},{8,9},{9,8},{10,11... | collective-permute-start | bytes 9437192 | tf_op jit(solution)/shard_map/ppermute | solution.py:18
  479.8 158.9 %reduce-scatter.14.cloned.1.call-start = ((), (), s32[]{:S(2)}) async-start(), calls=%async_computation.14 | async-start | bytes 2621440 | tf_op jit(solution)/shard_map/reduce_scatter | solution.py:55
  520.5 50.1 %collective-permute-start.69 = (bf16[768,2048]{1,0:T(8,128)(2,1)}, bf16[768,2048]{1,0:T(8,128)(2,1)S(1)}, u32[]{:S(2)}, u32[]{:S(2)}) collective-permute-start(bf16[768,2048]{1,0:T(8,128)(2,1)} %convolution_convert_fusion.3), channel_id=1, source_target_pairs={{0,1},{1,0},{2,3},{3,2},{4,5},{5,4},{6,7},{7,6},{8,9},{9,8},{10,11... | collective-permute-start | bytes 9437192 | tf_op jit(solution)/shard_map/ppermute | solution.py:18
  523.9 46.6 %collective-permute-start.68 = (bf16[256,2048]{1,0:T(8,128)(2,1)}, bf16[256,2048]{1,0:T(8,128)(2,1)}, u32[]{:S(2)}, u32[]{:S(2)}) collective-permute-start(bf16[256,2048]{1,0:T(8,128)(2,1)} %convolution_convert_fusion.11), channel_id=1, source_target_pairs={{0,1},{1,0},{2,3},{3,2},{4,5},{5,4},{6,7},{7,6},{8,9},{9,8},{10,11... | collective-permute-start | bytes 3145736 | tf_op jit(solution)/shard_map/ppermute | solution.py:18
  579.3 30.1 %collective-permute-start.70 = (bf16[128,2048]{1,0:T(8,128)(2,1)}, bf16[128,2048]{1,0:T(8,128)(2,1)}, u32[]{:S(2)}, u32[]{:S(2)}) collective-permute-start(bf16[128,2048]{1,0:T(8,128)(2,1)} %get-tuple-element.155), channel_id=1, source_target_pairs={{0,2},{1,3},{2,0},{3,1},{4,6},{5,7},{6,4},{7,5},{8,10},{9,11},{10,... | collective-permute-start | bytes 1572872 | tf_op jit(solution)/shard_map/ppermute | solution.py:18
  580.3 29.2 %collective-permute-start.75 = (bf16[128,2048]{1,0:T(8,128)(2,1)}, bf16[128,2048]{1,0:T(8,128)(2,1)}, u32[]{:S(2)}, u32[]{:S(2)}) collective-permute-start(bf16[128,2048]{1,0:T(8,128)(2,1)} %get-tuple-element.163), channel_id=1, source_target_pairs={{0,4},{4,0},{8,12},{12,8},{16,20},{20,16},{24,28},{28,24},{1,5},{5... | collective-permute-start | bytes 1572872 | tf_op jit(solution)/shard_map/ppermute | solution.py:18
  (136 other events, 1445.8 us)
Sparse Core Ops, SparseCore 0:
  22.1 47.7 all-gather.5
  74.6 46.5 all-gather.7
  133.5 63.9 all-gather.9
  198.9 62.1 all-gather.11
  263.1 62.1 all-gather.13
  327.5 58.8 reduce-scatter.5
  388.7 60.2 reduce-scatter.7
  451.3 60.2 reduce-scatter.9
  513.9 43.9 reduce-scatter.11
  560.7 42.5 reduce-scatter.13

commit v5 on v4

--- a/solution.py
+++ b/solution.py
@@ -70,6 +70,10 @@
         shards.append(in_order(own[:, piece], other[:, piece], odd, 1).astype(F32))
         start += width
     return shards
+
+
+def dot_rows(first, second):
+    return jnp.sum(first.astype(F32) * second.astype(F32), axis=1)
 
 
 def hold(value, *others):
@@ -217,9 +221,12 @@
     arrived_corner, arrived = core(far_corner, shares), core(far, shares)
     if before:
         arrived_corner, arrived = hold((arrived_corner, arrived), *before)
-    upper, lower = add_corner(near, arrived_corner)
+    return add_corner(near, arrived_corner), add_main(near, arrived)
+
+
+def send_sum(added, members, shares):
+    (upper, lower), (own, side_a, side_b, partner_a, partner_b) = added
     corners = across(upper, shares), to_partner(lower, members)
-    own, side_a, side_b, partner_a, partner_b = add_main(near, arrived)
     return corners, (own, side_b, partner_a, across(side_a, shares), to_partner(partner_b, members))
 
 
@@ -235,12 +242,11 @@
     return own + from_side + from_partner
 
 
-def sum_everywhere(values, axes):
-    for axis, count in axes:
-        mask = 1
-        while mask < count:
-            values = values + exchange(values, axis, count, mask)
-            mask <<= 1
+def sum_everywhere(values, axis, mask, stop):
+    count = lax.axis_size(axis)
+    while mask < stop:
+        values = values + exchange(values, axis, count, mask)
+        mask <<= 1
     return values
 
 
@@ -450,6 +456,105 @@
         send_ref[side, here, pl.ds(offset, group * head_size)] = gate_grad_ref[side, here, :]
 
 
+def units_kernel(rows_ref, gate_weights_ref, up_weights_ref, gate_ref, up_ref, mid_ref):
+    rows = rows_ref[...]
+    gate = matmul(rows, gate_weights_ref[...])
+    gate_ref[...] = gate
+    up = matmul(rows, up_weights_ref[...])
+    up_ref[...] = up
+    mid_ref[...] = (gate * jax.nn.sigmoid(gate) * up).astype(BF16)
+
+
+def hidden_units(normed, gate_weights, up_weights):
+    rows, width = normed.shape
+    units = gate_weights.shape[1]
+    tile = rows // 8
+    tokens = pl.BlockSpec((tile, width), lambda i: (i, 0))
+    hidden = pl.BlockSpec((tile, units), lambda i: (i, 0))
+    weight = pl.BlockSpec((width, units), lambda i: (0, 0), pipeline_mode=pl.Buffered(1))
+    return pl.pallas_call(
+        units_kernel,
+        grid=(8,),
+        in_specs=[tokens, weight, weight],
+        out_specs=[hidden, hidden, hidden],
+        out_shape=[jax.ShapeDtypeStruct((rows, units), kind) for kind in (F32, F32, BF16)],
+        compiler_params=pltpu.CompilerParams(vmem_limit_bytes=32 << 20),
+        cost_estimate=light_cost(),
+        name="hidden_units",
+    )(normed, gate_weights, up_weights)
+
+
+def unit_grads_kernel(
+    near_steps,
+    far_steps,
+    branch_ref,
+    gate_ref,
+    up_ref,
+    down_weights_ref,
+    gate_weights_ref,
+    up_weights_ref,
+    gate_grad_ref,
+    up_grad_ref,
+    near_ref,
+    far_ref,
+    corner_ref,
+):
+    step = pl.program_id(0)
+    mid_grad = matmul(branch_ref[...], down_weights_ref[...])
+    gate, up = gate_ref[...], up_ref[...]
+    sig = jax.nn.sigmoid(gate)
+    gate_grad = (mid_grad * up * sig * (1.0 + gate * (1.0 - sig))).astype(BF16)
+    up_grad = (mid_grad * (gate * sig)).astype(BF16)
+    gate_grad_ref[...] = gate_grad
+    up_grad_ref[...] = up_grad
+    back = matmul_nt(gate_grad, gate_weights_ref[...]) + matmul_nt(up_grad, up_weights_ref[...])
+    back = back.astype(BF16)
+
+    @pl.when(step < near_steps)
+    def _():
+        near_ref[...] = back
+
+    @pl.when((step >= near_steps) & (step < near_steps + far_steps))
+    def _():
+        far_ref[...] = back
+
+    @pl.when(step == near_steps + far_steps)
+    def _():
+        corner_ref[...] = back
+
+
+def unit_grads(branch, ffn_gate, ffn_up, down_weights, gate_weights, up_weights):
+    rows, width = branch.shape
+    units = ffn_gate.shape[1]
+    tile = rows // 8
+    tokens = pl.BlockSpec((tile, width), lambda i: (i, 0))
+    hidden = pl.BlockSpec((tile, units), lambda i: (i, 0))
+    weight = pl.BlockSpec((width, units), lambda i: (0, 0), pipeline_mode=pl.Buffered(1))
+    gate_grad, up_grad, *parts = pl.pallas_call(
+        functools.partial(unit_grads_kernel, 4, 3),
+        grid=(8,),
+        in_specs=[tokens, hidden, hidden, weight, weight, weight],
+        out_specs=[
+            hidden,
+            hidden,
+            pl.BlockSpec((tile, width), lambda i: (jnp.minimum(i, 3), 0)),
+            pl.BlockSpec((tile, width), lambda i: (jnp.clip(i - 4, 0, 2), 0)),
+            pl.BlockSpec((tile, width), lambda i: (0, 0)),
+        ],
+        out_shape=[
+            jax.ShapeDtypeStruct((rows, units), BF16),
+            jax.ShapeDtypeStruct((rows, units), BF16),
+            jax.ShapeDtypeStruct((4 * tile, width), BF16),
+            jax.ShapeDtypeStruct((3 * tile, width), BF16),
+            jax.ShapeDtypeStruct((tile, width), BF16),
+        ],
+        compiler_params=pltpu.CompilerParams(vmem_limit_bytes=44 << 20),
+        cost_estimate=light_cost(),
+        name="unit_grads",
+    )(branch, ffn_gate, ffn_up, down_weights, gate_weights, up_weights)
+    return gate_grad, up_grad, parts
+
+
 def head_specs(slots, group, kv_heads, head_size):
     half = slots // 2
     wide = group * head_size
@@ -574,8 +679,8 @@
         return rows_in(values, members, shares, *before)
 
     def sum_rows(parts, first, last):
-        opened = open_sum(parts, members, shares, *first)
-        return close_sum(*opened, members, shares, *last)
+        added = open_sum(parts, members, shares, *first)
+        return close_sum(*send_sum(added, members, shares), members, shares, *last)
 
     def in_parts(function):
         corner = function(slice(2 * half_rows - local_rows, 2 * half_rows)).astype(BF16)
@@ -609,26 +714,20 @@
     gate_sig = jax.nn.sigmoid(gate_pre)
     gated_out = (attended * gate_sig).astype(BF16)
     attn_parts = in_parts(lambda rows: matmul_nt(gated_out[rows], out_full))
-    middle = residual + sum_rows(attn_parts, (), ())
+    middle = residual + sum_rows(attn_parts, (), (gate_weights,))
     unit_two, root_two = normalize(middle)
     normed_two = gather_rows((unit_two * mlp_gain).astype(BF16))
     one_weights = jnp.concatenate([qkv_full, gate_full], axis=1)
-    ffn_gate = matmul(normed_two, gate_weights)
-    branch_full = gather_rows(hold(grad_rows.astype(BF16), normed_two), ffn_gate, one_weights)
-    ffn_up = matmul(normed_two, up_weights)
-    ffn_sig = jax.nn.sigmoid(ffn_gate)
-    ffn_act = ffn_gate * ffn_sig
-    ffn_mid = (ffn_act * ffn_up).astype(BF16)
+    ffn_gate, ffn_up, ffn_mid = hidden_units(normed_two, gate_weights, up_weights)
+    branch_full = gather_rows(
+        hold(grad_rows.astype(BF16), normed_two), None, one_weights, ffn_mid
+    )
 
     down_part = matmul_tn(branch_full, ffn_mid).astype(BF16)
     down_sum = scatter_line(down_part, members)
 
-    mid_grad = matmul(branch_full, hold(down_weights, down_part))
-    gate_grad = (mid_grad * ffn_up * ffn_sig * (1.0 + ffn_gate * (1.0 - ffn_sig))).astype(BF16)
-    up_grad = (mid_grad * ffn_act).astype(BF16)
-    back_parts = in_parts(
-        lambda rows: matmul_nt(gate_grad[rows], gate_weights)
-        + matmul_nt(up_grad[rows], up_weights)
+    gate_grad, up_grad, back_parts = unit_grads(
+        branch_full, ffn_gate, ffn_up, hold(down_weights, down_part), gate_weights, up_weights
     )
     gate_part = matmul_tn(normed_two, hold(gate_grad, back_parts)).astype(BF16)
     gate_sum = scatter_line(gate_part, members)
@@ -641,23 +740,25 @@
     mid_late = hold(ffn_mid, norm_two_grad)
     branch_parts = in_parts(lambda rows: matmul_nt(mid_late[rows], down_weights))
     attn_full_grad = gather_rows(middle_grad.astype(BF16), None, branch_parts, gate_sum)
+    branch_added = open_sum(branch_parts, members, shares)
     down_swap = swap_rows(hold(down_sum, attn_full_grad), odd, members)
     gate_swap = swap_rows(hold(gate_sum, attn_full_grad), odd, members)
-
+    attn_full_grad = hold(attn_full_grad, branch_added)
+    corners, opened = send_sum(hold(branch_added, attn_full_grad), members, shares)
     gated_grad = matmul(attn_full_grad, out_full)
     attended_grad = (gated_grad * gate_sig).astype(BF16)
     gate_pre_grad = (gated_grad * attended * gate_sig * (1.0 - gate_sig)).astype(BF16)
+    gate_attn_part = matmul_tn(normed_one, gate_pre_grad).astype(BF16)
     gate_out_part = jnp.concatenate(
         [
-            matmul_tn(normed_one, gate_pre_grad).astype(BF16),
+            gate_attn_part,
             matmul_tn(attn_full_grad, gated_out).astype(BF16),
         ],
         axis=1,
     )
     gate_out_sum = scatter_line(gate_out_part, members)
-    corners, opened = open_sum(hold(branch_parts, attn_full_grad), members, shares)
     one_send, gain_parts = attend_backward(
-        hold(attended_grad, gate_out_part, down_swap, gate_swap),
+        hold(attended_grad, gate_out_part),
         gate_pre_grad,
         qkv_raw,
         kept,
@@ -668,29 +769,40 @@
         masks,
         sizes,
     )
+    one_send = hold(one_send, corners, opened, down_swap, gate_swap)
     ffn_branch = close_sum(corners, opened, members, shares, one_send)
     output = ((middle + ffn_branch) * valid_rows).astype(BF16)
     units = up_sum.shape[1]
-    (down_shard,) = own_shard(*down_swap, odd, (units,))
-    (gate_shard,) = own_shard(*gate_swap, odd, (units,))
     one_parts = in_parts(lambda rows: matmul_nt(one_send[rows], one_weights))
     qkv_send = hold(one_send, up_sum, one_parts)[:, : qkv_raw.shape[1]]
     qkv_part = matmul_tn(normed_one, qkv_send).astype(BF16)
     qkv_sum = scatter_line(qkv_part, members)
-    norm_one_grad = sum_rows(one_parts, (qkv_part, ffn_branch), (gate_out_sum, output, down_shard, gate_shard))
-    attn_gain_part = jnp.sum(norm_one_grad * unit_one, axis=0)
+    attn_gain_part = (
+        dot_rows(qkv_part, qkv_full) + dot_rows(gate_attn_part, gate_full)
+    ) / attn_gain
+    up_swap = swap_rows(hold(up_sum, one_send), odd, members)
+    added_one = open_sum(one_parts, members, shares, qkv_part, ffn_branch)
+    gain_parts = hold(
+        jnp.concatenate([attn_gain_part, mlp_gain_part, gain_parts[0], gain_parts[1]]), added_one
+    )
+    gain_parts = sum_everywhere(gain_parts, "fsdp", 2, members)
+    gain_parts = sum_everywhere(gain_parts, "tensor", 1, 2)
+    norm_one_grad = close_sum(
+        *send_sum(added_one, members, shares), members, shares, gate_out_sum, gain_parts, up_swap
+    )
+    gain_totals = hold(gain_parts, norm_one_grad)
+    gain_totals = sum_everywhere(gain_totals, "tensor", 2, shares)
+    gain_totals = sum_everywhere(gain_totals, "fsdp", 1, 2)
     grad_hidden = middle_grad + norm_back(norm_one_grad, unit_one, root_one, attn_gain)
-    gain_totals = sum_everywhere(
-        jnp.concatenate([attn_gain_part, mlp_gain_part, gain_parts[0], gain_parts[1]]),
-        (("tensor", shares), ("fsdp", members)),
-    )
-    up_swap = swap_rows(hold(up_sum, norm_one_grad), odd, members)
-    gate_out_swap = swap_rows(hold(gate_out_sum, norm_one_grad), odd, members)
+    (down_shard,) = own_shard(*down_swap, odd, (units,))
+    (gate_shard,) = own_shard(*gate_swap, odd, (units,))
+    gate_out_swap = swap_rows(hold(gate_out_sum, norm_one_grad, qkv_sum), odd, members)
     (up_shard,) = own_shard(*up_swap, odd, (units,))
     gate_attn_shard, out_shard = own_shard(*gate_out_swap, odd, (query_width,) * 2)
     qkv_sum = hold(
         qkv_sum,
         norm_one_grad,
+        gain_totals,
         output,
         down_shard,
         gate_shard,

time: 660 us -> 645 us (0.977)
  matrix products: 159 us -> 98 us
  Pallas kernels: 67.8 us -> 118 us
  waiting for transfers between devices: 254 us -> 232 us
  local copies, waits for them, and re-layouts: 44.7 us -> 51.9 us
  starting transfers between devices: 64.7 us -> 71.7 us
    pallas_call x0 -> x2, Pallas kernels: none -> 50.5 us  [the longest x1 34.8 us: unit_grads(): pl.pallas_call(functools.partial(unit_grads_kernel, 4, 3), grid=(8,), in_...]
    dot_general x6 -> x3, matrix products: 62.3 us -> 22.9 us  [matmul(): return jnp.dot(first_op, second_op, preferred_element_type=F32)]
    dot_general x15 -> x9, matrix products: 54.2 us -> 31.6 us  [matmul_nt(): lax.dot_general(first_op, second_op, (((1,), (1,)), ((), ())), preferred_...]
    all_gather x5, waiting for transfers between devices: 26.1 us -> 9.51 us  [gather_line(): lax.all_gather(rows, 'fsdp', axis=0, tiled=True, axis_index_groups=lines(...]
    unnamed x145 -> x157, local copies, waits for them, and re-layouts: 31 us -> 37.4 us
  transfers between devices with their start and end apart: 94 -> 94, of which waited for: 39 -> 34; matrix products, arithmetic and copies ran while one was open for 32% -> 26% of each run, Pallas kernels for 10% -> 18%
where the time goes in v5:
time: 645 us; the launch traced here: 641 us
  waiting for transfers between devices  232 us (36%)
  Pallas kernels  118 us (18%)
  matrix products  98 us (15%)
  starting transfers between devices  71.7 us (11%)
  other arithmetic  53.8 us (8%)
  local copies, waits for them, and re-layouts  51.9 us (8%)
  between operations  16.2 us (3%)
    ppermute x84, waiting for transfers between devices, exchange(): return lax.ppermute(values, axis, [(i, i ^ mask) for i in range(size)])  222 us
    ppermute x84, starting transfers between devices, exchange(): return lax.ppermute(values, axis, [(i, i ^ mask) for i in range(size)])  70 us
    dot_general x6, matrix products, matmul_tn(): lax.dot_general(first_op, second_op, (((0,), (0,)), ((), ())), preferred_...  43.5 us
    unnamed x157, local copies, waits for them, and re-layouts  37.4 us
    pallas_call x1, Pallas kernels, unit_grads(): pl.pallas_call(functools.partial(unit_grads_kernel, 4, 3), grid=(8,), in_...  34.8 us
    dot_general x9, matrix products, matmul_nt(): lax.dot_general(first_op, second_op, (((1,), (1,)), ((), ())), preferred_...  31.6 us
    pallas_call x1, Pallas kernels, attend_backward(): pl.pallas_call(functools.partial(attend_backward_kernel, masks, head_size...  23.3 us
    dot_general x3, matrix products, matmul(): return jnp.dot(first_op, second_op, preferred_element_type=F32)  22.9 us
  transfers between devices with their start and end apart: 94, of which 34 were waited for; matrix products, arithmetic and copies ran while one was open for 26% of the time, Pallas kernels for 18%

profile of v5, /device:TPU:0, one launch (start us, length us, event | category | flops | bytes accessed | tf_op | source)
XLA Modules:
  0.0 641.1 jit_solution(8864172077804726072)
XLA Ops:
  31.9 7.6 %collective-permute-done.2 = bf16[256,768]{1,0:T(8,128)(2,1)S(1)} collective-permute-done((bf16[256,768]{1,0:T(8,128)(2,1)S(1)}, bf16[256,768]{1,0:T(8,128)(2,1)S(1)}, u32[]{:S(2)}, u32[]{:S(2)}) %collective-permute-start.2) | collective-permute-done | bytes 393248 | tf_op jit(solution)/shard_map/ppermute | solution.py:18
  43.4 20.0 %collective-permute-done.3.refs_1_ = bf16[256,2048]{1,0:T(8,128)(2,1)S(1)} collective-permute-done((bf16[256,2048]{1,0:T(8,128)(2,1)S(1)}, bf16[256,2048]{1,0:T(8,128)(2,1)S(1)}, u32[]{:S(2)}, u32[]{:S(2)}) %collective-permute-start.3) | collective-permute-done | bytes 1048608 | tf_op jit(solution)/shard_map/ppermute | solution.py:18
  67.6 7.4 %collective-permute-done = s32[1]{0:T(128)} collective-permute-done((s32[1]{0:T(128)}, s32[1]{0:T(128)}, u32[]{:S(2)}, u32[]{:S(2)}) %collective-permute-start) | collective-permute-done | bytes 36 | tf_op jit(solution)/shard_map/ppermute | solution.py:18
  90.7 10.6 %fusion.41 = f32[2048,512]{1,0:T(8,128)} fusion(bf16[2048,2048]{1,0:T(8,128)(2,1)} %copy-done.10, bf16[2048,512]{0,1:T(8,128)(2,1)} %all-gather.6.cloned.1.call-done), kind=kOutput, calls=%fused_computation.168 | convolution fusion | flops 4294967296 | bytes 14680064 | tf_op jit(solution)/shard_map/dot_general | solution.py:254
  101.3 17.8 %attend_forward.1 = (f32[2,2,512,256]{3,2,1,0:T(8,128)}, f32[2,1024,256]{2,1,0:T(8,128)}, bf16[2,1024,256]{2,1,0:T(8,128)(2,1)}, bf16[2,1024,128]{2,1,0:T(8,128)(2,1)}, bf16[2,1024,128]{2,1,0:T(8,128)(2,1)}) custom-call(s32[1]{0:T(128)} %bitcast.share_ref, s32[2]{0:T(128)} %pad_add_fusion.length_ref, f32[2,2,512,512]{3,2,1,0:T(8,128)} %bitcast.44, ...), custom_call_target="tpu_custom_call" | custom-call | flops 1024 | bytes 1024 | tf_op jit(solution)/shard_map/attend_forward/pallas_call | solution.py:582
  121.5 8.4 %multiply_convert_fusion.4 = (bf16[2048,256]{1,0:T(8,128)(2,1)S(1)}, f32[2048,256]{1,0:T(8,128)}) fusion(f32[2,2,512,256]{3,2,1,0:T(8,128)} %get-tuple-element.109, bf16[2048,2048]{1,0:T(8,128)(2,1)} %copy-done.10, bf16[2048,512]{0,1:T(8,128)(2,1)} %all-gather.8.cloned.1.call-done), kind=kOutput, calls=%fused_computation.49 | convolution fusion | flops 2150105088 | bytes 14680064 | tf_op jit(solution)/shard_map/dot_general | solution.py:254
  148.4 7.5 %collective-permute-done.20 = bf16[128,2048]{1,0:T(8,128)(2,1)} collective-permute-done((bf16[128,2048]{1,0:T(8,128)(2,1)}, bf16[128,2048]{1,0:T(8,128)(2,1)}, u32[]{:S(2)}, u32[]{:S(2)}) %collective-permute-start.20) | collective-permute-done | bytes 524320 | tf_op jit(solution)/shard_map/ppermute | solution.py:18
  161.5 10.6 %collective-permute-done.21 = bf16[128,2048]{1,0:T(8,128)(2,1)S(1)} collective-permute-done((bf16[128,2048]{1,0:T(8,128)(2,1)S(1)}, bf16[128,2048]{1,0:T(8,128)(2,1)S(1)}, u32[]{:S(2)}, u32[]{:S(2)}) %collective-permute-start.21) | collective-permute-done | bytes 524320 | tf_op jit(solution)/shard_map/ppermute | solution.py:18
  173.8 9.3 %all-gather.10.cloned.1.call-done.gate_weights_ref = bf16[2048,768]{1,0:T(8,128)(2,1)} async-done(((bf16[512,768]{1,0:T(8,128)(2,1)}), bf16[2048,768]{1,0:T(8,128)(2,1)}) %all-gather.10.cloned.1.call-update) | async-done | bytes 3145744 | tf_op jit(solution)/shard_map/all_gather | solution.py:51
  188.7 21.9 %collective-permute-done.23.refs_1_ = bf16[256,2048]{1,0:T(8,128)(2,1)S(1)} collective-permute-done((bf16[256,2048]{1,0:T(8,128)(2,1)S(1)}, bf16[256,2048]{1,0:T(8,128)(2,1)S(1)}, u32[]{:S(2)}, u32[]{:S(2)}) %collective-permute-start.23) | collective-permute-done | bytes 1048608 | tf_op jit(solution)/shard_map/ppermute | solution.py:18
  216.2 8.5 %collective-permute-done.25.refs_3_ = bf16[128,2048]{1,0:T(8,128)(2,1)} collective-permute-done((bf16[128,2048]{1,0:T(8,128)(2,1)}, bf16[128,2048]{1,0:T(8,128)(2,1)}, u32[]{:S(2)}, u32[]{:S(2)}) %collective-permute-start.25) | collective-permute-done | bytes 524320 | tf_op jit(solution)/shard_map/ppermute | solution.py:18
  241.1 23.9 %collective-permute-done.32.refs_1_ = bf16[256,2048]{1,0:T(8,128)(2,1)} collective-permute-done((bf16[256,2048]{1,0:T(8,128)(2,1)}, bf16[256,2048]{1,0:T(8,128)(2,1)}, u32[]{:S(2)}, u32[]{:S(2)}) %collective-permute-start.32) | collective-permute-done | bytes 1048608 | tf_op jit(solution)/shard_map/ppermute | solution.py:18
  273.2 15.7 %hidden_units.1 = (f32[2048,768]{1,0:T(8,128)S(1)}, f32[2048,768]{1,0:T(8,128)S(1)}, bf16[2048,768]{1,0:T(8,128)(2,1)S(1)}) custom-call(bf16[2048,2048]{1,0:T(8,128)(2,1)} %copy-done.2, bf16[2048,768]{1,0:T(8,128)(2,1)S(1)} %copy-done.8, bf16[2048,768]{1,0:T(8,128)(2,1)S(1)} %copy-done.9), custom_call_target="tpu_custom_call" | custom-call | flops 1024 | bytes 1024 | tf_op jit(solution)/shard_map/hidden_units/pallas_call | solution.py:475
  301.4 8.2 %convolution_convert_fusion.8 = bf16[2048,768]{1,0:T(8,128)(2,1)} fusion(bf16[2048,2048]{1,0:T(8,128)(2,1)S(1)} %stack_rows.6.branch_ref, bf16[2048,768]{1,0:T(8,128)(2,1)S(1)} %get-tuple-element.153), kind=kOutput, calls=%fused_computation.9 | convolution fusion | flops 6444023808 | bytes 14680064 | tf_op jit(solution)/shard_map/dot_general | solution.py:258
  310.4 34.8 %unit_grads.1 = (bf16[2048,768]{1,0:T(8,128)(2,1)S(1)}, bf16[2048,768]{1,0:T(8,128)(2,1)S(1)}, bf16[1024,2048]{1,0:T(8,128)(2,1)}, bf16[768,2048]{1,0:T(8,128)(2,1)}, bf16[256,2048]{1,0:T(8,128)(2,1)}) custom-call(bf16[2048,2048]{1,0:T(8,128)(2,1)} %copy-done.3, f32[2048,768]{1,0:T(8,128)} %copy-done.11, f32[2048,768]{1,0:T(8,128)} %copy-done.12, ...), custom_call_target="tpu_custom_call" | custom-call | flops 1024 | bytes 1024 | tf_op jit(solution)/shard_map/unit_grads/pallas_call | solution.py:533
  347.4 10.4 %convolution_convert_fusion.7 = bf16[2048,768]{1,0:T(8,128)(2,1)} fusion(bf16[2048,2048]{1,0:T(8,128)(2,1)} %copy-done.2, bf16[2048,768]{1,0:T(8,128)(2,1)S(1)} %get-tuple-element.139), kind=kOutput, calls=%fused_computation.8 | convolution fusion | flops 6444023808 | bytes 14680064 | tf_op jit(solution)/shard_map/dot_general | solution.py:258
  381.6 8.6 %convolution_convert_fusion.6 = bf16[2048,768]{1,0:T(8,128)(2,1)} fusion(bf16[2048,2048]{1,0:T(8,128)(2,1)S(1)} %bitcast.41, bf16[2048,768]{1,0:T(8,128)(2,1)S(1)} %copy-done.30), kind=kOutput, calls=%fused_computation.7 | convolution fusion | flops 6444023808 | bytes 14680064 | tf_op jit(solution)/shard_map/dot_general | solution.py:258
  390.1 9.4 %collective-permute-done.47 = bf16[128,2048]{1,0:T(8,128)(2,1)} collective-permute-done((bf16[128,2048]{1,0:T(8,128)(2,1)}, bf16[128,2048]{1,0:T(8,128)(2,1)}, u32[]{:S(2)}, u32[]{:S(2)}) %collective-permute-start.47) | collective-permute-done | bytes 524320 | tf_op jit(solution)/shard_map/ppermute | solution.py:18
  414.2 14.1 %collective-permute-done.51.refs_1_ = bf16[256,2048]{1,0:T(8,128)(2,1)S(1)} collective-permute-done((bf16[256,2048]{1,0:T(8,128)(2,1)S(1)}, bf16[256,2048]{1,0:T(8,128)(2,1)S(1)}, u32[]{:S(2)}, u32[]{:S(2)}) %collective-permute-start.51) | collective-permute-done | bytes 1048608 | tf_op jit(solution)/shard_map/ppermute | solution.py:18
  457.5 7.6 %collective-permute-done.66 = bf16[256,768]{1,0:T(8,128)(2,1)S(1)} collective-permute-done((bf16[256,768]{1,0:T(8,128)(2,1)S(1)}, bf16[256,768]{1,0:T(8,128)(2,1)S(1)}, u32[]{:S(2)}, u32[]{:S(2)}) %collective-permute-start.66) | collective-permute-done | bytes 393248 | tf_op jit(solution)/shard_map/ppermute | solution.py:18
  465.3 7.5 %collective-permute-done.67 = bf16[256,768]{1,0:T(8,128)(2,1)S(1)} collective-permute-done((bf16[256,768]{1,0:T(8,128)(2,1)S(1)}, bf16[256,768]{1,0:T(8,128)(2,1)S(1)}, u32[]{:S(2)}, u32[]{:S(2)}) %collective-permute-start.67) | collective-permute-done | bytes 393248 | tf_op jit(solution)/shard_map/ppermute | solution.py:18
  497.1 23.3 %attend_backward.1 = (bf16[2,2,512,768]{3,2,1,0:T(8,128)(2,1)}, f32[8,128]{1,0:T(8,128)}) custom-call(s32[1]{0:T(128)} %bitcast.share_ref, s32[2]{0:T(128)} %pad_add_fusion.length_ref, bf16[2,2,512,256]{3,2,1,0:T(8,128)(2,1)} %bitcast.52, bf16[2,2,512,256]{3,2,1,0:T(8,128)(2,1)} %bitcast.51, f32[2,2,512,512]{3,2,1,0:T(8,128)} %bitcast.47, ...), custom_call_target="tpu_custom_call" | custom-call | flops 1024 | bytes 1024 | tf_op jit(solution)/shard_map/attend_backward/pallas_call | solution.py:607
  537.0 10.8 %multiply_reduce_fusion = (f32[2048]{0:T(1024)}, bf16[2048,512]{0,1:T(8,128)(2,1)}) fusion(bf16[2048,512]{0,1:T(8,128)(2,1)S(1)} %copy-done.65, bf16[2048,2048]{1,0:T(8,128)(2,1)} %copy-done.10, bf16[2048,768]{1,0:T(8,128)(2,1)} %bitcast.59), kind=kOutput, calls=%fused_computation | convolution fusion | flops 4300208128 | bytes 14688256 | tf_op jit(solution)/shard_map/dot_general | solution.py:258
  591.4 17.8 %collective-permute-done.74 = bf16[128,2048]{1,0:T(8,128)(2,1)} collective-permute-done((bf16[128,2048]{1,0:T(8,128)(2,1)}, bf16[128,2048]{1,0:T(8,128)(2,1)}, u32[]{:S(2)}, u32[]{:S(2)}) %collective-permute-start.74) | collective-permute-done | bytes 524320 | tf_op jit(solution)/shard_map/ppermute | solution.py:18
  (459 shorter events, 303.2 us)
Async XLA Ops:
  7.2 83.6 %all-gather.6.cloned.1.call-start = ((), (), s32[]{:S(2)}) async-start(), calls=%async_computation.5 | async-start | bytes 2621440 | tf_op jit(solution)/shard_map/all_gather | solution.py:51
  21.1 100.4 %all-gather.8.cloned.1.call-start = ((), (), s32[]{:S(2)}) async-start(), calls=%async_computation.6 | async-start | bytes 2621440 | tf_op jit(solution)/shard_map/all_gather | solution.py:51
  43.1 140.0 %all-gather.10.cloned.1.call-start = ((), (), s32[]{:S(2)}) async-start(), calls=%async_computation.7 | async-start | bytes 3932160 | tf_op jit(solution)/shard_map/all_gather | solution.py:51
  88.5 30.6 %collective-permute-start.14 = (bf16[256,768]{1,0:T(8,128)(2,1)S(1)}, bf16[256,768]{1,0:T(8,128)(2,1)S(1)}, u32[]{:S(2)}, u32[]{:S(2)}) collective-permute-start(bf16[256,768]{1,0:T(8,128)(2,1)S(1)} %broadcast_select_fusion.15), channel_id=1, source_target_pairs={{0,4},{4,0},{8,12},{12,8},{16,20},{20,16},{24,28},{28,24},{1,5},{5... | collective-permute-start | bytes 1179656 | tf_op jit(solution)/shard_map/ppermute | solution.py:18
  90.2 29.0 %collective-permute-start.13 = (bf16[256,768]{1,0:T(8,128)(2,1)S(1)}, bf16[256,768]{1,0:T(8,128)(2,1)S(1)}, u32[]{:S(2)}, u32[]{:S(2)}) collective-permute-start(bf16[256,768]{1,0:T(8,128)(2,1)S(1)} %broadcast_select_fusion.19), channel_id=1, source_target_pairs={{0,4},{4,0},{8,12},{12,8},{16,20},{20,16},{24,28},{28,24},{1,5},{5... | collective-permute-start | bytes 1179656 | tf_op jit(solution)/shard_map/ppermute | solution.py:18
  119.2 152.1 %all-gather.12.cloned.1.call-start = ((), (), s32[]{:S(2)}) async-start(), calls=%async_computation.8 | async-start | bytes 3932160 | tf_op jit(solution)/shard_map/all_gather | solution.py:51
  143.0 167.4 %all-gather.14.cloned.1.call-start = ((), (), s32[]{:S(2)}) async-start(), calls=%async_computation.9 | async-start | bytes 3932160 | tf_op jit(solution)/shard_map/all_gather | solution.py:51
  215.9 183.6 %reduce-scatter.6.cloned.1.call-start = ((), (), s32[]{:S(2)}) async-start(), calls=%async_computation.10 | async-start | bytes 3932160 | tf_op jit(solution)/shard_map/reduce_scatter | solution.py:55
  240.6 26.9 %collective-permute-start.33 = (bf16[256,2048]{1,0:T(8,128)(2,1)}, bf16[256,2048]{1,0:T(8,128)(2,1)}, u32[]{:S(2)}, u32[]{:S(2)}) collective-permute-start(bf16[256,2048]{1,0:T(8,128)(2,1)} %fusion.13.refs_0_), channel_id=1, source_target_pairs={{0,4},{4,0},{8,12},{12,8},{16,20},{20,16},{24,28},{28,24},{1,5},{5... | collective-permute-start | bytes 3145736 | tf_op jit(solution)/shard_map/ppermute | solution.py:18
  309.7 130.3 %reduce-scatter.8.cloned.1.call-start = ((), (), s32[]{:S(2)}) async-start(), calls=%async_computation.11 | async-start | bytes 3932160 | tf_op jit(solution)/shard_map/reduce_scatter | solution.py:55
  357.8 176.0 %reduce-scatter.10.cloned.1.call-start = ((), (), s32[]{:S(2)}) async-start(), calls=%async_computation.12 | async-start | bytes 3932160 | tf_op jit(solution)/shard_map/reduce_scatter | solution.py:55
  369.5 30.0 %collective-permute-start.43 = (bf16[128,2048]{1,0:T(8,128)(2,1)}, bf16[128,2048]{1,0:T(8,128)(2,1)S(1)}, u32[]{:S(2)}, u32[]{:S(2)}) collective-permute-start(bf16[128,2048]{1,0:T(8,128)(2,1)} %get-tuple-element.142), channel_id=1, source_target_pairs={{0,2},{1,3},{2,0},{3,1},{4,6},{5,7},{6,4},{7,5},{8,10},{9,11},{10,... | collective-permute-start | bytes 1572872 | tf_op jit(solution)/shard_map/ppermute | solution.py:18
  370.1 29.4 %collective-permute-start.48 = (bf16[128,2048]{1,0:T(8,128)(2,1)}, bf16[128,2048]{1,0:T(8,128)(2,1)S(1)}, u32[]{:S(2)}, u32[]{:S(2)}) collective-permute-start(bf16[128,2048]{1,0:T(8,128)(2,1)} %get-tuple-element.152), channel_id=1, source_target_pairs={{0,4},{4,0},{8,12},{12,8},{16,20},{20,16},{24,28},{28,24},{1,5},{5... | collective-permute-start | bytes 1572872 | tf_op jit(solution)/shard_map/ppermute | solution.py:18
  406.9 184.5 %reduce-scatter.12.cloned.1.call-start = ((), (), s32[]{:S(2)}) async-start(), calls=%async_computation.13 | async-start | bytes 2621440 | tf_op jit(solution)/shard_map/reduce_scatter | solution.py:55
  407.0 36.8 %collective-permute-start.55 = (bf16[256,2048]{1,0:T(8,128)(2,1)S(1)}, bf16[256,2048]{1,0:T(8,128)(2,1)}, u32[]{:S(2)}, u32[]{:S(2)}) collective-permute-start(bf16[256,2048]{1,0:T(8,128)(2,1)S(1)} %get-tuple-element.226.refs_0_), channel_id=1, source_target_pairs={{0,1},{1,0},{2,3},{3,2},{4,5},{5,4},{6,7},{7,6},{8,9},{9,8},{10,11... | collective-permute-start | bytes 3145736 | tf_op jit(solution)/shard_map/ppermute | solution.py:18
  413.8 59.9 %collective-permute-start.50 = (bf16[768,2048]{1,0:T(8,128)(2,1)}, bf16[768,2048]{1,0:T(8,128)(2,1)}, u32[]{:S(2)}, u32[]{:S(2)}) collective-permute-start(bf16[768,2048]{1,0:T(8,128)(2,1)} %convolution_convert_fusion.4), channel_id=1, source_target_pairs={{0,1},{1,0},{2,3},{3,2},{4,5},{5,4},{6,7},{7,6},{8,9},{9,8},{10,11... | collective-permute-start | bytes 9437192 | tf_op jit(solution)/shard_map/ppermute | solution.py:18
  478.7 41.6 %collective-permute-start.60 = (bf16[128,2048]{1,0:T(8,128)(2,1)S(1)}, bf16[128,2048]{1,0:T(8,128)(2,1)}, u32[]{:S(2)}, u32[]{:S(2)}) collective-permute-start(bf16[128,2048]{1,0:T(8,128)(2,1)S(1)} %get-tuple-element.165), channel_id=1, source_target_pairs={{0,2},{1,3},{2,0},{3,1},{4,6},{5,7},{6,4},{7,5},{8,10},{9,11},{10,... | collective-permute-start | bytes 1572872 | tf_op jit(solution)/shard_map/ppermute | solution.py:18
  480.4 39.9 %collective-permute-start.61 = (bf16[128,2048]{1,0:T(8,128)(2,1)S(1)}, bf16[128,2048]{1,0:T(8,128)(2,1)}, u32[]{:S(2)}, u32[]{:S(2)}) collective-permute-start(bf16[128,2048]{1,0:T(8,128)(2,1)S(1)} %get-tuple-element.167), channel_id=1, source_target_pairs={{0,4},{4,0},{8,12},{12,8},{16,20},{20,16},{24,28},{28,24},{1,5},{5... | collective-permute-start | bytes 1572872 | tf_op jit(solution)/shard_map/ppermute | solution.py:18
  481.1 39.3 %collective-permute-start.63 = (bf16[128,2048]{1,0:T(8,128)(2,1)S(1)}, bf16[128,2048]{1,0:T(8,128)(2,1)}, u32[]{:S(2)}, u32[]{:S(2)}) collective-permute-start(bf16[128,2048]{1,0:T(8,128)(2,1)S(1)} %get-tuple-element.169), channel_id=1, source_target_pairs={{0,2},{1,3},{2,0},{3,1},{4,6},{5,7},{6,4},{7,5},{8,10},{9,11},{10,... | collective-permute-start | bytes 1572872 | tf_op jit(solution)/shard_map/ppermute | solution.py:18
  481.4 38.9 %collective-permute-start.65 = (bf16[128,2048]{1,0:T(8,128)(2,1)S(1)}, bf16[128,2048]{1,0:T(8,128)(2,1)}, u32[]{:S(2)}, u32[]{:S(2)}) collective-permute-start(bf16[128,2048]{1,0:T(8,128)(2,1)S(1)} %get-tuple-element.176), channel_id=1, source_target_pairs={{0,4},{4,0},{8,12},{12,8},{16,20},{20,16},{24,28},{28,24},{1,5},{5... | collective-permute-start | bytes 1572872 | tf_op jit(solution)/shard_map/ppermute | solution.py:18
  493.9 118.8 %reduce-scatter.14.cloned.1.call-start = ((), (), s32[]{:S(2)}) async-start(), calls=%async_computation.14 | async-start | bytes 2621440 | tf_op jit(solution)/shard_map/reduce_scatter | solution.py:55
  526.8 42.2 %collective-permute-start.69 = (bf16[768,2048]{1,0:T(8,128)(2,1)}, bf16[768,2048]{1,0:T(8,128)(2,1)S(1)}, u32[]{:S(2)}, u32[]{:S(2)}) collective-permute-start(bf16[768,2048]{1,0:T(8,128)(2,1)} %convolution_convert_fusion.3), channel_id=1, source_target_pairs={{0,1},{1,0},{2,3},{3,2},{4,5},{5,4},{6,7},{7,6},{8,9},{9,8},{10,11... | collective-permute-start | bytes 9437192 | tf_op jit(solution)/shard_map/ppermute | solution.py:18
  575.2 34.0 %collective-permute-start.70 = (bf16[128,2048]{1,0:T(8,128)(2,1)}, bf16[128,2048]{1,0:T(8,128)(2,1)}, u32[]{:S(2)}, u32[]{:S(2)}) collective-permute-start(bf16[128,2048]{1,0:T(8,128)(2,1)} %get-tuple-element.185), channel_id=1, source_target_pairs={{0,2},{1,3},{2,0},{3,1},{4,6},{5,7},{6,4},{7,5},{8,10},{9,11},{10,... | collective-permute-start | bytes 1572872 | tf_op jit(solution)/shard_map/ppermute | solution.py:18
  575.6 33.6 %collective-permute-start.79 = (bf16[128,2048]{1,0:T(8,128)(2,1)}, bf16[128,2048]{1,0:T(8,128)(2,1)}, u32[]{:S(2)}, u32[]{:S(2)}) collective-permute-start(bf16[128,2048]{1,0:T(8,128)(2,1)} %get-tuple-element.192), channel_id=1, source_target_pairs={{0,4},{4,0},{8,12},{12,8},{16,20},{20,16},{24,28},{28,24},{1,5},{5... | collective-permute-start | bytes 1572872 | tf_op jit(solution)/shard_map/ppermute | solution.py:18
  (142 other events, 1614.3 us)
Sparse Core Ops, SparseCore 0:
  21.2 47.3 all-gather.5
  70.8 44.7 all-gather.7
  119.3 63.7 all-gather.9
  184.6 62.1 all-gather.11
  248.2 62.1 all-gather.13
  312.5 58.8 reduce-scatter.5
  373.8 60.2 reduce-scatter.7
  436.4 60.2 reduce-scatter.9
  499.0 43.8 reduce-scatter.11
  547.9 44.3 reduce-scatter.13

commit v6 on v5

--- a/solution.py
+++ b/solution.py
@@ -781,14 +781,14 @@
         dot_rows(qkv_part, qkv_full) + dot_rows(gate_attn_part, gate_full)
     ) / attn_gain
     up_swap = swap_rows(hold(up_sum, one_send), odd, members)
-    added_one = open_sum(one_parts, members, shares, qkv_part, ffn_branch)
+    added_one = open_sum(one_parts, members, shares, qkv_part)
     gain_parts = hold(
         jnp.concatenate([attn_gain_part, mlp_gain_part, gain_parts[0], gain_parts[1]]), added_one
     )
     gain_parts = sum_everywhere(gain_parts, "fsdp", 2, members)
     gain_parts = sum_everywhere(gain_parts, "tensor", 1, 2)
     norm_one_grad = close_sum(
-        *send_sum(added_one, members, shares), members, shares, gate_out_sum, gain_parts, up_swap
+        *send_sum(added_one, members, shares), members, shares, gate_out_sum, gain_parts, up_swap, output
     )
     gain_totals = hold(gain_parts, norm_one_grad)
     gain_totals = sum_everywhere(gain_totals, "tensor", 2, shares)
@@ -799,17 +799,7 @@
     gate_out_swap = swap_rows(hold(gate_out_sum, norm_one_grad, qkv_sum), odd, members)
     (up_shard,) = own_shard(*up_swap, odd, (units,))
     gate_attn_shard, out_shard = own_shard(*gate_out_swap, odd, (query_width,) * 2)
-    qkv_sum = hold(
-        qkv_sum,
-        norm_one_grad,
-        gain_totals,
-        output,
-        down_shard,
-        gate_shard,
-        up_shard,
-        gate_attn_shard,
-        out_shard,
-    )
+    qkv_sum = hold(qkv_sum, norm_one_grad)
     query_shard, key_shard, value_shard = own_shard(
         *swap_rows(qkv_sum, odd, members), odd, (query_width, key_width, key_width)
     )

time: 645 us -> 631 us (0.978)
  waiting for transfers between devices: 232 us -> 223 us
    ppermute x84, waiting for transfers between devices: 222 us -> 214 us  [exchange(): return lax.ppermute(values, axis, [(i, i ^ mask) for i in range(size)])]
  transfers between devices with their start and end apart: 94 -> 94, of which waited for: 34 -> 34; matrix products, arithmetic and copies ran while one was open for 26% -> 25% of each run, Pallas kernels for 18% -> 19%
where the time goes in v6:
time: 631 us; the launch traced here: 628 us
  waiting for transfers between devices  223 us (35%)
  Pallas kernels  120 us (19%)
  matrix products  92.3 us (15%)
  starting transfers between devices  72 us (11%)
  local copies, waits for them, and re-layouts  52.4 us (8%)
  other arithmetic  51.7 us (8%)
  between operations  16.2 us (3%)
    ppermute x84, waiting for transfers between devices, exchange(): return lax.ppermute(values, axis, [(i, i ^ mask) for i in range(size)])  214 us
    ppermute x84, starting transfers between devices, exchange(): return lax.ppermute(values, axis, [(i, i ^ mask) for i in range(size)])  70.3 us
    dot_general x6, matrix products, matmul_tn(): lax.dot_general(first_op, second_op, (((0,), (0,)), ((), ())), preferred_...  38 us
    unnamed x157, local copies, waits for them, and re-layouts  37.9 us
    pallas_call x1, Pallas kernels, unit_grads(): pl.pallas_call(functools.partial(unit_grads_kernel, 4, 3), grid=(8,), in_...  34.8 us
    dot_general x9, matrix products, matmul_nt(): lax.dot_general(first_op, second_op, (((1,), (1,)), ((), ())), preferred_...  31.5 us
    pallas_call x1, Pallas kernels, attend_backward(): pl.pallas_call(functools.partial(attend_backward_kernel, masks, head_size...  23.2 us
    dot_general x3, matrix products, matmul(): return jnp.dot(first_op, second_op, preferred_element_type=F32)  22.9 us
  transfers between devices with their start and end apart: 94, of which 34 were waited for; matrix products, arithmetic and copies ran while one was open for 25% of the time, Pallas kernels for 19%

profile of v6, /device:TPU:0, one launch (start us, length us, event | category | flops | bytes accessed | tf_op | source)
XLA Modules:
  0.0 627.7 jit_solution(2129028584663651587)
XLA Ops:
  31.9 7.6 %collective-permute-done.2 = bf16[256,768]{1,0:T(8,128)(2,1)S(1)} collective-permute-done((bf16[256,768]{1,0:T(8,128)(2,1)S(1)}, bf16[256,768]{1,0:T(8,128)(2,1)S(1)}, u32[]{:S(2)}, u32[]{:S(2)}) %collective-permute-start.2) | collective-permute-done | bytes 393248 | tf_op jit(solution)/shard_map/ppermute | solution.py:18
  43.4 20.0 %collective-permute-done.3.refs_1_ = bf16[256,2048]{1,0:T(8,128)(2,1)S(1)} collective-permute-done((bf16[256,2048]{1,0:T(8,128)(2,1)S(1)}, bf16[256,2048]{1,0:T(8,128)(2,1)S(1)}, u32[]{:S(2)}, u32[]{:S(2)}) %collective-permute-start.3) | collective-permute-done | bytes 1048608 | tf_op jit(solution)/shard_map/ppermute | solution.py:18
  67.6 7.4 %collective-permute-done = s32[1]{0:T(128)} collective-permute-done((s32[1]{0:T(128)}, s32[1]{0:T(128)}, u32[]{:S(2)}, u32[]{:S(2)}) %collective-permute-start) | collective-permute-done | bytes 36 | tf_op jit(solution)/shard_map/ppermute | solution.py:18
  90.8 10.6 %fusion.39 = f32[2048,512]{1,0:T(8,128)} fusion(bf16[2048,2048]{1,0:T(8,128)(2,1)} %copy-done.10, bf16[2048,512]{0,1:T(8,128)(2,1)} %all-gather.6.cloned.1.call-done), kind=kOutput, calls=%fused_computation.165 | convolution fusion | flops 4294967296 | bytes 14680064 | tf_op jit(solution)/shard_map/dot_general | solution.py:254
  101.4 17.8 %attend_forward.1 = (f32[2,2,512,256]{3,2,1,0:T(8,128)}, f32[2,1024,256]{2,1,0:T(8,128)}, bf16[2,1024,256]{2,1,0:T(8,128)(2,1)}, bf16[2,1024,128]{2,1,0:T(8,128)(2,1)}, bf16[2,1024,128]{2,1,0:T(8,128)(2,1)}) custom-call(s32[1]{0:T(128)} %bitcast.share_ref, s32[2]{0:T(128)} %pad_add_fusion.length_ref, f32[2,2,512,512]{3,2,1,0:T(8,128)} %bitcast.46, ...), custom_call_target="tpu_custom_call" | custom-call | flops 1024 | bytes 1024 | tf_op jit(solution)/shard_map/attend_forward/pallas_call | solution.py:582
  121.6 8.4 %multiply_convert_fusion.4 = (bf16[2048,256]{1,0:T(8,128)(2,1)S(1)}, f32[2048,256]{1,0:T(8,128)}) fusion(f32[2,2,512,256]{3,2,1,0:T(8,128)} %get-tuple-element.109, bf16[2048,2048]{1,0:T(8,128)(2,1)} %copy-done.10, bf16[2048,512]{0,1:T(8,128)(2,1)} %all-gather.8.cloned.1.call-done), kind=kOutput, calls=%fused_computation.48 | convolution fusion | flops 2150105088 | bytes 14680064 | tf_op jit(solution)/shard_map/dot_general | solution.py:254
  148.5 7.5 %collective-permute-done.20 = bf16[128,2048]{1,0:T(8,128)(2,1)} collective-permute-done((bf16[128,2048]{1,0:T(8,128)(2,1)}, bf16[128,2048]{1,0:T(8,128)(2,1)}, u32[]{:S(2)}, u32[]{:S(2)}) %collective-permute-start.20) | collective-permute-done | bytes 524320 | tf_op jit(solution)/shard_map/ppermute | solution.py:18
  161.6 10.6 %collective-permute-done.21 = bf16[128,2048]{1,0:T(8,128)(2,1)S(1)} collective-permute-done((bf16[128,2048]{1,0:T(8,128)(2,1)S(1)}, bf16[128,2048]{1,0:T(8,128)(2,1)S(1)}, u32[]{:S(2)}, u32[]{:S(2)}) %collective-permute-start.21) | collective-permute-done | bytes 524320 | tf_op jit(solution)/shard_map/ppermute | solution.py:18
  173.9 9.3 %all-gather.10.cloned.1.call-done.gate_weights_ref = bf16[2048,768]{1,0:T(8,128)(2,1)} async-done(((bf16[512,768]{1,0:T(8,128)(2,1)}), bf16[2048,768]{1,0:T(8,128)(2,1)}) %all-gather.10.cloned.1.call-update) | async-done | bytes 3145744 | tf_op jit(solution)/shard_map/all_gather | solution.py:51
  188.8 21.9 %collective-permute-done.23.refs_1_ = bf16[256,2048]{1,0:T(8,128)(2,1)S(1)} collective-permute-done((bf16[256,2048]{1,0:T(8,128)(2,1)S(1)}, bf16[256,2048]{1,0:T(8,128)(2,1)S(1)}, u32[]{:S(2)}, u32[]{:S(2)}) %collective-permute-start.23) | collective-permute-done | bytes 1048608 | tf_op jit(solution)/shard_map/ppermute | solution.py:18
  216.2 8.5 %collective-permute-done.25.refs_3_ = bf16[128,2048]{1,0:T(8,128)(2,1)} collective-permute-done((bf16[128,2048]{1,0:T(8,128)(2,1)}, bf16[128,2048]{1,0:T(8,128)(2,1)}, u32[]{:S(2)}, u32[]{:S(2)}) %collective-permute-start.25) | collective-permute-done | bytes 524320 | tf_op jit(solution)/shard_map/ppermute | solution.py:18
  241.2 23.9 %collective-permute-done.32.refs_1_ = bf16[256,2048]{1,0:T(8,128)(2,1)} collective-permute-done((bf16[256,2048]{1,0:T(8,128)(2,1)}, bf16[256,2048]{1,0:T(8,128)(2,1)}, u32[]{:S(2)}, u32[]{:S(2)}) %collective-permute-start.32) | collective-permute-done | bytes 1048608 | tf_op jit(solution)/shard_map/ppermute | solution.py:18
  273.2 15.7 %hidden_units.1 = (f32[2048,768]{1,0:T(8,128)S(1)}, f32[2048,768]{1,0:T(8,128)S(1)}, bf16[2048,768]{1,0:T(8,128)(2,1)S(1)}) custom-call(bf16[2048,2048]{1,0:T(8,128)(2,1)} %copy-done.2, bf16[2048,768]{1,0:T(8,128)(2,1)S(1)} %copy-done.8, bf16[2048,768]{1,0:T(8,128)(2,1)S(1)} %copy-done.9), custom_call_target="tpu_custom_call" | custom-call | flops 1024 | bytes 1024 | tf_op jit(solution)/shard_map/hidden_units/pallas_call | solution.py:475
  301.5 8.2 %convolution_convert_fusion.8 = bf16[2048,768]{1,0:T(8,128)(2,1)} fusion(bf16[2048,2048]{1,0:T(8,128)(2,1)S(1)} %stack_rows.6.branch_ref, bf16[2048,768]{1,0:T(8,128)(2,1)S(1)} %get-tuple-element.153), kind=kOutput, calls=%fused_computation.9 | convolution fusion | flops 6444023808 | bytes 14680064 | tf_op jit(solution)/shard_map/dot_general | solution.py:258
  310.4 34.8 %unit_grads.1 = (bf16[2048,768]{1,0:T(8,128)(2,1)S(1)}, bf16[2048,768]{1,0:T(8,128)(2,1)S(1)}, bf16[1024,2048]{1,0:T(8,128)(2,1)}, bf16[768,2048]{1,0:T(8,128)(2,1)}, bf16[256,2048]{1,0:T(8,128)(2,1)}) custom-call(bf16[2048,2048]{1,0:T(8,128)(2,1)} %copy-done.3, f32[2048,768]{1,0:T(8,128)} %copy-done.11, f32[2048,768]{1,0:T(8,128)} %copy-done.12, ...), custom_call_target="tpu_custom_call" | custom-call | flops 1024 | bytes 1024 | tf_op jit(solution)/shard_map/unit_grads/pallas_call | solution.py:533
  347.4 10.4 %convolution_convert_fusion.7 = bf16[2048,768]{1,0:T(8,128)(2,1)} fusion(bf16[2048,2048]{1,0:T(8,128)(2,1)} %copy-done.2, bf16[2048,768]{1,0:T(8,128)(2,1)S(1)} %get-tuple-element.139), kind=kOutput, calls=%fused_computation.8 | convolution fusion | flops 6444023808 | bytes 14680064 | tf_op jit(solution)/shard_map/dot_general | solution.py:258
  381.6 8.6 %convolution_convert_fusion.6 = bf16[2048,768]{1,0:T(8,128)(2,1)} fusion(bf16[2048,2048]{1,0:T(8,128)(2,1)S(1)} %bitcast.41, bf16[2048,768]{1,0:T(8,128)(2,1)S(1)} %copy-done.32), kind=kOutput, calls=%fused_computation.7 | convolution fusion | flops 6444023808 | bytes 14680064 | tf_op jit(solution)/shard_map/dot_general | solution.py:258
  390.2 9.4 %collective-permute-done.47 = bf16[128,2048]{1,0:T(8,128)(2,1)} collective-permute-done((bf16[128,2048]{1,0:T(8,128)(2,1)}, bf16[128,2048]{1,0:T(8,128)(2,1)}, u32[]{:S(2)}, u32[]{:S(2)}) %collective-permute-start.47) | collective-permute-done | bytes 524320 | tf_op jit(solution)/shard_map/ppermute | solution.py:18
  407.1 6.7 %convolution_convert_fusion.4 = bf16[768,2048]{1,0:T(8,128)(2,1)} fusion(bf16[2048,768]{1,0:T(8,128)(2,1)} %all-gather.14.cloned.1.call-done.down_weights_ref, bf16[2048,768]{1,0:T(8,128)(2,1)} %copy-done.29), kind=kOutput, calls=%fused_computation.5 | convolution fusion | flops 2417491968 | bytes 7471104 | tf_op jit(solution)/shard_map/dot_general | solution.py:264
  414.3 14.2 %collective-permute-done.51.refs_1_ = bf16[256,2048]{1,0:T(8,128)(2,1)S(1)} collective-permute-done((bf16[256,2048]{1,0:T(8,128)(2,1)S(1)}, bf16[256,2048]{1,0:T(8,128)(2,1)S(1)}, u32[]{:S(2)}, u32[]{:S(2)}) %collective-permute-start.51) | collective-permute-done | bytes 1048608 | tf_op jit(solution)/shard_map/ppermute | solution.py:18
  457.6 7.6 %collective-permute-done.66 = bf16[256,768]{1,0:T(8,128)(2,1)S(1)} collective-permute-done((bf16[256,768]{1,0:T(8,128)(2,1)S(1)}, bf16[256,768]{1,0:T(8,128)(2,1)S(1)}, u32[]{:S(2)}, u32[]{:S(2)}) %collective-permute-start.66) | collective-permute-done | bytes 393248 | tf_op jit(solution)/shard_map/ppermute | solution.py:18
  493.5 23.2 %attend_backward.1 = (bf16[2,2,512,768]{3,2,1,0:T(8,128)(2,1)}, f32[8,128]{1,0:T(8,128)}) custom-call(s32[1]{0:T(128)} %bitcast.share_ref, s32[2]{0:T(128)} %pad_add_fusion.length_ref, bf16[2,2,512,256]{3,2,1,0:T(8,128)(2,1)} %bitcast.54, bf16[2,2,512,256]{3,2,1,0:T(8,128)(2,1)} %bitcast.53, f32[2,2,512,512]{3,2,1,0:T(8,128)} %bitcast.49, ...), custom_call_target="tpu_custom_call" | custom-call | flops 1024 | bytes 1024 | tf_op jit(solution)/shard_map/attend_backward/pallas_call | solution.py:607
  517.6 6.4 %convolution_convert_fusion.3 = bf16[768,2048]{1,0:T(8,128)(2,1)} fusion(bf16[2048,768]{1,0:T(8,128)(2,1)} %bitcast.60, bf16[2048,256]{0,1:T(8,128)(2,1)S(1)} %copy-done.53, bf16[2048,512]{0,1:T(8,128)(2,1)} %all-gather.6.cloned.1.call-done), kind=kOutput, calls=%fused_computation.4 | convolution fusion | flops 2423783424 | bytes 7471104 | tf_op jit(solution)/shard_map/dot_general | solution.py:264
  578.6 16.2 %collective-permute-done.74 = bf16[128,2048]{1,0:T(8,128)(2,1)} collective-permute-done((bf16[128,2048]{1,0:T(8,128)(2,1)}, bf16[128,2048]{1,0:T(8,128)(2,1)}, u32[]{:S(2)}, u32[]{:S(2)}) %collective-permute-start.74) | collective-permute-done | bytes 524320 | tf_op jit(solution)/shard_map/ppermute | solution.py:18
  (460 shorter events, 296.6 us)
Async XLA Ops:
  7.2 83.6 %all-gather.6.cloned.1.call-start = ((), (), s32[]{:S(2)}) async-start(), calls=%async_computation.5 | async-start | bytes 2621440 | tf_op jit(solution)/shard_map/all_gather | solution.py:51
  21.1 100.5 %all-gather.8.cloned.1.call-start = ((), (), s32[]{:S(2)}) async-start(), calls=%async_computation.6 | async-start | bytes 2621440 | tf_op jit(solution)/shard_map/all_gather | solution.py:51
  43.1 140.1 %all-gather.10.cloned.1.call-start = ((), (), s32[]{:S(2)}) async-start(), calls=%async_computation.7 | async-start | bytes 3932160 | tf_op jit(solution)/shard_map/all_gather | solution.py:51
  88.6 30.6 %collective-permute-start.14 = (bf16[256,768]{1,0:T(8,128)(2,1)S(1)}, bf16[256,768]{1,0:T(8,128)(2,1)S(1)}, u32[]{:S(2)}, u32[]{:S(2)}) collective-permute-start(bf16[256,768]{1,0:T(8,128)(2,1)S(1)} %broadcast_select_fusion.15), channel_id=1, source_target_pairs={{0,4},{4,0},{8,12},{12,8},{16,20},{20,16},{24,28},{28,24},{1,5},{5... | collective-permute-start | bytes 1179656 | tf_op jit(solution)/shard_map/ppermute | solution.py:18
  90.2 29.0 %collective-permute-start.13 = (bf16[256,768]{1,0:T(8,128)(2,1)S(1)}, bf16[256,768]{1,0:T(8,128)(2,1)S(1)}, u32[]{:S(2)}, u32[]{:S(2)}) collective-permute-start(bf16[256,768]{1,0:T(8,128)(2,1)S(1)} %broadcast_select_fusion.19), channel_id=1, source_target_pairs={{0,4},{4,0},{8,12},{12,8},{16,20},{20,16},{24,28},{28,24},{1,5},{5... | collective-permute-start | bytes 1179656 | tf_op jit(solution)/shard_map/ppermute | solution.py:18
  119.3 152.1 %all-gather.12.cloned.1.call-start = ((), (), s32[]{:S(2)}) async-start(), calls=%async_computation.8 | async-start | bytes 3932160 | tf_op jit(solution)/shard_map/all_gather | solution.py:51
  143.0 167.4 %all-gather.14.cloned.1.call-start = ((), (), s32[]{:S(2)}) async-start(), calls=%async_computation.9 | async-start | bytes 3932160 | tf_op jit(solution)/shard_map/all_gather | solution.py:51
  215.9 183.6 %reduce-scatter.6.cloned.1.call-start = ((), (), s32[]{:S(2)}) async-start(), calls=%async_computation.10 | async-start | bytes 3932160 | tf_op jit(solution)/shard_map/reduce_scatter | solution.py:55
  240.6 26.9 %collective-permute-start.33 = (bf16[256,2048]{1,0:T(8,128)(2,1)}, bf16[256,2048]{1,0:T(8,128)(2,1)}, u32[]{:S(2)}, u32[]{:S(2)}) collective-permute-start(bf16[256,2048]{1,0:T(8,128)(2,1)} %fusion.13.refs_0_), channel_id=1, source_target_pairs={{0,4},{4,0},{8,12},{12,8},{16,20},{20,16},{24,28},{28,24},{1,5},{5... | collective-permute-start | bytes 3145736 | tf_op jit(solution)/shard_map/ppermute | solution.py:18
  309.8 130.2 %reduce-scatter.8.cloned.1.call-start = ((), (), s32[]{:S(2)}) async-start(), calls=%async_computation.11 | async-start | bytes 3932160 | tf_op jit(solution)/shard_map/reduce_scatter | solution.py:55
  357.9 159.7 %reduce-scatter.10.cloned.1.call-start = ((), (), s32[]{:S(2)}) async-start(), calls=%async_computation.12 | async-start | bytes 3932160 | tf_op jit(solution)/shard_map/reduce_scatter | solution.py:55
  369.6 30.0 %collective-permute-start.43 = (bf16[128,2048]{1,0:T(8,128)(2,1)}, bf16[128,2048]{1,0:T(8,128)(2,1)S(1)}, u32[]{:S(2)}, u32[]{:S(2)}) collective-permute-start(bf16[128,2048]{1,0:T(8,128)(2,1)} %get-tuple-element.142), channel_id=1, source_target_pairs={{0,2},{1,3},{2,0},{3,1},{4,6},{5,7},{6,4},{7,5},{8,10},{9,11},{10,... | collective-permute-start | bytes 1572872 | tf_op jit(solution)/shard_map/ppermute | solution.py:18
  370.1 29.5 %collective-permute-start.48 = (bf16[128,2048]{1,0:T(8,128)(2,1)}, bf16[128,2048]{1,0:T(8,128)(2,1)S(1)}, u32[]{:S(2)}, u32[]{:S(2)}) collective-permute-start(bf16[128,2048]{1,0:T(8,128)(2,1)} %get-tuple-element.152), channel_id=1, source_target_pairs={{0,4},{4,0},{8,12},{12,8},{16,20},{20,16},{24,28},{28,24},{1,5},{5... | collective-permute-start | bytes 1572872 | tf_op jit(solution)/shard_map/ppermute | solution.py:18
  407.0 171.6 %reduce-scatter.12.cloned.1.call-start = ((), (), s32[]{:S(2)}) async-start(), calls=%async_computation.13 | async-start | bytes 2621440 | tf_op jit(solution)/shard_map/reduce_scatter | solution.py:55
  407.0 36.9 %collective-permute-start.55 = (bf16[256,2048]{1,0:T(8,128)(2,1)S(1)}, bf16[256,2048]{1,0:T(8,128)(2,1)}, u32[]{:S(2)}, u32[]{:S(2)}) collective-permute-start(bf16[256,2048]{1,0:T(8,128)(2,1)S(1)} %get-tuple-element.224.refs_0_), channel_id=1, source_target_pairs={{0,1},{1,0},{2,3},{3,2},{4,5},{5,4},{6,7},{7,6},{8,9},{9,8},{10,11... | collective-permute-start | bytes 3145736 | tf_op jit(solution)/shard_map/ppermute | solution.py:18
  413.8 52.9 %collective-permute-start.50 = (bf16[768,2048]{1,0:T(8,128)(2,1)}, bf16[768,2048]{1,0:T(8,128)(2,1)}, u32[]{:S(2)}, u32[]{:S(2)}) collective-permute-start(bf16[768,2048]{1,0:T(8,128)(2,1)} %convolution_convert_fusion.4), channel_id=1, source_target_pairs={{0,1},{1,0},{2,3},{3,2},{4,5},{5,4},{6,7},{7,6},{8,9},{9,8},{10,11... | collective-permute-start | bytes 9437192 | tf_op jit(solution)/shard_map/ppermute | solution.py:18
  456.1 27.8 %collective-permute-start.67 = (bf16[256,768]{1,0:T(8,128)(2,1)S(1)}, bf16[256,768]{1,0:T(8,128)(2,1)}, u32[]{:S(2)}, u32[]{:S(2)}) collective-permute-start(bf16[256,768]{1,0:T(8,128)(2,1)S(1)} %broadcast_select_fusion.8), channel_id=1, source_target_pairs={{0,4},{4,0},{8,12},{12,8},{16,20},{20,16},{24,28},{28,24},{1,5},{5... | collective-permute-start | bytes 1179656 | tf_op jit(solution)/shard_map/ppermute | solution.py:18
  483.9 114.4 %reduce-scatter.14.cloned.1.call-start = ((), (), s32[]{:S(2)}) async-start(), calls=%async_computation.14 | async-start | bytes 2621440 | tf_op jit(solution)/shard_map/reduce_scatter | solution.py:55
  484.0 33.5 %collective-permute-start.60 = (bf16[128,2048]{1,0:T(8,128)(2,1)S(1)}, bf16[128,2048]{1,0:T(8,128)(2,1)}, u32[]{:S(2)}, u32[]{:S(2)}) collective-permute-start(bf16[128,2048]{1,0:T(8,128)(2,1)S(1)} %get-tuple-element.165), channel_id=1, source_target_pairs={{0,2},{1,3},{2,0},{3,1},{4,6},{5,7},{6,4},{7,5},{8,10},{9,11},{10,... | collective-permute-start | bytes 1572872 | tf_op jit(solution)/shard_map/ppermute | solution.py:18
  485.7 31.8 %collective-permute-start.61 = (bf16[128,2048]{1,0:T(8,128)(2,1)S(1)}, bf16[128,2048]{1,0:T(8,128)(2,1)}, u32[]{:S(2)}, u32[]{:S(2)}) collective-permute-start(bf16[128,2048]{1,0:T(8,128)(2,1)S(1)} %get-tuple-element.167), channel_id=1, source_target_pairs={{0,4},{4,0},{8,12},{12,8},{16,20},{20,16},{24,28},{28,24},{1,5},{5... | collective-permute-start | bytes 1572872 | tf_op jit(solution)/shard_map/ppermute | solution.py:18
  487.4 30.2 %collective-permute-start.63 = (bf16[128,2048]{1,0:T(8,128)(2,1)S(1)}, bf16[128,2048]{1,0:T(8,128)(2,1)}, u32[]{:S(2)}, u32[]{:S(2)}) collective-permute-start(bf16[128,2048]{1,0:T(8,128)(2,1)S(1)} %get-tuple-element.169), channel_id=1, source_target_pairs={{0,2},{1,3},{2,0},{3,1},{4,6},{5,7},{6,4},{7,5},{8,10},{9,11},{10,... | collective-permute-start | bytes 1572872 | tf_op jit(solution)/shard_map/ppermute | solution.py:18
  487.7 29.8 %collective-permute-start.65 = (bf16[128,2048]{1,0:T(8,128)(2,1)S(1)}, bf16[128,2048]{1,0:T(8,128)(2,1)}, u32[]{:S(2)}, u32[]{:S(2)}) collective-permute-start(bf16[128,2048]{1,0:T(8,128)(2,1)S(1)} %get-tuple-element.176), channel_id=1, source_target_pairs={{0,4},{4,0},{8,12},{12,8},{16,20},{20,16},{24,28},{28,24},{1,5},{5... | collective-permute-start | bytes 1572872 | tf_op jit(solution)/shard_map/ppermute | solution.py:18
  564.1 30.7 %collective-permute-start.70 = (bf16[128,2048]{1,0:T(8,128)(2,1)}, bf16[128,2048]{1,0:T(8,128)(2,1)}, u32[]{:S(2)}, u32[]{:S(2)}) collective-permute-start(bf16[128,2048]{1,0:T(8,128)(2,1)} %get-tuple-element.185), channel_id=1, source_target_pairs={{0,2},{1,3},{2,0},{3,1},{4,6},{5,7},{6,4},{7,5},{8,10},{9,11},{10,... | collective-permute-start | bytes 1572872 | tf_op jit(solution)/shard_map/ppermute | solution.py:18
  564.5 30.3 %collective-permute-start.79 = (bf16[128,2048]{1,0:T(8,128)(2,1)}, bf16[128,2048]{1,0:T(8,128)(2,1)}, u32[]{:S(2)}, u32[]{:S(2)}) collective-permute-start(bf16[128,2048]{1,0:T(8,128)(2,1)} %get-tuple-element.192), channel_id=1, source_target_pairs={{0,4},{4,0},{8,12},{12,8},{16,20},{20,16},{24,28},{28,24},{1,5},{5... | collective-permute-start | bytes 1572872 | tf_op jit(solution)/shard_map/ppermute | solution.py:18
  (142 other events, 1677.9 us)
Sparse Core Ops, SparseCore 0:
  21.2 47.3 all-gather.5
  70.8 44.7 all-gather.7
  119.4 63.8 all-gather.9
  184.7 62.1 all-gather.11
  248.2 62.1 all-gather.13
  312.6 58.8 reduce-scatter.5
  373.8 60.2 reduce-scatter.7
  436.4 60.2 reduce-scatter.9
  499.1 43.8 reduce-scatter.11
  545.2 44.0 reduce-scatter.13

commit v7 on v6

--- a/solution.py
+++ b/solution.py
@@ -486,7 +486,6 @@
 
 def unit_grads_kernel(
     near_steps,
-    far_steps,
     branch_ref,
     gate_ref,
     up_ref,
@@ -510,45 +509,49 @@
     back = matmul_nt(gate_grad, gate_weights_ref[...]) + matmul_nt(up_grad, up_weights_ref[...])
     back = back.astype(BF16)
 
+    rows = back.shape[0]
+    half = rows // 2
+
     @pl.when(step < near_steps)
     def _():
         near_ref[...] = back
 
-    @pl.when((step >= near_steps) & (step < near_steps + far_steps))
+    @pl.when(step == near_steps)
     def _():
-        far_ref[...] = back
-
-    @pl.when(step == near_steps + far_steps)
+        far_ref[:rows, :] = back
+
+    @pl.when(step == near_steps + 1)
     def _():
-        corner_ref[...] = back
+        far_ref[rows:, :] = back[:half]
+        corner_ref[...] = back[half:]
 
 
 def unit_grads(branch, ffn_gate, ffn_up, down_weights, gate_weights, up_weights):
     rows, width = branch.shape
     units = ffn_gate.shape[1]
-    tile = rows // 8
+    tile = rows // 4
     tokens = pl.BlockSpec((tile, width), lambda i: (i, 0))
     hidden = pl.BlockSpec((tile, units), lambda i: (i, 0))
     weight = pl.BlockSpec((width, units), lambda i: (0, 0), pipeline_mode=pl.Buffered(1))
     gate_grad, up_grad, *parts = pl.pallas_call(
-        functools.partial(unit_grads_kernel, 4, 3),
-        grid=(8,),
+        functools.partial(unit_grads_kernel, 2),
+        grid=(4,),
         in_specs=[tokens, hidden, hidden, weight, weight, weight],
         out_specs=[
             hidden,
             hidden,
-            pl.BlockSpec((tile, width), lambda i: (jnp.minimum(i, 3), 0)),
-            pl.BlockSpec((tile, width), lambda i: (jnp.clip(i - 4, 0, 2), 0)),
-            pl.BlockSpec((tile, width), lambda i: (0, 0)),
+            pl.BlockSpec((tile, width), lambda i: (jnp.minimum(i, 1), 0)),
+            pl.BlockSpec((3 * tile // 2, width), lambda i: (0, 0)),
+            pl.BlockSpec((tile // 2, width), lambda i: (0, 0)),
         ],
         out_shape=[
             jax.ShapeDtypeStruct((rows, units), BF16),
             jax.ShapeDtypeStruct((rows, units), BF16),
-            jax.ShapeDtypeStruct((4 * tile, width), BF16),
-            jax.ShapeDtypeStruct((3 * tile, width), BF16),
-            jax.ShapeDtypeStruct((tile, width), BF16),
-        ],
-        compiler_params=pltpu.CompilerParams(vmem_limit_bytes=44 << 20),
+            jax.ShapeDtypeStruct((2 * tile, width), BF16),
+            jax.ShapeDtypeStruct((3 * tile // 2, width), BF16),
+            jax.ShapeDtypeStruct((tile // 2, width), BF16),
+        ],
+        compiler_params=pltpu.CompilerParams(vmem_limit_bytes=58 << 20),
         cost_estimate=light_cost(),
         name="unit_grads",
     )(branch, ffn_gate, ffn_up, down_weights, gate_weights, up_weights)

time: 631 us -> 632 us (level)
    unnamed x157 -> x155, local copies, waits for them, and re-layouts: 37.9 us -> 36.2 us
where the time goes in v7:
time: 632 us; the launch traced here: 629 us
  waiting for transfers between devices  228 us (36%)
  Pallas kernels  121 us (19%)
  matrix products  93.6 us (15%)
  starting transfers between devices  66.9 us (11%)
  other arithmetic  51.9 us (8%)
  local copies, waits for them, and re-layouts  50.7 us (8%)
  between operations  16.3 us (3%)
    ppermute x84, waiting for transfers between devices, exchange(): return lax.ppermute(values, axis, [(i, i ^ mask) for i in range(size)])  218 us
    ppermute x84, starting transfers between devices, exchange(): return lax.ppermute(values, axis, [(i, i ^ mask) for i in range(size)])  65.3 us
    dot_general x6, matrix products, matmul_tn(): lax.dot_general(first_op, second_op, (((0,), (0,)), ((), ())), preferred_...  39.1 us
    unnamed x155, local copies, waits for them, and re-layouts  36.2 us
    pallas_call x1, Pallas kernels, unit_grads(): pl.pallas_call(functools.partial(unit_grads_kernel, 2), grid=(4,), in_spe...  36 us
    dot_general x9, matrix products, matmul_nt(): lax.dot_general(first_op, second_op, (((1,), (1,)), ((), ())), preferred_...  31.7 us
    pallas_call x1, Pallas kernels, attend_backward(): pl.pallas_call(functools.partial(attend_backward_kernel, masks, head_size...  23.2 us
    dot_general x3, matrix products, matmul(): return jnp.dot(first_op, second_op, preferred_element_type=F32)  22.9 us
  transfers between devices with their start and end apart: 94, of which 34 were waited for; matrix products, arithmetic and copies ran while one was open for 25% of the time, Pallas kernels for 19%

profile of v7, /device:TPU:0, one launch (start us, length us, event | category | flops | bytes accessed | tf_op | source)
XLA Modules:
  0.0 628.6 jit_solution(2461914923104241885)
XLA Ops:
  31.9 7.6 %collective-permute-done.2 = bf16[256,768]{1,0:T(8,128)(2,1)S(1)} collective-permute-done((bf16[256,768]{1,0:T(8,128)(2,1)S(1)}, bf16[256,768]{1,0:T(8,128)(2,1)S(1)}, u32[]{:S(2)}, u32[]{:S(2)}) %collective-permute-start.2) | collective-permute-done | bytes 393248 | tf_op jit(solution)/shard_map/ppermute | solution.py:18
  43.4 20.0 %collective-permute-done.3.refs_1_ = bf16[256,2048]{1,0:T(8,128)(2,1)S(1)} collective-permute-done((bf16[256,2048]{1,0:T(8,128)(2,1)S(1)}, bf16[256,2048]{1,0:T(8,128)(2,1)S(1)}, u32[]{:S(2)}, u32[]{:S(2)}) %collective-permute-start.3) | collective-permute-done | bytes 1048608 | tf_op jit(solution)/shard_map/ppermute | solution.py:18
  67.6 7.4 %collective-permute-done = s32[1]{0:T(128)} collective-permute-done((s32[1]{0:T(128)}, s32[1]{0:T(128)}, u32[]{:S(2)}, u32[]{:S(2)}) %collective-permute-start) | collective-permute-done | bytes 36 | tf_op jit(solution)/shard_map/ppermute | solution.py:18
  90.7 10.6 %fusion.39 = f32[2048,512]{1,0:T(8,128)} fusion(bf16[2048,2048]{1,0:T(8,128)(2,1)} %copy-done.10, bf16[2048,512]{0,1:T(8,128)(2,1)} %all-gather.6.cloned.1.call-done), kind=kOutput, calls=%fused_computation.165 | convolution fusion | flops 4294967296 | bytes 14680064 | tf_op jit(solution)/shard_map/dot_general | solution.py:254
  101.3 17.9 %attend_forward.1 = (f32[2,2,512,256]{3,2,1,0:T(8,128)}, f32[2,1024,256]{2,1,0:T(8,128)}, bf16[2,1024,256]{2,1,0:T(8,128)(2,1)}, bf16[2,1024,128]{2,1,0:T(8,128)(2,1)}, bf16[2,1024,128]{2,1,0:T(8,128)(2,1)}) custom-call(s32[1]{0:T(128)} %bitcast.share_ref, s32[2]{0:T(128)} %pad_add_fusion.length_ref, f32[2,2,512,512]{3,2,1,0:T(8,128)} %bitcast.46, ...), custom_call_target="tpu_custom_call" | custom-call | flops 1024 | bytes 1024 | tf_op jit(solution)/shard_map/attend_forward/pallas_call | solution.py:585
  121.5 8.4 %multiply_convert_fusion.4 = (bf16[2048,256]{1,0:T(8,128)(2,1)S(1)}, f32[2048,256]{1,0:T(8,128)}) fusion(f32[2,2,512,256]{3,2,1,0:T(8,128)} %get-tuple-element.109, bf16[2048,2048]{1,0:T(8,128)(2,1)} %copy-done.10, bf16[2048,512]{0,1:T(8,128)(2,1)} %all-gather.8.cloned.1.call-done), kind=kOutput, calls=%fused_computation.48 | convolution fusion | flops 2150105088 | bytes 14680064 | tf_op jit(solution)/shard_map/dot_general | solution.py:254
  148.4 7.5 %collective-permute-done.20 = bf16[128,2048]{1,0:T(8,128)(2,1)} collective-permute-done((bf16[128,2048]{1,0:T(8,128)(2,1)}, bf16[128,2048]{1,0:T(8,128)(2,1)}, u32[]{:S(2)}, u32[]{:S(2)}) %collective-permute-start.20) | collective-permute-done | bytes 524320 | tf_op jit(solution)/shard_map/ppermute | solution.py:18
  161.4 10.6 %collective-permute-done.21 = bf16[128,2048]{1,0:T(8,128)(2,1)S(1)} collective-permute-done((bf16[128,2048]{1,0:T(8,128)(2,1)S(1)}, bf16[128,2048]{1,0:T(8,128)(2,1)S(1)}, u32[]{:S(2)}, u32[]{:S(2)}) %collective-permute-start.21) | collective-permute-done | bytes 524320 | tf_op jit(solution)/shard_map/ppermute | solution.py:18
  173.8 9.4 %all-gather.10.cloned.1.call-done.gate_weights_ref = bf16[2048,768]{1,0:T(8,128)(2,1)} async-done(((bf16[512,768]{1,0:T(8,128)(2,1)}), bf16[2048,768]{1,0:T(8,128)(2,1)}) %all-gather.10.cloned.1.call-update) | async-done | bytes 3145744 | tf_op jit(solution)/shard_map/all_gather | solution.py:51
  188.7 21.9 %collective-permute-done.23.refs_1_ = bf16[256,2048]{1,0:T(8,128)(2,1)S(1)} collective-permute-done((bf16[256,2048]{1,0:T(8,128)(2,1)S(1)}, bf16[256,2048]{1,0:T(8,128)(2,1)S(1)}, u32[]{:S(2)}, u32[]{:S(2)}) %collective-permute-start.23) | collective-permute-done | bytes 1048608 | tf_op jit(solution)/shard_map/ppermute | solution.py:18
  216.3 8.3 %collective-permute-done.25.refs_3_ = bf16[128,2048]{1,0:T(8,128)(2,1)} collective-permute-done((bf16[128,2048]{1,0:T(8,128)(2,1)}, bf16[128,2048]{1,0:T(8,128)(2,1)}, u32[]{:S(2)}, u32[]{:S(2)}) %collective-permute-start.25) | collective-permute-done | bytes 524320 | tf_op jit(solution)/shard_map/ppermute | solution.py:18
  241.1 23.9 %collective-permute-done.32.refs_1_ = bf16[256,2048]{1,0:T(8,128)(2,1)} collective-permute-done((bf16[256,2048]{1,0:T(8,128)(2,1)}, bf16[256,2048]{1,0:T(8,128)(2,1)}, u32[]{:S(2)}, u32[]{:S(2)}) %collective-permute-start.32) | collective-permute-done | bytes 1048608 | tf_op jit(solution)/shard_map/ppermute | solution.py:18
  273.2 15.7 %hidden_units.1 = (f32[2048,768]{1,0:T(8,128)S(1)}, f32[2048,768]{1,0:T(8,128)S(1)}, bf16[2048,768]{1,0:T(8,128)(2,1)S(1)}) custom-call(bf16[2048,2048]{1,0:T(8,128)(2,1)} %copy-done.2, bf16[2048,768]{1,0:T(8,128)(2,1)S(1)} %copy-done.8, bf16[2048,768]{1,0:T(8,128)(2,1)S(1)} %copy-done.9), custom_call_target="tpu_custom_call" | custom-call | flops 1024 | bytes 1024 | tf_op jit(solution)/shard_map/hidden_units/pallas_call | solution.py:475
  301.4 8.2 %convolution_convert_fusion.8 = bf16[2048,768]{1,0:T(8,128)(2,1)} fusion(bf16[2048,2048]{1,0:T(8,128)(2,1)S(1)} %stack_rows.6.branch_ref, bf16[2048,768]{1,0:T(8,128)(2,1)S(1)} %get-tuple-element.153), kind=kOutput, calls=%fused_computation.9 | convolution fusion | flops 6444023808 | bytes 14680064 | tf_op jit(solution)/shard_map/dot_general | solution.py:258
  310.4 36.0 %unit_grads.1 = (bf16[2048,768]{1,0:T(8,128)(2,1)}, bf16[2048,768]{1,0:T(8,128)(2,1)}, bf16[1024,2048]{1,0:T(8,128)(2,1)}, bf16[768,2048]{1,0:T(8,128)(2,1)}, bf16[256,2048]{1,0:T(8,128)(2,1)}) custom-call(bf16[2048,2048]{1,0:T(8,128)(2,1)} %copy-done.3, f32[2048,768]{1,0:T(8,128)} %copy-done.11, f32[2048,768]{1,0:T(8,128)} %copy-done.12, ...), custom_call_target="tpu_custom_call" | custom-call | flops 1024 | bytes 1024 | tf_op jit(solution)/shard_map/unit_grads/pallas_call | solution.py:536
  346.9 11.4 %convolution_convert_fusion.7 = bf16[2048,768]{1,0:T(8,128)(2,1)} fusion(bf16[2048,2048]{1,0:T(8,128)(2,1)} %copy-done.2, bf16[2048,768]{1,0:T(8,128)(2,1)} %get-tuple-element.139), kind=kOutput, calls=%fused_computation.8 | convolution fusion | flops 6444023808 | bytes 14680064 | tf_op jit(solution)/shard_map/dot_general | solution.py:258
  382.1 8.6 %convolution_convert_fusion.6 = bf16[2048,768]{1,0:T(8,128)(2,1)} fusion(bf16[2048,2048]{1,0:T(8,128)(2,1)S(1)} %bitcast.41, bf16[2048,768]{1,0:T(8,128)(2,1)S(1)} %copy-done.60), kind=kOutput, calls=%fused_computation.7 | convolution fusion | flops 6444023808 | bytes 14680064 | tf_op jit(solution)/shard_map/dot_general | solution.py:258
  390.7 9.5 %collective-permute-done.47 = bf16[128,2048]{1,0:T(8,128)(2,1)} collective-permute-done((bf16[128,2048]{1,0:T(8,128)(2,1)}, bf16[128,2048]{1,0:T(8,128)(2,1)}, u32[]{:S(2)}, u32[]{:S(2)}) %collective-permute-start.47) | collective-permute-done | bytes 524320 | tf_op jit(solution)/shard_map/ppermute | solution.py:18
  407.4 6.7 %convolution_convert_fusion.4 = bf16[768,2048]{1,0:T(8,128)(2,1)} fusion(bf16[2048,768]{1,0:T(8,128)(2,1)} %all-gather.14.cloned.1.call-done.down_weights_ref, bf16[2048,768]{1,0:T(8,128)(2,1)} %copy-done.29), kind=kOutput, calls=%fused_computation.5 | convolution fusion | flops 2417491968 | bytes 7471104 | tf_op jit(solution)/shard_map/dot_general | solution.py:264
  414.6 14.6 %collective-permute-done.51.refs_1_ = bf16[256,2048]{1,0:T(8,128)(2,1)S(1)} collective-permute-done((bf16[256,2048]{1,0:T(8,128)(2,1)S(1)}, bf16[256,2048]{1,0:T(8,128)(2,1)S(1)}, u32[]{:S(2)}, u32[]{:S(2)}) %collective-permute-start.51) | collective-permute-done | bytes 1048608 | tf_op jit(solution)/shard_map/ppermute | solution.py:18
  458.5 7.6 %collective-permute-done.66 = bf16[256,768]{1,0:T(8,128)(2,1)S(1)} collective-permute-done((bf16[256,768]{1,0:T(8,128)(2,1)S(1)}, bf16[256,768]{1,0:T(8,128)(2,1)S(1)}, u32[]{:S(2)}, u32[]{:S(2)}) %collective-permute-start.66) | collective-permute-done | bytes 393248 | tf_op jit(solution)/shard_map/ppermute | solution.py:18
  494.3 23.2 %attend_backward.1 = (bf16[2,2,512,768]{3,2,1,0:T(8,128)(2,1)}, f32[8,128]{1,0:T(8,128)}) custom-call(s32[1]{0:T(128)} %bitcast.share_ref, s32[2]{0:T(128)} %pad_add_fusion.length_ref, bf16[2,2,512,256]{3,2,1,0:T(8,128)(2,1)} %bitcast.54, bf16[2,2,512,256]{3,2,1,0:T(8,128)(2,1)} %bitcast.53, f32[2,2,512,512]{3,2,1,0:T(8,128)} %bitcast.49, ...), custom_call_target="tpu_custom_call" | custom-call | flops 1024 | bytes 1024 | tf_op jit(solution)/shard_map/attend_backward/pallas_call | solution.py:610
  545.1 6.4 %collective-permute-done.78 = bf16[256,768]{1,0:T(8,128)(2,1)S(1)} collective-permute-done((bf16[256,768]{1,0:T(8,128)(2,1)S(1)}, bf16[256,768]{1,0:T(8,128)(2,1)S(1)}, u32[]{:S(2)}, u32[]{:S(2)}) %collective-permute-start.78) | collective-permute-done | bytes 393248 | tf_op jit(solution)/shard_map/ppermute | solution.py:18
  578.7 16.9 %collective-permute-done.74 = bf16[128,2048]{1,0:T(8,128)(2,1)} collective-permute-done((bf16[128,2048]{1,0:T(8,128)(2,1)}, bf16[128,2048]{1,0:T(8,128)(2,1)}, u32[]{:S(2)}, u32[]{:S(2)}) %collective-permute-start.74) | collective-permute-done | bytes 524320 | tf_op jit(solution)/shard_map/ppermute | solution.py:18
  (458 shorter events, 294.0 us)
Async XLA Ops:
  7.2 83.5 %all-gather.6.cloned.1.call-start = ((), (), s32[]{:S(2)}) async-start(), calls=%async_computation.5 | async-start | bytes 2621440 | tf_op jit(solution)/shard_map/all_gather | solution.py:51
  21.1 100.4 %all-gather.8.cloned.1.call-start = ((), (), s32[]{:S(2)}) async-start(), calls=%async_computation.6 | async-start | bytes 2621440 | tf_op jit(solution)/shard_map/all_gather | solution.py:51
  43.1 140.0 %all-gather.10.cloned.1.call-start = ((), (), s32[]{:S(2)}) async-start(), calls=%async_computation.7 | async-start | bytes 3932160 | tf_op jit(solution)/shard_map/all_gather | solution.py:51
  88.5 30.6 %collective-permute-start.14 = (bf16[256,768]{1,0:T(8,128)(2,1)S(1)}, bf16[256,768]{1,0:T(8,128)(2,1)S(1)}, u32[]{:S(2)}, u32[]{:S(2)}) collective-permute-start(bf16[256,768]{1,0:T(8,128)(2,1)S(1)} %broadcast_select_fusion.15), channel_id=1, source_target_pairs={{0,4},{4,0},{8,12},{12,8},{16,20},{20,16},{24,28},{28,24},{1,5},{5... | collective-permute-start | bytes 1179656 | tf_op jit(solution)/shard_map/ppermute | solution.py:18
  90.2 29.0 %collective-permute-start.13 = (bf16[256,768]{1,0:T(8,128)(2,1)S(1)}, bf16[256,768]{1,0:T(8,128)(2,1)S(1)}, u32[]{:S(2)}, u32[]{:S(2)}) collective-permute-start(bf16[256,768]{1,0:T(8,128)(2,1)S(1)} %broadcast_select_fusion.19), channel_id=1, source_target_pairs={{0,4},{4,0},{8,12},{12,8},{16,20},{20,16},{24,28},{28,24},{1,5},{5... | collective-permute-start | bytes 1179656 | tf_op jit(solution)/shard_map/ppermute | solution.py:18
  119.2 152.1 %all-gather.12.cloned.1.call-start = ((), (), s32[]{:S(2)}) async-start(), calls=%async_computation.8 | async-start | bytes 3932160 | tf_op jit(solution)/shard_map/all_gather | solution.py:51
  142.9 167.5 %all-gather.14.cloned.1.call-start = ((), (), s32[]{:S(2)}) async-start(), calls=%async_computation.9 | async-start | bytes 3932160 | tf_op jit(solution)/shard_map/all_gather | solution.py:51
  215.9 184.3 %reduce-scatter.6.cloned.1.call-start = ((), (), s32[]{:S(2)}) async-start(), calls=%async_computation.10 | async-start | bytes 3932160 | tf_op jit(solution)/shard_map/reduce_scatter | solution.py:55
  240.5 26.9 %collective-permute-start.33 = (bf16[256,2048]{1,0:T(8,128)(2,1)}, bf16[256,2048]{1,0:T(8,128)(2,1)}, u32[]{:S(2)}, u32[]{:S(2)}) collective-permute-start(bf16[256,2048]{1,0:T(8,128)(2,1)} %fusion.13.refs_0_), channel_id=1, source_target_pairs={{0,4},{4,0},{8,12},{12,8},{16,20},{20,16},{24,28},{28,24},{1,5},{5... | collective-permute-start | bytes 3145736 | tf_op jit(solution)/shard_map/ppermute | solution.py:18
  309.7 130.7 %reduce-scatter.8.cloned.1.call-start = ((), (), s32[]{:S(2)}) async-start(), calls=%async_computation.11 | async-start | bytes 3932160 | tf_op jit(solution)/shard_map/reduce_scatter | solution.py:55
  358.4 159.9 %reduce-scatter.10.cloned.1.call-start = ((), (), s32[]{:S(2)}) async-start(), calls=%async_computation.12 | async-start | bytes 3932160 | tf_op jit(solution)/shard_map/reduce_scatter | solution.py:55
  370.1 30.1 %collective-permute-start.43 = (bf16[128,2048]{1,0:T(8,128)(2,1)}, bf16[128,2048]{1,0:T(8,128)(2,1)S(1)}, u32[]{:S(2)}, u32[]{:S(2)}) collective-permute-start(bf16[128,2048]{1,0:T(8,128)(2,1)} %get-tuple-element.142), channel_id=1, source_target_pairs={{0,2},{1,3},{2,0},{3,1},{4,6},{5,7},{6,4},{7,5},{8,10},{9,11},{10,... | collective-permute-start | bytes 1572872 | tf_op jit(solution)/shard_map/ppermute | solution.py:18
  370.6 29.6 %collective-permute-start.48 = (bf16[128,2048]{1,0:T(8,128)(2,1)}, bf16[128,2048]{1,0:T(8,128)(2,1)S(1)}, u32[]{:S(2)}, u32[]{:S(2)}) collective-permute-start(bf16[128,2048]{1,0:T(8,128)(2,1)} %get-tuple-element.152), channel_id=1, source_target_pairs={{0,4},{4,0},{8,12},{12,8},{16,20},{20,16},{24,28},{28,24},{1,5},{5... | collective-permute-start | bytes 1572872 | tf_op jit(solution)/shard_map/ppermute | solution.py:18
  407.3 171.4 %reduce-scatter.12.cloned.1.call-start = ((), (), s32[]{:S(2)}) async-start(), calls=%async_computation.13 | async-start | bytes 2621440 | tf_op jit(solution)/shard_map/reduce_scatter | solution.py:55
  407.3 37.4 %collective-permute-start.55 = (bf16[256,2048]{1,0:T(8,128)(2,1)S(1)}, bf16[256,2048]{1,0:T(8,128)(2,1)}, u32[]{:S(2)}, u32[]{:S(2)}) collective-permute-start(bf16[256,2048]{1,0:T(8,128)(2,1)S(1)} %get-tuple-element.224.refs_0_), channel_id=1, source_target_pairs={{0,1},{1,0},{2,3},{3,2},{4,5},{5,4},{6,7},{7,6},{8,9},{9,8},{10,11... | collective-permute-start | bytes 3145736 | tf_op jit(solution)/shard_map/ppermute | solution.py:18
  414.1 53.4 %collective-permute-start.50 = (bf16[768,2048]{1,0:T(8,128)(2,1)}, bf16[768,2048]{1,0:T(8,128)(2,1)}, u32[]{:S(2)}, u32[]{:S(2)}) collective-permute-start(bf16[768,2048]{1,0:T(8,128)(2,1)} %convolution_convert_fusion.4), channel_id=1, source_target_pairs={{0,1},{1,0},{2,3},{3,2},{4,5},{5,4},{6,7},{7,6},{8,9},{9,8},{10,11... | collective-permute-start | bytes 9437192 | tf_op jit(solution)/shard_map/ppermute | solution.py:18
  457.0 27.8 %collective-permute-start.67 = (bf16[256,768]{1,0:T(8,128)(2,1)S(1)}, bf16[256,768]{1,0:T(8,128)(2,1)}, u32[]{:S(2)}, u32[]{:S(2)}) collective-permute-start(bf16[256,768]{1,0:T(8,128)(2,1)S(1)} %broadcast_select_fusion.8), channel_id=1, source_target_pairs={{0,4},{4,0},{8,12},{12,8},{16,20},{20,16},{24,28},{28,24},{1,5},{5... | collective-permute-start | bytes 1179656 | tf_op jit(solution)/shard_map/ppermute | solution.py:18
  484.7 114.4 %reduce-scatter.14.cloned.1.call-start = ((), (), s32[]{:S(2)}) async-start(), calls=%async_computation.14 | async-start | bytes 2621440 | tf_op jit(solution)/shard_map/reduce_scatter | solution.py:55
  484.8 33.4 %collective-permute-start.60 = (bf16[128,2048]{1,0:T(8,128)(2,1)S(1)}, bf16[128,2048]{1,0:T(8,128)(2,1)}, u32[]{:S(2)}, u32[]{:S(2)}) collective-permute-start(bf16[128,2048]{1,0:T(8,128)(2,1)S(1)} %get-tuple-element.165), channel_id=1, source_target_pairs={{0,2},{1,3},{2,0},{3,1},{4,6},{5,7},{6,4},{7,5},{8,10},{9,11},{10,... | collective-permute-start | bytes 1572872 | tf_op jit(solution)/shard_map/ppermute | solution.py:18
  485.5 32.7 %collective-permute-start.61 = (bf16[128,2048]{1,0:T(8,128)(2,1)S(1)}, bf16[128,2048]{1,0:T(8,128)(2,1)}, u32[]{:S(2)}, u32[]{:S(2)}) collective-permute-start(bf16[128,2048]{1,0:T(8,128)(2,1)S(1)} %get-tuple-element.167), channel_id=1, source_target_pairs={{0,4},{4,0},{8,12},{12,8},{16,20},{20,16},{24,28},{28,24},{1,5},{5... | collective-permute-start | bytes 1572872 | tf_op jit(solution)/shard_map/ppermute | solution.py:18
  487.1 31.1 %collective-permute-start.63 = (bf16[128,2048]{1,0:T(8,128)(2,1)S(1)}, bf16[128,2048]{1,0:T(8,128)(2,1)}, u32[]{:S(2)}, u32[]{:S(2)}) collective-permute-start(bf16[128,2048]{1,0:T(8,128)(2,1)S(1)} %get-tuple-element.169), channel_id=1, source_target_pairs={{0,2},{1,3},{2,0},{3,1},{4,6},{5,7},{6,4},{7,5},{8,10},{9,11},{10,... | collective-permute-start | bytes 1572872 | tf_op jit(solution)/shard_map/ppermute | solution.py:18
  488.5 29.8 %collective-permute-start.65 = (bf16[128,2048]{1,0:T(8,128)(2,1)S(1)}, bf16[128,2048]{1,0:T(8,128)(2,1)}, u32[]{:S(2)}, u32[]{:S(2)}) collective-permute-start(bf16[128,2048]{1,0:T(8,128)(2,1)S(1)} %get-tuple-element.176), channel_id=1, source_target_pairs={{0,4},{4,0},{8,12},{12,8},{16,20},{20,16},{24,28},{28,24},{1,5},{5... | collective-permute-start | bytes 1572872 | tf_op jit(solution)/shard_map/ppermute | solution.py:18
  563.7 31.9 %collective-permute-start.70 = (bf16[128,2048]{1,0:T(8,128)(2,1)}, bf16[128,2048]{1,0:T(8,128)(2,1)}, u32[]{:S(2)}, u32[]{:S(2)}) collective-permute-start(bf16[128,2048]{1,0:T(8,128)(2,1)} %get-tuple-element.185), channel_id=1, source_target_pairs={{0,2},{1,3},{2,0},{3,1},{4,6},{5,7},{6,4},{7,5},{8,10},{9,11},{10,... | collective-permute-start | bytes 1572872 | tf_op jit(solution)/shard_map/ppermute | solution.py:18
  564.5 31.1 %collective-permute-start.79 = (bf16[128,2048]{1,0:T(8,128)(2,1)}, bf16[128,2048]{1,0:T(8,128)(2,1)}, u32[]{:S(2)}, u32[]{:S(2)}) collective-permute-start(bf16[128,2048]{1,0:T(8,128)(2,1)} %get-tuple-element.192), channel_id=1, source_target_pairs={{0,4},{4,0},{8,12},{12,8},{16,20},{20,16},{24,28},{28,24},{1,5},{5... | collective-permute-start | bytes 1572872 | tf_op jit(solution)/shard_map/ppermute | solution.py:18
  (141 other events, 1678.9 us)
Sparse Core Ops, SparseCore 0:
  21.2 47.3 all-gather.5
  70.8 44.6 all-gather.7
  119.3 63.8 all-gather.9
  184.6 62.1 all-gather.11
  248.2 62.1 all-gather.13
  312.5 58.8 reduce-scatter.5
  373.8 60.2 reduce-scatter.7
  436.4 60.2 reduce-scatter.9
  499.0 43.8 reduce-scatter.11
  545.1 44.0 reduce-scatter.13
